TPU v7x, 128 devices: a whole 4x4x4 slice. The times are simulated.
128 devices in a mesh: grp: 4 (over y), shard: 32 (over x, z, core).
Axes of the slice: x: 4, y: 4, z: 4, core: 2. Of those that a mesh axis runs over, the one named last changes fastest.
Arguments:
- candidates: int32 [32768, 16], P(('grp', 'shard')), may hold values from 0 to 3199
- affinity: float32 [32768, 2048], P(('grp', 'shard')), may hold values from -6 to 6
- exposure: float32 [32768, 2048], P(('grp', 'shard')), may hold values from 0.5 to 2
- lengths: int32 [32768], P(('grp', 'shard')), may hold values from 256 to 2048, as said below
- item_limit: float32 [409600], P('shard'), may hold values from 0.02 to 0.2
- item_duals: float32 [409600], P('shard'), may hold values from 0 to 1
Outputs:
- primal: float32 [32768, 2048], P(('grp', 'shard'))
- duals_out: float32 [409600], P('shard')
Inputs may be any that keep to these rules, and one draw needn't show every extreme that they name: `lengths`: multiples of 128; among the members of every device at least one has 2048 live slots.
All inputs are finite; a program needn't handle non-finite values.
Results may differ from a plain program's by a relative error of at most 0.0003.
Values sent between devices are 32-bit elements; how exact they have to be, the bound alone decides.
No kernel may reach another device: no remote copies, remote signals or barrier semaphores. Data moves between devices by JAX's collectives and lax.ppermute only.
A program may use at most 64 MiB of HBM per device.

v0:
```python
import jax
import jax.numpy as jnp
from jax import lax
from jax.sharding import PartitionSpec as P

BLOCK = 128
ITERS = 2
BISECT = 16


gamma_reg = 0.5
step_eta = 0.5


def copy_for_each(array, axis):
    peers = lax.axis_size(axis)
    return lax.all_to_all(
        jnp.broadcast_to(array[None], (peers, *array.shape)), axis, 0, 0, tiled=True
    )


def in_order(parts, dim):
    parts = jnp.moveaxis(parts, 0, dim)
    shape = parts.shape
    return parts.reshape(*shape[:dim], shape[dim] * shape[dim + 1], *shape[dim + 2 :])


def collect(array, axis, dim):
    parts = copy_for_each(array, axis)
    return in_order(parts, dim)


def cut_along(array, dim, peers):
    shape = array.shape
    parts = array.reshape(*shape[:dim], peers, shape[dim] // peers, *shape[dim + 1 :])
    return jnp.moveaxis(parts, dim, 0)


def sum_at_owner(array, axis, dim):
    parts = cut_along(array, dim, lax.axis_size(axis))
    arrived = lax.all_to_all(parts, axis, split_axis=0, concat_axis=0, tiled=True)
    return arrived.sum(axis=0)


def of_everyone(array, axis):
    everything = copy_for_each(array, axis)
    return jnp.sum(everything, axis=0)


def project(scaled, live_mask):
    zero_f = jnp.zeros((), jnp.float32)
    lowest = jnp.asarray(-1e30, jnp.float32)
    upper_t = jnp.max(jnp.where(live_mask, scaled, lowest), axis=1)
    lower_t = jnp.zeros_like(upper_t)
    for _ in range(BISECT):
        middle = (lower_t + upper_t) * 0.5
        bigger = (
            jnp.sum(
                jnp.where(live_mask, jnp.clip(scaled - middle[:, None], 0.0, 1.0), zero_f), axis=1
            )
            > 1.0
        )
        lower_t = jnp.where(bigger, middle, lower_t)
        upper_t = jnp.where(bigger, upper_t, middle)
    return jnp.where(live_mask, jnp.clip(scaled - upper_t[:, None], 0.0, 1.0), zero_f)


def local(candidates, affinity, exposure, lengths, item_limit, item_duals):
    shard_count = lax.axis_size("shard")
    item_count = item_limit.shape[0] * shard_count
    block_rows = item_count // BLOCK
    members, slots = affinity.shape
    positions = jnp.arange(slots, dtype=jnp.int32)
    live_mask = positions[None, :] < lengths[:, None]
    flat_blocks = candidates.reshape(-1)
    duals = item_duals
    primal = affinity
    for _ in range(ITERS):
        all_duals = collect(duals, "shard", 0)
        slot_duals = all_duals.reshape(block_rows, BLOCK)[flat_blocks].reshape(members, slots)
        scaled = (affinity - exposure * slot_duals) / gamma_reg
        primal = project(scaled, live_mask)
        contrib = (exposure * primal).reshape(-1, BLOCK)
        partial_value = (
            jnp.zeros((block_rows, BLOCK), jnp.float32).at[flat_blocks].add(contrib).reshape(-1)
        )
        item_load = sum_at_owner(partial_value, "shard", 0)
        item_load = of_everyone(item_load, "grp")
        gradient = item_load - item_limit
        sum_sq = of_everyone(jnp.sum(gradient * gradient), "shard")
        scale = jnp.sqrt(sum_sq / item_count + 1e-06)
        duals = jnp.maximum(duals + step_eta * gradient / scale, 0.0)
    return (primal, duals)


def solution(mesh):
    placed = (
        P(("grp", "shard"), None),
        P(("grp", "shard"), None),
        P(("grp", "shard"), None),
        P(("grp", "shard")),
        P("shard"),
        P("shard"),
    )
    return jax.shard_map(
        local,
        mesh=mesh,
        in_specs=placed,
        out_specs=(P(("grp", "shard"), None), P("shard")),
        check_vma=False,
    )
```

profile of v0, /device:TPU:1, one launch (start us, length us, event | category | flops | bytes accessed | tf_op | source)
XLA Modules:
  0.0 279.5 jit_solution(7831433371905680487)
XLA Ops:
  0.6 2.8 %broadcast_in_dim.51 = f32[32,1,12800]{2,1,0:T(1,128)} broadcast(f32[12800]{0:T(1024)} %param.11), dimensions={2} | broadcast | bytes 1689600 | tf_op jit(solution)/shard_map/broadcast_in_dim | solution.py:18
  3.5 9.4 %all-to-all-start = ((f32[32,1,12800]{2,1,0:T(1,128)}), f32[32,1,12800]{2,1,0:T(1,128)S(1)}, u32[]{:S(2)}, u32[]{:S(2)}) async-start(f32[32,1,12800]{2,1,0:T(1,128)} %broadcast_in_dim.51), calls=%async_computation | async-start | bytes 3276800 | tf_op jit(solution)/shard_map/all_to_all | solution.py:17
  13.2 23.1 %all-to-all-done = f32[32,1,12800]{2,1,0:T(1,128)S(1)} async-done(((f32[32,1,12800]{2,1,0:T(1,128)}), f32[32,1,12800]{2,1,0:T(1,128)S(1)}, u32[]{:S(2)}, u32[]{:S(2)}) %all-to-all-start) | async-done | bytes 1638432 | tf_op jit(solution)/shard_map/all_to_all | solution.py:17
  36.3 14.2 %gather_fusion = f32[4096,128]{1,0:T(8,128)} fusion(f32[3200,128]{1,0:T(8,128)S(1)} %bitcast.5, s32[4096]{0:T(1024)S(1)} %broadcast_clamp_fusion), kind=kCustom, calls=%fused_computation | custom fusion | bytes 4210688 | tf_op jit(solution)/shard_map/gather | solution.py:80
  50.5 2.9 %reshape.855 = f32[256,2048]{1,0:T(8,128)} reshape(f32[4096,128]{1,0:T(8,128)} %gather_fusion) | data formatting | bytes 4194304 | tf_op jit(solution)/shard_map/reshape | solution.py:80
  53.4 2.8 %select_reduce_fusion.33 = (f32[256]{0:T(256)S(1)}, f32[256,2048]{1,0:T(8,128)S(1)}) fusion(s32[256]{0:T(256)S(1)} %copy-done.2, f32[256,2048]{1,0:T(8,128)} %param.7, f32[256,2048]{1,0:T(8,128)S(1)} %copy-done, f32[256,2048]{1,0:T(8,128)} %reshape.855), kind=kLoop, calls=%fused_computation.40 | loop fusion | flops 3145472 | bytes 8390656 | tf_op jit(solution)/shard_map/reduce_max | solution.py:53
  56.2 0.5 select_reduce_fusion.32
  56.7 0.5 select_reduce_fusion.31
  57.2 0.5 select_reduce_fusion.30
  57.7 0.5 select_reduce_fusion.29
  58.2 0.5 select_reduce_fusion.28
  58.7 0.5 select_reduce_fusion.27
  59.3 0.5 select_reduce_fusion.26
  59.8 0.5 select_reduce_fusion.25
  60.3 0.5 select_reduce_fusion.24
  60.8 0.5 select_reduce_fusion.23
  61.3 0.5 select_reduce_fusion.22
  61.8 0.5 select_reduce_fusion.21
  62.3 0.5 select_reduce_fusion.20
  62.8 0.5 select_reduce_fusion.19
  63.4 0.5 select_reduce_fusion.18
  63.9 0.5 select_reduce_fusion.17
  64.4 1.8 select_multiply_fusion
  66.2 2.7 reshape.879
  68.9 23.1 %scatter_custom_fusion = f32[3200,128]{1,0:T(8,128)S(1)} fusion(s32[4096]{0:T(1024)S(1)} %bitcast.10, f32[4096,128]{1,0:T(8,128)} %reshape.879, f32[]{:T(128)} %constant.10.clone.1), kind=kCustom, calls=%fused_computation.45 | custom fusion | flops 524288 | bytes 1638912 | tf_op jit(solution)/shard_map/scatter-add | solution.py:85
  92.0 27.1 %all_to_all.54 = f32[32,1,12800]{2,1,0:T(1,128)S(1)} all-to-all(f32[32,1,12800]{2,1,0:T(1,128)S(1)} %bitcast.8), channel_id=1, replica_groups=mesh['grp'=4,'shard'=32] {'shard'}, dimensions={0} | all-to-all | bytes 3276800 | tf_op jit(solution)/shard_map/all_to_all | solution.py:41
  119.1 0.9 reduce_sum.376
  120.1 10.1 %all_to_all.55 = f32[4,1,12800]{2,1,0:T(1,128)S(1)} all-to-all(f32[4,1,12800]{2,1,0:T(1,128)S(1)} %broadcast_in_dim.53), channel_id=1, replica_groups=mesh['grp'=4,'shard'=32] {'grp'}, dimensions={0} | all-to-all | bytes 409600 | tf_op jit(solution)/shard_map/all_to_all | solution.py:17
  130.4 0.6 multiply_reduce_fusion.1
  131.0 0.7 broadcast_in_dim.54
  131.7 11.1 %all_to_all.56 = f32[32,1,1]{2,1,0:T(1,128)S(1)} all-to-all(f32[32,1,1]{2,1,0:T(1,128)S(1)} %broadcast_in_dim.54), channel_id=1, replica_groups=mesh['grp'=4,'shard'=32] {'shard'}, dimensions={0} | all-to-all | bytes 256 | tf_op jit(solution)/shard_map/all_to_all | solution.py:17
  142.7 0.6 reduce_sum.379
  144.1 0.8 broadcast_in_dim.55
  145.0 27.2 %all_to_all.57 = f32[32,1,12800]{2,1,0:T(1,128)S(1)} all-to-all(f32[32,1,12800]{2,1,0:T(1,128)S(1)} %broadcast_in_dim.55), channel_id=1, replica_groups=mesh['grp'=4,'shard'=32] {'shard'}, dimensions={0} | all-to-all | bytes 3276800 | tf_op jit(solution)/shard_map/all_to_all | solution.py:17
  172.2 14.2 %gather_fusion.1 = f32[4096,128]{1,0:T(8,128)} fusion(f32[3200,128]{1,0:T(8,128)S(1)} %bitcast.6, s32[4096]{0:T(1024)S(1)} %broadcast_clamp_fusion), kind=kCustom, calls=%fused_computation.1 | custom fusion | bytes 4210688 | tf_op jit(solution)/shard_map/gather | solution.py:80
  186.4 2.9 %reshape.857 = f32[256,2048]{1,0:T(8,128)} reshape(f32[4096,128]{1,0:T(8,128)} %gather_fusion.1) | data formatting | bytes 4194304 | tf_op jit(solution)/shard_map/reshape | solution.py:80
  189.3 2.8 %select_reduce_fusion.16 = (f32[256]{0:T(256)S(1)}, f32[256,2048]{1,0:T(8,128)S(1)}) fusion(s32[256]{0:T(256)S(1)} %copy-done.2, f32[256,2048]{1,0:T(8,128)} %param.7, f32[256,2048]{1,0:T(8,128)S(1)} %copy-done.1, f32[256,2048]{1,0:T(8,128)} %reshape.857), kind=kLoop, calls=%fused_computation.21 | loop fusion | flops 3145472 | bytes 8390656 | tf_op jit(solution)/shard_map/reduce_max | solution.py:53
  192.1 0.5 select_reduce_fusion.15
  192.6 0.5 select_reduce_fusion.14
  193.1 0.5 select_reduce_fusion.13
  193.6 0.5 select_reduce_fusion.12
  194.1 0.5 select_reduce_fusion.11
  194.6 0.5 select_reduce_fusion.10
  195.1 0.5 select_reduce_fusion.9
  195.6 0.5 select_reduce_fusion.8
  196.2 0.5 select_reduce_fusion.7
  196.7 0.5 select_reduce_fusion.6
  197.2 0.5 select_reduce_fusion.5
  197.7 0.5 select_reduce_fusion.4
  198.2 0.5 select_reduce_fusion.3
  198.7 0.5 select_reduce_fusion.2
  199.2 0.5 select_reduce_fusion.1
  199.7 0.5 select_reduce_fusion
  200.2 2.5 fusion.60
  202.8 2.7 reshape.887
  205.5 23.1 %scatter_custom_fusion.1 = f32[3200,128]{1,0:T(8,128)S(1)} fusion(s32[4096]{0:T(1024)S(1)} %bitcast.11, f32[4096,128]{1,0:T(8,128)} %reshape.887, f32[]{:T(128)} %constant.10.clone.1), kind=kCustom, calls=%fused_computation.43 | custom fusion | flops 524288 | bytes 1638912 | tf_op jit(solution)/shard_map/scatter-add | solution.py:85
  228.5 27.0 %all_to_all.58 = f32[32,1,12800]{2,1,0:T(1,128)S(1)} all-to-all(f32[32,1,12800]{2,1,0:T(1,128)S(1)} %bitcast.7), channel_id=1, replica_groups=mesh['grp'=4,'shard'=32] {'shard'}, dimensions={0} | all-to-all | bytes 3276800 | tf_op jit(solution)/shard_map/all_to_all | solution.py:41
  255.5 0.9 reduce_sum.396
  256.5 8.5 %all_to_all.59 = f32[4,1,12800]{2,1,0:T(1,128)S(1)} all-to-all(f32[4,1,12800]{2,1,0:T(1,128)S(1)} %broadcast_in_dim.56), channel_id=1, replica_groups=mesh['grp'=4,'shard'=32] {'grp'}, dimensions={0} | all-to-all | bytes 409600 | tf_op jit(solution)/shard_map/all_to_all | solution.py:17
  265.2 0.6 multiply_reduce_fusion
  265.8 0.7 broadcast_in_dim.57
  266.5 11.1 %all_to_all.60 = f32[32,1,1]{2,1,0:T(1,128)S(1)} all-to-all(f32[32,1,1]{2,1,0:T(1,128)S(1)} %broadcast_in_dim.57), channel_id=1, replica_groups=mesh['grp'=4,'shard'=32] {'shard'}, dimensions={0} | all-to-all | bytes 256 | tf_op jit(solution)/shard_map/all_to_all | solution.py:17
  277.5 0.6 reduce_sum.399
  278.9 0.6 add_maximum_fusion
  (55 shorter events, 1.3 us)
Async XLA Ops:
  0.6 12.3 %copy-start.5 = (s32[256,16]{0,1:T(8,128)S(1)}, s32[256,16]{0,1:T(8,128)}, u32[]{:S(2)}) copy-start(s32[256,16]{0,1:T(8,128)} %param.6) | copy-start | bytes 49156
  3.5 32.8 %all-to-all-start = ((f32[32,1,12800]{2,1,0:T(1,128)}), f32[32,1,12800]{2,1,0:T(1,128)S(1)}, u32[]{:S(2)}, u32[]{:S(2)}) async-start(f32[32,1,12800]{2,1,0:T(1,128)} %broadcast_in_dim.51), calls=%async_computation | async-start | bytes 3276800 | tf_op jit(solution)/shard_map/all_to_all | solution.py:17
  50.5 2.9 %copy-start = (f32[256,2048]{1,0:T(8,128)S(1)}, f32[256,2048]{1,0:T(8,128)}, u32[]{:S(2)}) copy-start(f32[256,2048]{1,0:T(8,128)} %param.8) | copy-start | bytes 6291460
  50.5 2.9 %copy-start.2 = (s32[256]{0:T(256)S(1)}, s32[256]{0:T(256)}, u32[]{:S(2)}) copy-start(s32[256]{0:T(256)} %param.9) | copy-start | bytes 3076
  119.1 11.3 %copy-start.3 = (f32[12800]{0:T(1024)S(1)}, f32[12800]{0:T(1024)}, u32[]{:S(2)}) copy-start(f32[12800]{0:T(1024)} %param.10) | copy-start | bytes 153604
  119.1 25.0 %copy-start.4 = (f32[12800]{0:T(1024)S(1)}, f32[12800]{0:T(1024)}, u32[]{:S(2)}) copy-start(f32[12800]{0:T(1024)} %param.11) | copy-start | bytes 153604
  186.4 2.9 %copy-start.1 = (f32[256,2048]{1,0:T(8,128)S(1)}, f32[256,2048]{1,0:T(8,128)}, u32[]{:S(2)}) copy-start(f32[256,2048]{1,0:T(8,128)} %param.8) | copy-start | bytes 6291460
where the time goes:
time: 280 us; the launch traced here: 279 us
  blocking collectives  122 us (44%)
  other arithmetic  77.7 us (28%)
  local copies, waits for them, and re-layouts  45 us (16%)
  waiting for transfers between devices  23.1 us (8%)
  starting transfers between devices  9.42 us (3%)
    all_to_all x5, blocking collectives, copy_for_each(): lax.all_to_all(jnp.broadcast_to(array[None], (peers, *array.shape)), axis...  67.9 us
    all_to_all x2, blocking collectives, sum_at_owner(): lax.all_to_all(parts, axis, split_axis=0, concat_axis=0, tiled=True)  54 us
    scatter-add x2, other arithmetic, local(): jnp.zeros((block_rows, BLOCK), jnp.float32).at[flat_blocks].add(contrib)  46.1 us
    gather x2, local copies, waits for them, and re-layouts, local(): all_duals.reshape(block_rows, BLOCK)[flat_blocks].reshape(members, slots)  28.4 us
    all_to_all x1, waiting for transfers between devices, copy_for_each(): lax.all_to_all(jnp.broadcast_to(array[None], (peers, *array.shape)), axis...  23.1 us
    reduce_sum x32, other arithmetic, project(): jnp.sum(jnp.where(live_mask, jnp.clip(scaled - middle[:, None], 0.0, 1.0)...  15.9 us
    all_to_all x1, starting transfers between devices, copy_for_each(): lax.all_to_all(jnp.broadcast_to(array[None], (peers, *array.shape)), axis...  9.42 us
    reshape x2, local copies, waits for them, and re-layouts, local(): all_duals.reshape(block_rows, BLOCK)[flat_blocks].reshape(members, slots)  5.77 us
  transfers between devices with their start and end apart: 1, of which 1 were waited for; matrix products, arithmetic and copies ran while one was open for 0% of the time, Pallas kernels for 0%

commit v1 on v0

v1 whole, which is shorter than its diff:
```python
import jax
import jax.numpy as jnp
from jax import lax
from jax.experimental import pallas as pl
from jax.experimental.pallas import tpu as pltpu
from jax.sharding import PartitionSpec as P

BLOCK = 128
BISECT = 16
SUB = 8
BATCH = 32
COPIES = 4
DEAD = -1e30

AXES = ("grp", "shard")


def pad8(n):
    return -(-n // SUB) * SUB


def iteration_kernel(second, groups, blocks, half, item_count):
    full = 2 * half
    members = groups * SUB
    table_vregs = full // SUB

    def body(*refs):
        if second:
            (gidx, sidx, ncopy, own_d, other_d, own_g, other_g, aff, exp, nlive,
             keep, send, primal, sumsq, table, work, scaled, acc, lo, up, fills) = refs
        else:
            (gidx, sidx, ncopy, own_d, other_d, aff, exp, nlive,
             keep, send, table, work, scaled, acc, lo, up, fills) = refs

        if second:
            def square(i, s):
                r = pl.multiple_of(i * SUB, SUB)
                a = own_g[pl.ds(r, SUB), :]
                b = other_g[pl.ds(r, SUB), :]
                return s + (a * a + b * b)

            s = lax.fori_loop(0, half // SUB, square, jnp.zeros((SUB, BLOCK), jnp.float32), unroll=8)
            total = jnp.sum(jnp.sum(s, axis=1, keepdims=True), axis=0, keepdims=True)
            sumsq[...] = jnp.broadcast_to(total, (SUB, BLOCK))
            scale = jnp.sqrt(jnp.broadcast_to(total, (SUB, BLOCK)) / item_count + 1e-6)

            def fill_table(i, c):
                r = pl.multiple_of(i * SUB, SUB)
                for d, g, off in ((own_d, own_g, 0), (other_d, other_g, half)):
                    table[pl.ds(r + off, SUB), :] = jnp.maximum(
                        d[pl.ds(r, SUB), :] + 0.5 * g[pl.ds(r, SUB), :] / scale, 0.0)
                return c
        else:
            def fill_table(i, c):
                r = pl.multiple_of(i * SUB, SUB)
                table[pl.ds(r, SUB), :] = own_d[pl.ds(r, SUB), :]
                table[pl.ds(r + half, SUB), :] = other_d[pl.ds(r, SUB), :]
                return c

        lax.fori_loop(0, half // SUB, fill_table, 0, unroll=8)

        def gather(g, c):
            base = g * (SUB * blocks)
            live = nlive[pl.ds(pl.multiple_of(g * SUB, SUB), SUB), :]
            peak = jnp.full((SUB, BLOCK), DEAD, jnp.float32)
            for b in range(blocks):
                r0 = pl.multiple_of(base + b * SUB, SUB)
                for s in range(SUB):
                    work[pl.ds(r0 + s, 1), :] = table[pl.ds(gidx[base + s * blocks + b], 1), :]
                rows = pl.ds(r0, SUB)
                v = (aff[rows, :] - exp[rows, :] * work[rows, :]) * 2.0
                v = jnp.where(live > b, v, DEAD)
                scaled[rows, :] = v
                peak = jnp.maximum(peak, v)
            rows = pl.ds(pl.multiple_of(g * SUB, SUB), SUB)
            up[rows, :] = jnp.broadcast_to(jnp.max(peak, axis=1, keepdims=True), (SUB, BLOCK))
            lo[rows, :] = jnp.zeros((SUB, BLOCK), jnp.float32)
            return c

        lax.fori_loop(0, groups, gather, 0)

        def bisect(p, c):
            for g in range(groups):
                rows = pl.ds(g * SUB, SUB)
                mid = (lo[rows, :] + up[rows, :]) * 0.5
                a = None
                for b in range(blocks):
                    v = jnp.clip(scaled[pl.ds((g * blocks + b) * SUB, SUB), :] - mid, 0.0, 1.0)
                    a = v if a is None else a + v
                fill = jnp.broadcast_to(jnp.sum(a, axis=1, keepdims=True), (SUB, BLOCK))
                bigger = fill > 1.0
                lo[rows, :] = jnp.where(bigger, mid, lo[rows, :])
                up[rows, :] = jnp.where(bigger, up[rows, :], mid)
            return c

        lax.fori_loop(0, BISECT, bisect, 0)

        def allocate(g, c):
            th = up[pl.ds(pl.multiple_of(g * SUB, SUB), SUB), :]
            live = nlive[pl.ds(pl.multiple_of(g * SUB, SUB), SUB), :]
            for b in range(blocks):
                rows = pl.ds(pl.multiple_of((g * blocks + b) * SUB, SUB), SUB)
                x = jnp.where(live > b, jnp.clip(scaled[rows, :] - th, 0.0, 1.0), 0.0)
                if second:
                    primal[rows, :] = x
                work[rows, :] = exp[rows, :] * x
            return c

        lax.fori_loop(0, groups, allocate, 0)

        zero = jnp.zeros((SUB, BLOCK), jnp.float32)
        n = ncopy[0]

        def clear(i, c):
            acc[pl.ds(pl.multiple_of(i * SUB, SUB), SUB), :] = zero
            return c

        fast = n <= COPIES
        used = jnp.where(fast, n, 1)

        def clear_copy(t, c):
            return lax.fori_loop(0, table_vregs, lambda i, c: clear(t * table_vregs + i, c), c, unroll=16)

        lax.fori_loop(0, used, clear_copy, 0)

        per_member = BATCH // blocks

        @pl.when(fast)
        def _():
            def scatter(g, c):
                for q in range(SUB // per_member):
                    where = []
                    for s in range(q * per_member, (q + 1) * per_member):
                        for b in range(blocks):
                            where.append((sidx[g * (SUB * blocks) + s * blocks + b],
                                          g * (SUB * blocks) + b * SUB + s))
                    sums = [acc[pl.ds(i, 1), :] + work[pl.ds(r, 1), :] for i, r in where]
                    for (i, _), v in zip(where, sums):
                        acc[pl.ds(i, 1), :] = v
                return c

            lax.fori_loop(0, groups, scatter, 0)

        @pl.when(jnp.logical_not(fast))
        def _():
            def one(k, c):
                m = k // blocks
                b = k - m * blocks
                g = m // SUB
                r = (g * blocks + b) * SUB + (m - g * SUB)
                i = gidx[k]
                acc[pl.ds(i, 1), :] = acc[pl.ds(i, 1), :] + work[pl.ds(r, 1), :]
                return c

            lax.fori_loop(0, members * blocks, one, 0)

        def finish(i, c):
            r = pl.multiple_of(i * SUB, SUB)

            def more(t, v):
                o = pl.multiple_of(t * full + r, SUB)
                return (v[0] + acc[pl.ds(o, SUB), :], v[1] + acc[pl.ds(o + half, SUB), :])

            v = (acc[pl.ds(r, SUB), :], acc[pl.ds(r + half, SUB), :])
            keep[pl.ds(r, SUB), :], send[pl.ds(r, SUB), :] = v
            return c

        lax.fori_loop(0, half // SUB, finish, 0, unroll=8)

        def finish_more(t, c):
            def add(i, c):
                r = pl.multiple_of(i * SUB, SUB)
                o = pl.multiple_of(t * full + r, SUB)
                keep[pl.ds(r, SUB), :] += acc[pl.ds(o, SUB), :]
                send[pl.ds(r, SUB), :] += acc[pl.ds(o + half, SUB), :]
                return c

            return lax.fori_loop(0, half // SUB, add, c, unroll=8)

        lax.fori_loop(1, used, finish_more, 0)

    rows = members * blocks
    f32 = jnp.float32
    smem = pl.BlockSpec(memory_space=pltpu.SMEM)
    vmem = pl.BlockSpec(memory_space=pltpu.VMEM)
    outs = [jax.ShapeDtypeStruct((half, BLOCK), f32)] * 2
    if second:
        outs += [jax.ShapeDtypeStruct((rows, BLOCK), f32), jax.ShapeDtypeStruct((SUB, BLOCK), f32)]
    return pl.pallas_call(
        body,
        out_shape=outs,
        in_specs=[smem] * 3 + [vmem] * (7 if second else 5),
        out_specs=[vmem] * len(outs),
        scratch_shapes=[
            pltpu.VMEM((full, BLOCK), f32),
            pltpu.VMEM((rows, BLOCK), f32),
            pltpu.VMEM((rows, BLOCK), f32),
            pltpu.VMEM((COPIES * full, BLOCK), f32),
            pltpu.VMEM((members, BLOCK), f32),
            pltpu.VMEM((members, BLOCK), f32),
            pltpu.VMEM((SUB, BLOCK), f32),
        ],
        name="iterate2" if second else "iterate1",
    )


def local(candidates, affinity, exposure, lengths, item_limit, item_duals, *, grp_size, shard_size):
    chips = shard_size // 2
    same_core = [[2 * p + c for p in range(chips)] for c in range(2)]
    swap = [(g * shard_size + s, g * shard_size + (s ^ 1)) for g in range(grp_size) for s in range(shard_size)]
    members, slots = affinity.shape
    blocks = slots // BLOCK
    groups = members // SUB
    own_items = item_limit.shape[0]
    item_count = own_items * shard_size
    own_rows = own_items // BLOCK
    padded = pad8(own_rows)
    half = chips * padded
    full = 2 * half
    core = lax.axis_index("shard") % 2

    def swap_cores(x):
        return lax.ppermute(x, AXES, swap)

    def as_rows(x):
        return x.reshape(groups, SUB, blocks, BLOCK).transpose(0, 2, 1, 3).reshape(-1, BLOCK)

    def own_block(x):
        return jnp.pad(x.reshape(own_rows, BLOCK), ((0, padded - own_rows), (0, 0)))

    def gather_halves(x):
        every = lax.all_to_all(
            jnp.broadcast_to(x[None], (chips, padded, BLOCK)), "shard", 0, 0,
            axis_index_groups=same_core, tiled=True).reshape(half, BLOCK)
        return every, swap_cores(every)

    def reduce_loads(keep, send):
        chip = keep + swap_cores(send)
        plane = lax.all_to_all(
            chip.reshape(chips, padded, BLOCK), "shard", 0, 0,
            axis_index_groups=same_core, tiled=True).sum(axis=0)
        shifted = [
            lax.ppermute(plane, "grp", [(g, (g + d) % grp_size) for g in range(grp_size)])
            for d in range(1, grp_size)
        ]
        return (plane + shifted[1]) + (shifted[0] + shifted[2])

    shard_of = candidates // own_rows
    gidx = (jnp.where(shard_of % 2 == core, 0, half) + (shard_of // 2) * padded + candidates % own_rows).reshape(-1)
    batch = gidx.reshape(-1, BATCH)
    earlier = jnp.arange(BATCH)[:, None] > jnp.arange(BATCH)[None, :]
    copy = jnp.sum((batch[:, :, None] == batch[:, None, :]) & earlier, axis=2, dtype=jnp.int32)
    sidx = (batch + full * copy).reshape(-1)
    ncopy = (jnp.max(copy) + 1).reshape(1)

    aff = as_rows(affinity)
    exp = as_rows(exposure)
    nlive = jnp.broadcast_to((lengths // BLOCK)[:, None], (members, BLOCK))
    limit = own_block(item_limit)
    duals = own_block(item_duals)

    own_d, other_d = gather_halves(duals)
    keep, send = iteration_kernel(False, groups, blocks, half, item_count)(
        gidx, sidx, ncopy, own_d, other_d, aff, exp, nlive)
    gradient = reduce_loads(keep, send) - limit

    own_g, other_g = gather_halves(gradient)
    keep, send, primal, sumsq = iteration_kernel(True, groups, blocks, half, item_count)(
        gidx, sidx, ncopy, own_d, other_d, own_g, other_g, aff, exp, nlive)
    scale = jnp.sqrt(sumsq[0:1, :] / item_count + 1e-6)
    duals = jnp.maximum(duals + 0.5 * gradient / scale, 0.0)

    gradient = reduce_loads(keep, send) - limit
    part = jnp.sum(gradient * gradient).reshape(1, 1)
    parts = lax.all_to_all(jnp.broadcast_to(part, (shard_size, 1)), "shard", 0, 0, tiled=True)
    scale = jnp.sqrt(jnp.sum(parts) / item_count + 1e-6)
    duals = jnp.maximum(duals + 0.5 * gradient / scale, 0.0)

    primal = primal.reshape(groups, blocks, SUB, BLOCK).transpose(0, 2, 1, 3).reshape(members, slots)
    return primal, duals[:own_rows].reshape(-1)


def solution(mesh):
    placed = (
        P(("grp", "shard"), None),
        P(("grp", "shard"), None),
        P(("grp", "shard"), None),
        P(("grp", "shard")),
        P("shard"),
        P("shard"),
    )

    def run(*args):
        return local(*args, grp_size=mesh.shape["grp"], shard_size=mesh.shape["shard"])

    return jax.shard_map(
        run,
        mesh=mesh,
        in_specs=placed,
        out_specs=(P(("grp", "shard"), None), P("shard")),
        check_vma=False,
    )
```

time: 280 us -> 179 us (0.64)
  blocking collectives: 122 us -> 48.7 us
  other arithmetic: 77.7 us -> 6.78 us
  Pallas kernels: 0 us -> 50.4 us
  local copies, waits for them, and re-layouts: 45 us -> 5.5 us
  starting transfers between devices: 9.42 us -> 31.4 us
  waiting for transfers between devices: 23.1 us -> 33.1 us
    all_to_all x7 -> x3, blocking collectives: 122 us -> 48.7 us  [the longest x2 33.7 us: reduce_loads(): lax.all_to_all(chip.reshape(chips, padded, BLOCK), 'shard', 0, 0, axis_in...]
    pallas_call x0 -> x2, Pallas kernels: none -> 50.4 us  [the longest x1 26.1 us: local(): iteration_kernel(True, groups, blocks, half, item_count)]
    scatter-add x2 -> x0, other arithmetic: 46.1 us -> none  [local(): jnp.zeros((block_rows, BLOCK), jnp.float32).at[flat_blocks].add(contrib)]
    gather x2 -> x0, local copies, waits for them, and re-layouts: 28.4 us -> none  [local(): all_duals.reshape(block_rows, BLOCK)[flat_blocks].reshape(members, slots)]
    reduce_sum x40 -> x5, other arithmetic: 20.6 us -> 1.62 us  [the longest x1 0.67 us: local(): part = jnp.sum(gradient * gradient).reshape(1, 1)]
    ppermute x0 -> x10, starting transfers between devices: none -> 15.8 us  [the longest x6 8.19 us: reduce_loads(): lax.ppermute(plane, 'grp', [(g, (g + d) % grp_size) for g in range(grp_si...]
    ppermute x0 -> x10, waiting for transfers between devices: none -> 13.4 us  [the longest x4 6.8 us: swap_cores(): return lax.ppermute(x, AXES, swap)]
    reshape x5 -> x1, local copies, waits for them, and re-layouts: 11.3 us -> 0.1 us  [local(): (jnp.where(shard_of % 2 == core, 0, half) + shard_of // 2 * padded + cand...]
  transfers between devices with their start and end apart: 1 -> 12, of which waited for: 1 -> 7; matrix products, arithmetic and copies ran while one was open for 0% -> 2% of each run, Pallas kernels for 0% -> 0%
where the time goes in v1:
time: 179 us; the launch traced here: 178 us
  Pallas kernels  50.4 us (28%)
  blocking collectives  48.7 us (27%)
  waiting for transfers between devices  33.1 us (18%)
  starting transfers between devices  31.4 us (18%)
  other arithmetic  6.78 us (4%)
  local copies, waits for them, and re-layouts  5.5 us (3%)
  between operations  2.13 us (1%)
    all_to_all x2, blocking collectives, reduce_loads(): lax.all_to_all(chip.reshape(chips, padded, BLOCK), 'shard', 0, 0, axis_in...  33.7 us
    pallas_call x1, Pallas kernels, local(): iteration_kernel(True, groups, blocks, half, item_count)  26.1 us
    pallas_call x1, Pallas kernels, local(): iteration_kernel(False, groups, blocks, half, item_count)  24.3 us
    all_to_all x1, blocking collectives, gather_halves(): lax.all_to_all(jnp.broadcast_to(x[None], (chips, padded, BLOCK)), 'shard'...  15.1 us
    all_to_all x1, waiting for transfers between devices, gather_halves(): lax.all_to_all(jnp.broadcast_to(x[None], (chips, padded, BLOCK)), 'shard'...  13.4 us
    all_to_all x1, starting transfers between devices, gather_halves(): lax.all_to_all(jnp.broadcast_to(x[None], (chips, padded, BLOCK)), 'shard'...  8.42 us
    ppermute x6, starting transfers between devices, reduce_loads(): lax.ppermute(plane, 'grp', [(g, (g + d) % grp_size) for g in range(grp_si...  8.19 us
    ppermute x4, starting transfers between devices, swap_cores(): return lax.ppermute(x, AXES, swap)  7.64 us
  transfers between devices with their start and end apart: 12, of which 7 were waited for; matrix products, arithmetic and copies ran while one was open for 2% of the time, Pallas kernels for 0%

profile of v1, /device:TPU:1, one launch (start us, length us, event | category | flops | bytes accessed | tf_op | source)
XLA Modules:
  0.0 178.1 jit_solution(9714004469404874052)
XLA Ops:
  0.6 0.0 copy-start.7
  0.6 0.0 copy-start.8
  0.6 0.8 pad.7
  1.5 1.0 broadcast_in_dim.15
  2.4 8.4 %all-to-all-start = ((f32[16,104,128]{2,1,0:T(8,128)}), f32[16,104,128]{2,1,0:T(8,128)S(1)}, u32[]{:S(2)}, u32[]{:S(2)}) async-start(f32[16,104,128]{2,1,0:T(8,128)} %broadcast_in_dim.15), calls=%async_computation | async-start | bytes 1703936 | tf_op jit(solution)/shard_map/all_to_all | solution.py:232
  10.9 13.4 %all-to-all-done = f32[16,104,128]{2,1,0:T(8,128)S(1)} async-done(((f32[16,104,128]{2,1,0:T(8,128)}), f32[16,104,128]{2,1,0:T(8,128)S(1)}, u32[]{:S(2)}, u32[]{:S(2)}) %all-to-all-start) | async-done | bytes 852000 | tf_op jit(solution)/shard_map/all_to_all | solution.py:232
  24.3 0.0 copy-start
  24.3 2.8 %collective-permute-start = (f32[1664,128]{1,0:T(8,128)S(1)}, f32[1664,128]{1,0:T(8,128)S(1)}, u32[]{:S(2)}, u32[]{:S(2)}) collective-permute-start(f32[1664,128]{1,0:T(8,128)S(1)} %bitcast.30), channel_id=1, source_target_pairs={{0,1},{1,0},{2,3},{3,2},{4,5},{5,4},{6,7},{7,6},{8,9},{9,8},{10,11... | collective-permute-start | bytes 2555912 | tf_op jit(solution)/shard_map/ppermute | solution.py:223
  27.1 0.0 copy-done.7
  27.1 0.1 copy.15
  27.2 0.1 reshape.78.refs_0_
  27.3 0.0 copy-start.4
  27.3 0.1 eq.28
  27.4 0.1 copy.17
  27.5 0.2 convert_reduce_fusion
  27.7 0.6 fusion.13
  29.0 0.1 copy.19
  29.1 0.1 mul.29
  29.2 0.6 add.78.refs_1_
  29.8 0.0 copy-done.8
  29.8 0.0 collective-permute-done.refs_4_
  29.8 0.0 copy-start.1
  29.8 0.9 broadcast_in_dim.16.refs_7_.refs_9_
  30.7 0.0 copy-done
  30.7 0.0 copy-done.4
  30.7 0.1 copy-done.1
  30.8 24.3 %iterate1.1 = (f32[1664,128]{1,0:T(8,128)}, f32[1664,128]{1,0:T(8,128)}) custom-call(s32[4096]{0:T(1024)} %copy-done.4, s32[4096]{0:T(1024)} %add.78.refs_1_, s32[1]{0:T(128)} %bitcast.refs_2_, f32[1664,128]{1,0:T(8,128)} %bitcast.31, f32[1664,128]{1,0:T(8,128)} %copy-done.1, f32[4096,128]{1,0:T(8,128)} %bitcast.26, f32[4096,128]{1,0:T(8,128)} %bitcast.28, ...), custom_call_target="tpu_custom_call" | custom-call | tf_op jit(solution)/shard_map/iterate1/pallas_call | solution.py:263
  55.1 0.0 collective-permute-start.1
  55.1 2.6 %collective-permute-done.1 = f32[1664,128]{1,0:T(8,128)S(1)} collective-permute-done((f32[1664,128]{1,0:T(8,128)}, f32[1664,128]{1,0:T(8,128)S(1)}, u32[]{:S(2)}, u32[]{:S(2)}) %collective-permute-start.1) | collective-permute-done | bytes 852000 | tf_op jit(solution)/shard_map/ppermute | solution.py:223
  57.7 1.3 add.80
  58.9 16.6 %all_to_all.26 = f32[16,104,128]{2,1,0:T(8,128)S(1)} all-to-all(f32[16,104,128]{2,1,0:T(8,128)S(1)} %bitcast.33), channel_id=1, replica_groups={{0,2,4,6,8,10,12,14,16,18,20,22,24,26,28,30},{1,3,5,7,9,11,13,15,17,19,..., dimensions={0} | all-to-all | bytes 1703936 | tf_op jit(solution)/shard_map/all_to_all | solution.py:239
  75.6 2.8 %collective-permute-start.4 = (f32[104,128]{1,0:T(8,128)S(1)}, f32[104,128]{1,0:T(8,128)S(1)}, u32[]{:S(2)}, u32[]{:S(2)}) collective-permute-start(f32[104,128]{1,0:T(8,128)S(1)} %reduce_sum.46), channel_id=1, source_target_pairs={{0,96},{32,0},{64,32},{96,64},{1,97},{33,1},{65,33},{97,65},{2,98}... | collective-permute-start | bytes 159752 | tf_op jit(solution)/shard_map/ppermute | solution.py:243
  78.4 0.0 collective-permute-start.3
  78.4 1.6 collective-permute-start.2
  80.1 0.0 collective-permute-done.4
  80.1 3.1 %collective-permute-done.3 = f32[104,128]{1,0:T(8,128)S(1)} collective-permute-done((f32[104,128]{1,0:T(8,128)S(1)}, f32[104,128]{1,0:T(8,128)S(1)}, u32[]{:S(2)}, u32[]{:S(2)}) %collective-permute-start.3) | collective-permute-done | bytes 53280 | tf_op jit(solution)/shard_map/ppermute | solution.py:243
  83.2 0.0 collective-permute-done.2
  83.2 0.0 copy-done.5
  83.2 0.1 broadcast_in_dim.17
  83.3 15.1 %all_to_all.27 = f32[16,104,128]{2,1,0:T(8,128)S(1)} all-to-all(f32[16,104,128]{2,1,0:T(8,128)S(1)} %broadcast_in_dim.17), channel_id=1, replica_groups={{0,2,4,6,8,10,12,14,16,18,20,22,24,26,28,30},{1,3,5,7,9,11,13,15,17,19,..., dimensions={0} | all-to-all | bytes 1703936 | tf_op jit(solution)/shard_map/all_to_all | solution.py:232
  98.4 4.5 %collective-permute-start.5 = (f32[1664,128]{1,0:T(8,128)S(1)}, f32[1664,128]{1,0:T(8,128)S(1)}, u32[]{:S(2)}, u32[]{:S(2)}) collective-permute-start(f32[1664,128]{1,0:T(8,128)S(1)} %bitcast.35), channel_id=1, source_target_pairs={{0,1},{1,0},{2,3},{3,2},{4,5},{5,4},{6,7},{7,6},{8,9},{9,8},{10,11... | collective-permute-start | bytes 2555912 | tf_op jit(solution)/shard_map/ppermute | solution.py:223
  102.9 2.0 %collective-permute-done.5.refs_6_ = f32[1664,128]{1,0:T(8,128)S(1)} collective-permute-done((f32[1664,128]{1,0:T(8,128)S(1)}, f32[1664,128]{1,0:T(8,128)S(1)}, u32[]{:S(2)}, u32[]{:S(2)}) %collective-permute-start.5) | collective-permute-done | bytes 852000 | tf_op jit(solution)/shard_map/ppermute | solution.py:223
  104.9 0.0 copy-done.2
  104.9 0.9 copy-done.3
  105.8 26.1 %iterate2.1 = (f32[1664,128]{1,0:T(8,128)}, f32[1664,128]{1,0:T(8,128)}, f32[4096,128]{1,0:T(8,128)}, f32[8,128]{1,0:T(8,128)}) custom-call(s32[4096]{0:T(1024)} %copy-done.4, s32[4096]{0:T(1024)} %add.78.refs_1_, s32[1]{0:T(128)} %bitcast.refs_2_, f32[1664,128]{1,0:T(8,128)} %bitcast.32, f32[1664,128]{1,0:T(8,128)} %copy-done.1, f32[1664,128]{1,0:T(8,128)} %bitcast.36, ...), custom_call_target="tpu_custom_call" | custom-call | tf_op jit(solution)/shard_map/iterate2/pallas_call | solution.py:268
  131.9 0.4 collective-permute-start.6
  132.3 2.2 %collective-permute-done.6 = f32[1664,128]{1,0:T(8,128)S(1)} collective-permute-done((f32[1664,128]{1,0:T(8,128)}, f32[1664,128]{1,0:T(8,128)S(1)}, u32[]{:S(2)}, u32[]{:S(2)}) %collective-permute-start.6) | collective-permute-done | bytes 852000 | tf_op jit(solution)/shard_map/ppermute | solution.py:223
  134.5 1.2 add.87
  135.8 0.0 copy-start.6
  135.8 17.0 %all_to_all.28 = f32[16,104,128]{2,1,0:T(8,128)S(1)} all-to-all(f32[16,104,128]{2,1,0:T(8,128)S(1)} %bitcast.34), channel_id=1, replica_groups={{0,2,4,6,8,10,12,14,16,18,20,22,24,26,28,30},{1,3,5,7,9,11,13,15,17,19,..., dimensions={0} | all-to-all | bytes 1703936 | tf_op jit(solution)/shard_map/all_to_all | solution.py:239
  152.9 2.5 %collective-permute-start.9 = (f32[104,128]{1,0:T(8,128)S(1)}, f32[104,128]{1,0:T(8,128)S(1)}, u32[]{:S(2)}, u32[]{:S(2)}) collective-permute-start(f32[104,128]{1,0:T(8,128)S(1)} %reduce_sum.47), channel_id=1, source_target_pairs={{0,96},{32,0},{64,32},{96,64},{1,97},{33,1},{65,33},{97,65},{2,98}... | collective-permute-start | bytes 159752 | tf_op jit(solution)/shard_map/ppermute | solution.py:243
  155.3 0.0 collective-permute-start.8
  155.3 1.3 collective-permute-start.7
  156.6 0.0 collective-permute-done.9
  156.6 3.5 %collective-permute-done.8 = f32[104,128]{1,0:T(8,128)S(1)} collective-permute-done((f32[104,128]{1,0:T(8,128)S(1)}, f32[104,128]{1,0:T(8,128)S(1)}, u32[]{:S(2)}, u32[]{:S(2)}) %collective-permute-start.8) | collective-permute-done | bytes 53280 | tf_op jit(solution)/shard_map/ppermute | solution.py:243
  160.1 0.0 collective-permute-done.7
  160.1 0.7 multiply_reduce_fusion
  160.8 1.2 broadcast_in_dim.18
  162.0 7.2 %all-to-all-start.4 = ((f32[32,1,1]{2,1,0:T(1,128)}), f32[32,1,1]{2,1,0:T(1,128)S(1)}, u32[]{:S(2)}, u32[]{:S(2)}) async-start(f32[32,1,1]{2,1,0:T(1,128)} %broadcast_in_dim.18), calls=%async_computation.4 | async-start | bytes 32768 | tf_op jit(solution)/shard_map/all_to_all | solution.py:275
  169.2 0.7 sqrt_bitcast_fusion
  169.9 6.2 %all-to-all-done.4 = f32[32,1,1]{2,1,0:T(1,128)S(1)} async-done(((f32[32,1,1]{2,1,0:T(1,128)}), f32[32,1,1]{2,1,0:T(1,128)S(1)}, u32[]{:S(2)}, u32[]{:S(2)}) %all-to-all-start.4) | async-done | bytes 160 | tf_op jit(solution)/shard_map/all_to_all | solution.py:275
  176.1 0.6 reduce_sum.49
  177.4 0.0 copy-done.6
  177.4 0.6 fusion.3
  (9 shorter events, 0.2 us)
Async XLA Ops:
  0.6 26.4 %copy-start.7 = (s32[256,16]{0,1:T(8,128)S(1)}, s32[256,16]{0,1:T(8,128)}, u32[]{:S(2)}) copy-start(s32[256,16]{0,1:T(8,128)} %param.6) | copy-start | bytes 49156
  0.6 29.2 %copy-start.8 = (s32[256]{0:T(256)S(1)}, s32[256]{0:T(256)}, u32[]{:S(2)}) copy-start(s32[256]{0:T(256)} %param.9) | copy-start | bytes 3076
  2.4 21.9 %all-to-all-start = ((f32[16,104,128]{2,1,0:T(8,128)}), f32[16,104,128]{2,1,0:T(8,128)S(1)}, u32[]{:S(2)}, u32[]{:S(2)}) async-start(f32[16,104,128]{2,1,0:T(8,128)} %broadcast_in_dim.15), calls=%async_computation | async-start | bytes 1703936 | tf_op jit(solution)/shard_map/all_to_all | solution.py:232
  24.3 6.4 %copy-start = (f32[16,104,128]{2,1,0:T(8,128)}, f32[16,104,128]{2,1,0:T(8,128)S(1)}, u32[]{:S(2)}) copy-start(f32[16,104,128]{2,1,0:T(8,128)S(1)} %all-to-all-done) | copy-start | bytes 2555908
  24.3 5.5 %collective-permute-start = (f32[1664,128]{1,0:T(8,128)S(1)}, f32[1664,128]{1,0:T(8,128)S(1)}, u32[]{:S(2)}, u32[]{:S(2)}) collective-permute-start(f32[1664,128]{1,0:T(8,128)S(1)} %bitcast.30), channel_id=1, source_target_pairs={{0,1},{1,0},{2,3},{3,2},{4,5},{5,4},{6,7},{7,6},{8,9},{9,8},{10,11... | collective-permute-start | bytes 2555912 | tf_op jit(solution)/shard_map/ppermute | solution.py:223
  27.3 3.4 %copy-start.4 = (s32[4096]{0:T(1024)}, s32[4096]{0:T(1024)S(1)}, u32[]{:S(2)}) copy-start(s32[4096]{0:T(1024)S(1)} %reshape.78.refs_0_) | copy-start | bytes 49156
  29.8 1.0 copy-start.1
  55.1 2.6 %collective-permute-start.1 = (f32[1664,128]{1,0:T(8,128)}, f32[1664,128]{1,0:T(8,128)S(1)}, u32[]{:S(2)}, u32[]{:S(2)}) collective-permute-start(f32[1664,128]{1,0:T(8,128)} %get-tuple-element.9), channel_id=1, source_target_pairs={{0,1},{1,0},{2,3},{3,2},{4,5},{5,4},{6,7},{7,6},{8,9},{9,8},{10,11... | collective-permute-start | bytes 2555912 | tf_op jit(solution)/shard_map/ppermute | solution.py:223
  57.7 25.5 %copy-start.5 = (f32[12800]{0:T(1024)S(1)}, f32[12800]{0:T(1024)}, u32[]{:S(2)}) copy-start(f32[12800]{0:T(1024)} %param.10) | copy-start | bytes 153604
  75.6 4.5 %collective-permute-start.4 = (f32[104,128]{1,0:T(8,128)S(1)}, f32[104,128]{1,0:T(8,128)S(1)}, u32[]{:S(2)}, u32[]{:S(2)}) collective-permute-start(f32[104,128]{1,0:T(8,128)S(1)} %reduce_sum.46), channel_id=1, source_target_pairs={{0,96},{32,0},{64,32},{96,64},{1,97},{33,1},{65,33},{97,65},{2,98}... | collective-permute-start | bytes 159752 | tf_op jit(solution)/shard_map/ppermute | solution.py:243
  78.4 4.8 %collective-permute-start.3 = (f32[104,128]{1,0:T(8,128)S(1)}, f32[104,128]{1,0:T(8,128)S(1)}, u32[]{:S(2)}, u32[]{:S(2)}) collective-permute-start(f32[104,128]{1,0:T(8,128)S(1)} %reduce_sum.46), channel_id=1, source_target_pairs={{0,32},{32,64},{64,96},{96,0},{1,33},{33,65},{65,97},{97,1},{2,34}... | collective-permute-start | bytes 159752 | tf_op jit(solution)/shard_map/ppermute | solution.py:243
  78.4 4.8 %collective-permute-start.2 = (f32[104,128]{1,0:T(8,128)S(1)}, f32[104,128]{1,0:T(8,128)S(1)}, u32[]{:S(2)}, u32[]{:S(2)}) collective-permute-start(f32[104,128]{1,0:T(8,128)S(1)} %reduce_sum.46), channel_id=1, source_target_pairs={{0,64},{32,96},{64,0},{96,32},{1,65},{33,97},{65,1},{97,33},{2,66}... | collective-permute-start | bytes 159752 | tf_op jit(solution)/shard_map/ppermute | solution.py:243
  98.4 6.5 %copy-start.2 = (f32[16,104,128]{2,1,0:T(8,128)}, f32[16,104,128]{2,1,0:T(8,128)S(1)}, u32[]{:S(2)}) copy-start(f32[16,104,128]{2,1,0:T(8,128)S(1)} %all_to_all.27) | copy-start | bytes 2555908
  98.4 6.5 %collective-permute-start.5 = (f32[1664,128]{1,0:T(8,128)S(1)}, f32[1664,128]{1,0:T(8,128)S(1)}, u32[]{:S(2)}, u32[]{:S(2)}) collective-permute-start(f32[1664,128]{1,0:T(8,128)S(1)} %bitcast.35), channel_id=1, source_target_pairs={{0,1},{1,0},{2,3},{3,2},{4,5},{5,4},{6,7},{7,6},{8,9},{9,8},{10,11... | collective-permute-start | bytes 2555912 | tf_op jit(solution)/shard_map/ppermute | solution.py:223
  104.9 0.9 copy-start.3
  131.9 2.6 %collective-permute-start.6 = (f32[1664,128]{1,0:T(8,128)}, f32[1664,128]{1,0:T(8,128)S(1)}, u32[]{:S(2)}, u32[]{:S(2)}) collective-permute-start(f32[1664,128]{1,0:T(8,128)} %get-tuple-element.13), channel_id=1, source_target_pairs={{0,1},{1,0},{2,3},{3,2},{4,5},{5,4},{6,7},{7,6},{8,9},{9,8},{10,11... | collective-permute-start | bytes 2555912 | tf_op jit(solution)/shard_map/ppermute | solution.py:223
  135.8 41.6 %copy-start.6 = (f32[12800]{0:T(1024)S(1)}, f32[12800]{0:T(1024)}, u32[]{:S(2)}) copy-start(f32[12800]{0:T(1024)} %param.11) | copy-start | bytes 153604
  152.9 3.7 %collective-permute-start.9 = (f32[104,128]{1,0:T(8,128)S(1)}, f32[104,128]{1,0:T(8,128)S(1)}, u32[]{:S(2)}, u32[]{:S(2)}) collective-permute-start(f32[104,128]{1,0:T(8,128)S(1)} %reduce_sum.47), channel_id=1, source_target_pairs={{0,96},{32,0},{64,32},{96,64},{1,97},{33,1},{65,33},{97,65},{2,98}... | collective-permute-start | bytes 159752 | tf_op jit(solution)/shard_map/ppermute | solution.py:243
  155.3 4.8 %collective-permute-start.8 = (f32[104,128]{1,0:T(8,128)S(1)}, f32[104,128]{1,0:T(8,128)S(1)}, u32[]{:S(2)}, u32[]{:S(2)}) collective-permute-start(f32[104,128]{1,0:T(8,128)S(1)} %reduce_sum.47), channel_id=1, source_target_pairs={{0,32},{32,64},{64,96},{96,0},{1,33},{33,65},{65,97},{97,1},{2,34}... | collective-permute-start | bytes 159752 | tf_op jit(solution)/shard_map/ppermute | solution.py:243
  155.3 4.8 %collective-permute-start.7 = (f32[104,128]{1,0:T(8,128)S(1)}, f32[104,128]{1,0:T(8,128)S(1)}, u32[]{:S(2)}, u32[]{:S(2)}) collective-permute-start(f32[104,128]{1,0:T(8,128)S(1)} %reduce_sum.47), channel_id=1, source_target_pairs={{0,64},{32,96},{64,0},{96,32},{1,65},{33,97},{65,1},{97,33},{2,66}... | collective-permute-start | bytes 159752 | tf_op jit(solution)/shard_map/ppermute | solution.py:243
  162.0 14.1 %all-to-all-start.4 = ((f32[32,1,1]{2,1,0:T(1,128)}), f32[32,1,1]{2,1,0:T(1,128)S(1)}, u32[]{:S(2)}, u32[]{:S(2)}) async-start(f32[32,1,1]{2,1,0:T(1,128)} %broadcast_in_dim.18), calls=%async_computation.4 | async-start | bytes 32768 | tf_op jit(solution)/shard_map/all_to_all | solution.py:275

commit v2 on v1

v2 whole, which is shorter than its diff:
```python
import jax
import jax.numpy as jnp
from jax import lax
from jax.experimental import pallas as pl
from jax.experimental.pallas import tpu as pltpu
from jax.sharding import PartitionSpec as P

BLOCK = 128
BISECT = 16
SUB = 8
DEAD = -1e30

AXES = ("grp", "shard")


def pad8(n):
    return -(-n // SUB) * SUB


def iteration_kernel(second, groups, blocks, half, item_count):
    full = 2 * half
    members = groups * SUB
    group_rows = SUB * blocks
    part = groups // 2
    per_pass = part // BISECT
    assert per_pass * BISECT * 2 == groups
    f32 = jnp.float32

    def body(*refs):
        if second:
            (gidx, sidx, ncopy, own_d, other_d, own_g, other_g, aff, exp, nlive,
             keep, send, primal, sumsq, table, work_a, work_b, acc, lo, up) = refs
        else:
            (gidx, sidx, ncopy, own_d, other_d, aff, exp, nlive,
             keep, send, table, work_a, work_b, acc, lo, up) = refs
        works = (work_a, work_b)

        if second:
            def square(i, s):
                r = pl.multiple_of(i * SUB, SUB)
                a = own_g[pl.ds(r, SUB), :]
                b = other_g[pl.ds(r, SUB), :]
                return s + (a * a + b * b)

            s = lax.fori_loop(0, half // SUB, square, jnp.zeros((SUB, BLOCK), f32), unroll=8)
            total = jnp.sum(jnp.sum(s, axis=1, keepdims=True), axis=0, keepdims=True)
            total = jnp.broadcast_to(total, (SUB, BLOCK))
            sumsq[...] = total
            scale = jnp.sqrt(total / item_count + 1e-6)

            def fill_table(i, c):
                r = pl.multiple_of(i * SUB, SUB)
                for d, g, off in ((own_d, own_g, 0), (other_d, other_g, half)):
                    table[pl.ds(r + off, SUB), :] = jnp.maximum(
                        d[pl.ds(r, SUB), :] + 0.5 * g[pl.ds(r, SUB), :] / scale, 0.0)
                return c
        else:
            def fill_table(i, c):
                r = pl.multiple_of(i * SUB, SUB)
                table[pl.ds(r, SUB), :] = own_d[pl.ds(r, SUB), :]
                table[pl.ds(r + half, SUB), :] = other_d[pl.ds(r, SUB), :]
                return c

        lax.fori_loop(0, half // SUB, fill_table, 0, unroll=8)

        n = ncopy[0]
        zero = jnp.zeros((SUB, BLOCK), f32)

        def clear(i, c):
            acc[pl.ds(pl.multiple_of(i * SUB, SUB), SUB), :] = zero
            return c

        lax.fori_loop(
            0, n, lambda t, c: lax.fori_loop(
                0, full // SUB, lambda i, c: clear(t * (full // SUB) + i, c), c, unroll=16), 0)

        def gather_steps(h, g):
            base = pl.multiple_of((h * part + g) * group_rows, group_rows)
            here = pl.multiple_of(g * group_rows, group_rows)
            work = works[h].at[pl.ds(here, group_rows), :]
            a_rows = aff.at[pl.ds(base, group_rows), :]
            e_rows = exp.at[pl.ds(base, group_rows), :]
            ids = gidx.at[pl.ds(base, group_rows)]
            mrows = pl.ds(pl.multiple_of((h * part + g) * SUB, SUB), SUB)
            live = nlive[mrows, :]
            peak = [jnp.full((SUB, BLOCK), DEAD, f32)]

            def step(b):
                for s in range(SUB):
                    work[pl.ds(b * SUB + s, 1), :] = table[pl.ds(ids[s * blocks + b], 1), :]
                rows = pl.ds(b * SUB, SUB)
                v = (a_rows[rows, :] - e_rows[rows, :] * work[rows, :]) * 2.0
                v = jnp.where(live > b, v, DEAD)
                work[rows, :] = v
                peak[0] = jnp.maximum(peak[0], v)

            def end():
                up[mrows, :] = peak[0]

            return [lambda b=b: step(b) for b in range(blocks)] + [end]

        def start_bisection(h):
            for g in range(part):
                rows = pl.ds((h * part + g) * SUB, SUB)
                up[rows, :] = jnp.broadcast_to(jnp.max(up[rows, :], axis=1, keepdims=True), (SUB, BLOCK))
                lo[rows, :] = zero

        def bisect_steps(h):
            def step(g):
                rows = pl.ds((h * part + g) * SUB, SUB)
                mid = (lo[rows, :] + up[rows, :]) * 0.5
                sums = [None, None]
                for b in range(blocks):
                    v = jnp.clip(works[h][pl.ds(g * group_rows + b * SUB, SUB), :] - mid, 0.0, 1.0)
                    sums[b % 2] = v if sums[b % 2] is None else sums[b % 2] + v
                fill = jnp.broadcast_to(jnp.sum(sums[0] + sums[1], axis=1, keepdims=True), (SUB, BLOCK))
                bigger = fill > 1.0
                lo[rows, :] = jnp.where(bigger, mid, lo[rows, :])
                up[rows, :] = jnp.where(bigger, up[rows, :], mid)

            return [lambda g=g: step(g) for g in range(part)]

        def scatter_steps(h, g):
            base = pl.multiple_of((h * part + g) * group_rows, group_rows)
            here = pl.multiple_of(g * group_rows, group_rows)
            work = works[h].at[pl.ds(here, group_rows), :]
            e_rows = exp.at[pl.ds(base, group_rows), :]
            ids = sidx.at[pl.ds(base, group_rows)]
            mrows = pl.ds(pl.multiple_of((h * part + g) * SUB, SUB), SUB)

            def allocate():
                th = up[mrows, :]
                live = nlive[mrows, :]
                for b in range(blocks):
                    rows = pl.ds(b * SUB, SUB)
                    x = jnp.where(live > b, jnp.clip(work[rows, :] - th, 0.0, 1.0), 0.0)
                    if second:
                        primal[pl.ds(base + b * SUB, SUB), :] = x
                    work[rows, :] = e_rows[rows, :] * x

            def add(s):
                where = [ids[s * blocks + b] for b in range(blocks)]
                sums = [acc[pl.ds(i, 1), :] + work[pl.ds(b * SUB + s, 1), :] for b, i in enumerate(where)]
                for i, v in zip(where, sums):
                    acc[pl.ds(i, 1), :] = v

            return [allocate] + [lambda s=s: add(s) for s in range(SUB)]

        def together(first, other):
            done = 0
            for k, f in enumerate(first):
                f()
                want = (k + 1) * len(other) // len(first)
                for o in other[done:want]:
                    o()
                done = want

        def run(steps):
            for f in steps:
                f()

        def loop(count, f):
            def trip(i, c):
                f(i)
                return c

            lax.fori_loop(0, count, trip, 0)

        def several(steps, h, p):
            return [f for k in range(per_pass) for f in steps(h, p * per_pass + k)]

        loop(part, lambda g: run(gather_steps(0, g)))
        start_bisection(0)
        loop(BISECT, lambda p: together(bisect_steps(0), several(gather_steps, 1, p)))
        start_bisection(1)
        loop(BISECT, lambda p: together(bisect_steps(1), several(scatter_steps, 0, p)))
        loop(part, lambda g: run(scatter_steps(1, g)))

        def finish(i, c):
            r = pl.multiple_of(i * SUB, SUB)
            keep[pl.ds(r, SUB), :] = acc[pl.ds(r, SUB), :]
            send[pl.ds(r, SUB), :] = acc[pl.ds(r + half, SUB), :]
            return c

        lax.fori_loop(0, half // SUB, finish, 0, unroll=8)

        def finish_copy(t, c):
            def more(i, c):
                r = pl.multiple_of(i * SUB, SUB)
                o = pl.multiple_of(t * full + r, SUB)
                keep[pl.ds(r, SUB), :] += acc[pl.ds(o, SUB), :]
                send[pl.ds(r, SUB), :] += acc[pl.ds(o + half, SUB), :]
                return c

            return lax.fori_loop(0, half // SUB, more, c, unroll=8)

        lax.fori_loop(1, n, finish_copy, 0)

    rows = members * blocks
    smem = pl.BlockSpec(memory_space=pltpu.SMEM)
    vmem = pl.BlockSpec(memory_space=pltpu.VMEM)
    outs = [jax.ShapeDtypeStruct((half, BLOCK), f32)] * 2
    if second:
        outs += [jax.ShapeDtypeStruct((rows, BLOCK), f32), jax.ShapeDtypeStruct((SUB, BLOCK), f32)]
    return pl.pallas_call(
        body,
        out_shape=outs,
        in_specs=[smem] * 3 + [vmem] * (7 if second else 5),
        out_specs=[vmem] * len(outs),
        scratch_shapes=[
            pltpu.VMEM((full, BLOCK), f32),
            pltpu.VMEM((rows // 2, BLOCK), f32),
            pltpu.VMEM((rows // 2, BLOCK), f32),
            pltpu.VMEM((blocks * full, BLOCK), f32),
            pltpu.VMEM((members, BLOCK), f32),
            pltpu.VMEM((members, BLOCK), f32),
        ],
        compiler_params=pltpu.CompilerParams(vmem_limit_bytes=44 << 20),
        name="iterate2" if second else "iterate1",
    )


def local(candidates, affinity, exposure, lengths, item_limit, item_duals, *, grp_size, shard_size):
    chips = shard_size // 2
    same_core = [[2 * p + c for p in range(chips)] for c in range(2)]
    swap = [(g * shard_size + s, g * shard_size + (s ^ 1)) for g in range(grp_size) for s in range(shard_size)]
    members, slots = affinity.shape
    blocks = slots // BLOCK
    groups = members // SUB
    own_items = item_limit.shape[0]
    item_count = own_items * shard_size
    own_rows = own_items // BLOCK
    padded = pad8(own_rows)
    half = chips * padded
    full = 2 * half
    core = lax.axis_index("shard") % 2

    def swap_cores(x):
        return lax.ppermute(x, AXES, swap)

    def as_rows(x):
        return x.reshape(groups, SUB, blocks, BLOCK).transpose(0, 2, 1, 3).reshape(-1, BLOCK)

    def own_block(x):
        return jnp.pad(x.reshape(own_rows, BLOCK), ((0, padded - own_rows), (0, 0)))

    def gather_halves(x):
        every = lax.all_to_all(
            jnp.broadcast_to(x[None], (chips, padded, BLOCK)), "shard", 0, 0,
            axis_index_groups=same_core, tiled=True).reshape(half, BLOCK)
        return every, swap_cores(every)

    def reduce_loads(keep, send):
        chip = keep + swap_cores(send)
        plane = lax.all_to_all(
            chip.reshape(chips, padded, BLOCK), "shard", 0, 0,
            axis_index_groups=same_core, tiled=True).sum(axis=0)
        shifted = [
            lax.ppermute(plane, "grp", [(g, (g + d) % grp_size) for g in range(grp_size)])
            for d in range(1, grp_size)
        ]
        return (plane + shifted[1]) + (shifted[0] + shifted[2])

    shard_of = candidates // own_rows
    gidx = (jnp.where(shard_of % 2 == core, 0, half) + (shard_of // 2) * padded + candidates % own_rows).reshape(-1)
    batch = gidx.reshape(-1, blocks)
    earlier = jnp.arange(blocks)[:, None] > jnp.arange(blocks)[None, :]
    copy = jnp.sum((batch[:, :, None] == batch[:, None, :]) & earlier, axis=2, dtype=jnp.int32)
    sidx = (batch + full * copy).reshape(-1)
    ncopy = (jnp.max(copy) + 1).reshape(1)

    aff = as_rows(affinity)
    exp = as_rows(exposure)
    nlive = jnp.broadcast_to((lengths // BLOCK)[:, None], (members, BLOCK))
    limit = own_block(item_limit)
    duals = own_block(item_duals)

    own_d, other_d = gather_halves(duals)
    keep, send = iteration_kernel(False, groups, blocks, half, item_count)(
        gidx, sidx, ncopy, own_d, other_d, aff, exp, nlive)
    gradient = reduce_loads(keep, send) - limit

    own_g, other_g = gather_halves(gradient)
    keep, send, primal, sumsq = iteration_kernel(True, groups, blocks, half, item_count)(
        gidx, sidx, ncopy, own_d, other_d, own_g, other_g, aff, exp, nlive)
    scale = jnp.sqrt(sumsq[0:1, :] / item_count + 1e-6)
    duals = jnp.maximum(duals + 0.5 * gradient / scale, 0.0)

    gradient = reduce_loads(keep, send) - limit
    part = jnp.sum(gradient * gradient).reshape(1, 1)
    parts = lax.all_to_all(jnp.broadcast_to(part, (shard_size, 1)), "shard", 0, 0, tiled=True)
    scale = jnp.sqrt(jnp.sum(parts) / item_count + 1e-6)
    duals = jnp.maximum(duals + 0.5 * gradient / scale, 0.0)

    primal = primal.reshape(groups, blocks, SUB, BLOCK).transpose(0, 2, 1, 3).reshape(members, slots)
    return primal, duals[:own_rows].reshape(-1)


def solution(mesh):
    placed = (
        P(("grp", "shard"), None),
        P(("grp", "shard"), None),
        P(("grp", "shard"), None),
        P(("grp", "shard")),
        P("shard"),
        P("shard"),
    )

    def run(*args):
        return local(*args, grp_size=mesh.shape["grp"], shard_size=mesh.shape["shard"])

    return jax.shard_map(
        run,
        mesh=mesh,
        in_specs=placed,
        out_specs=(P(("grp", "shard"), None), P("shard")),
        check_vma=False,
    )
```

time: 179 us -> 160 us (0.89)
  Pallas kernels: 50.4 us -> 33.7 us
  other arithmetic: 6.78 us -> 4.18 us
    pallas_call x1, Pallas kernels: 24.3 us -> 15.8 us  [local(): iteration_kernel(False, groups, blocks, half, item_count)]
    pallas_call x1, Pallas kernels: 26.1 us -> 17.9 us  [local(): iteration_kernel(True, groups, blocks, half, item_count)]
    add x2, other arithmetic: 2.49 us -> 0.17 us  [reduce_loads(): chip = keep + swap_cores(send)]
  transfers between devices with their start and end apart: 12 -> 12, of which waited for: 7 -> 8; matrix products, arithmetic and copies ran while one was open for 2% -> 1% of each run, Pallas kernels for 0% -> 0%
where the time goes in v2:
time: 160 us
  blocking collectives  49.3 us (31%)
  Pallas kernels  33.7 us (21%)
  waiting for transfers between devices  33.2 us (21%)
  starting transfers between devices  31.8 us (20%)
  local copies, waits for them, and re-layouts  5.25 us (3%)
  other arithmetic  4.18 us (3%)
  between operations  2.17 us (1%)
    all_to_all x2, blocking collectives, reduce_loads(): lax.all_to_all(chip.reshape(chips, padded, BLOCK), 'shard', 0, 0, axis_in...  34.2 us
    pallas_call x1, Pallas kernels, local(): iteration_kernel(True, groups, blocks, half, item_count)  17.9 us
    pallas_call x1, Pallas kernels, local(): iteration_kernel(False, groups, blocks, half, item_count)  15.8 us
    all_to_all x1, blocking collectives, gather_halves(): lax.all_to_all(jnp.broadcast_to(x[None], (chips, padded, BLOCK)), 'shard'...  15.2 us
    all_to_all x1, waiting for transfers between devices, gather_halves(): lax.all_to_all(jnp.broadcast_to(x[None], (chips, padded, BLOCK)), 'shard'...  13.4 us
    all_to_all x1, starting transfers between devices, gather_halves(): lax.all_to_all(jnp.broadcast_to(x[None], (chips, padded, BLOCK)), 'shard'...  8.42 us
    ppermute x6, starting transfers between devices, reduce_loads(): lax.ppermute(plane, 'grp', [(g, (g + d) % grp_size) for g in range(grp_si...  8.18 us
    ppermute x4, starting transfers between devices, swap_cores(): return lax.ppermute(x, AXES, swap)  8.03 us
  transfers between devices with their start and end apart: 12, of which 8 were waited for; matrix products, arithmetic and copies ran while one was open for 1% of the time, Pallas kernels for 0%

profile of v2, /device:TPU:1, one launch (start us, length us, event | category | flops | bytes accessed | tf_op | source)
XLA Modules:
  0.0 159.6 jit_solution(16970835768912779564)
XLA Ops:
  0.6 0.0 copy-start.5
  0.6 0.0 copy-start.6
  0.6 0.0 copy-start
  0.7 1.0 pad.7
  1.6 1.0 broadcast_in_dim.15
  2.6 8.4 %all-to-all-start = ((f32[16,104,128]{2,1,0:T(8,128)}), f32[16,104,128]{2,1,0:T(8,128)S(1)}, u32[]{:S(2)}, u32[]{:S(2)}) async-start(f32[16,104,128]{2,1,0:T(8,128)} %broadcast_in_dim.15), calls=%async_computation | async-start | bytes 1703936 | tf_op jit(solution)/shard_map/all_to_all | solution.py:248
  11.0 13.4 %all-to-all-done = f32[16,104,128]{2,1,0:T(8,128)S(1)} async-done(((f32[16,104,128]{2,1,0:T(8,128)}), f32[16,104,128]{2,1,0:T(8,128)S(1)}, u32[]{:S(2)}, u32[]{:S(2)}) %all-to-all-start) | async-done | bytes 852000 | tf_op jit(solution)/shard_map/all_to_all | solution.py:248
  24.5 2.8 %collective-permute-start = (f32[1664,128]{1,0:T(8,128)S(1)}, f32[1664,128]{1,0:T(8,128)}, u32[]{:S(2)}, u32[]{:S(2)}) collective-permute-start(f32[1664,128]{1,0:T(8,128)S(1)} %bitcast.30), channel_id=1, source_target_pairs={{0,1},{1,0},{2,3},{3,2},{4,5},{5,4},{6,7},{7,6},{8,9},{9,8},{10,11... | collective-permute-start | bytes 2555912 | tf_op jit(solution)/shard_map/ppermute | solution.py:239
  27.2 0.0 copy-done.5
  27.3 0.1 copy.16
  27.4 0.1 convert_reduce_fusion
  27.5 0.6 fusion.13
  28.8 0.1 copy.17
  28.9 0.1 reshape.77.refs_1_
  29.0 0.1 reshape.76.refs_0_
  29.1 0.0 copy-done.6
  29.1 0.2 collective-permute-done.refs_4_
  29.4 0.1 broadcast_in_dim.16.refs_7_.refs_9_
  29.4 0.0 copy-done
  29.5 0.0 copy-start.1
  29.5 1.6 copy-done.1
  31.0 15.8 %iterate1.1 = (f32[1664,128]{1,0:T(8,128)S(1)}, f32[1664,128]{1,0:T(8,128)S(1)}) custom-call(s32[4096]{0:T(1024)S(1)} %reshape.76.refs_0_, s32[4096]{0:T(1024)S(1)} %reshape.77.refs_1_, s32[1]{0:T(128)} %bitcast.refs_2_, f32[1664,128]{1,0:T(8,128)S(1)} %bitcast.31, f32[1664,128]{1,0:T(8,128)} %collective-permute-done.refs_4_, f32[4096,128]{1,0:T(8,128)S(1)} %bitcast.26, ...), custom_call_target="tpu_custom_call" | custom-call | tf_op jit(solution)/shard_map/iterate1/pallas_call | solution.py:279
  46.9 0.5 collective-permute-start.1
  47.4 2.0 %collective-permute-done.1 = f32[1664,128]{1,0:T(8,128)S(1)} collective-permute-done((f32[1664,128]{1,0:T(8,128)S(1)}, f32[1664,128]{1,0:T(8,128)S(1)}, u32[]{:S(2)}, u32[]{:S(2)}) %collective-permute-start.1) | collective-permute-done | bytes 852000 | tf_op jit(solution)/shard_map/ppermute | solution.py:239
  49.4 0.0 copy-start.3
  49.4 0.1 add.79
  49.5 17.1 %all_to_all.26 = f32[16,104,128]{2,1,0:T(8,128)} all-to-all(f32[16,104,128]{2,1,0:T(8,128)S(1)} %bitcast.35), channel_id=1, replica_groups={{0,2,4,6,8,10,12,14,16,18,20,22,24,26,28,30},{1,3,5,7,9,11,13,15,17,19,..., dimensions={0} | all-to-all | bytes 1703936 | tf_op jit(solution)/shard_map/all_to_all | solution.py:255
  66.6 1.2 reduce_sum.46
  67.8 0.0 copy-start.2
  67.8 2.8 %collective-permute-start.4 = (f32[104,128]{1,0:T(8,128)S(1)}, f32[104,128]{1,0:T(8,128)S(1)}, u32[]{:S(2)}, u32[]{:S(2)}) collective-permute-start(f32[104,128]{1,0:T(8,128)S(1)} %reduce_sum.46), channel_id=1, source_target_pairs={{0,96},{32,0},{64,32},{96,64},{1,97},{33,1},{65,33},{97,65},{2,98}... | collective-permute-start | bytes 159752 | tf_op jit(solution)/shard_map/ppermute | solution.py:259
  70.6 0.0 collective-permute-start.3
  70.6 1.6 %collective-permute-start.2 = (f32[104,128]{1,0:T(8,128)S(1)}, f32[104,128]{1,0:T(8,128)S(1)}, u32[]{:S(2)}, u32[]{:S(2)}) collective-permute-start(f32[104,128]{1,0:T(8,128)S(1)} %reduce_sum.46), channel_id=1, source_target_pairs={{0,64},{32,96},{64,0},{96,32},{1,65},{33,97},{65,1},{97,33},{2,66}... | collective-permute-start | bytes 159752 | tf_op jit(solution)/shard_map/ppermute | solution.py:259
  72.2 0.0 collective-permute-done.4
  72.3 3.1 %collective-permute-done.3 = f32[104,128]{1,0:T(8,128)S(1)} collective-permute-done((f32[104,128]{1,0:T(8,128)S(1)}, f32[104,128]{1,0:T(8,128)S(1)}, u32[]{:S(2)}, u32[]{:S(2)}) %collective-permute-start.3) | collective-permute-done | bytes 53280 | tf_op jit(solution)/shard_map/ppermute | solution.py:259
  75.4 0.0 collective-permute-done.2
  75.4 0.0 copy-done.3
  75.4 0.1 broadcast_in_dim.17
  75.5 15.2 %all_to_all.27 = f32[16,104,128]{2,1,0:T(8,128)S(1)} all-to-all(f32[16,104,128]{2,1,0:T(8,128)S(1)} %broadcast_in_dim.17), channel_id=1, replica_groups={{0,2,4,6,8,10,12,14,16,18,20,22,24,26,28,30},{1,3,5,7,9,11,13,15,17,19,..., dimensions={0} | all-to-all | bytes 1703936 | tf_op jit(solution)/shard_map/all_to_all | solution.py:248
  90.6 4.4 %collective-permute-start.5 = (f32[1664,128]{1,0:T(8,128)S(1)}, f32[1664,128]{1,0:T(8,128)S(1)}, u32[]{:S(2)}, u32[]{:S(2)}) collective-permute-start(f32[1664,128]{1,0:T(8,128)S(1)} %bitcast.33), channel_id=1, source_target_pairs={{0,1},{1,0},{2,3},{3,2},{4,5},{5,4},{6,7},{7,6},{8,9},{9,8},{10,11... | collective-permute-start | bytes 2555912 | tf_op jit(solution)/shard_map/ppermute | solution.py:239
  95.1 2.0 %collective-permute-done.5.refs_6_ = f32[1664,128]{1,0:T(8,128)S(1)} collective-permute-done((f32[1664,128]{1,0:T(8,128)S(1)}, f32[1664,128]{1,0:T(8,128)S(1)}, u32[]{:S(2)}, u32[]{:S(2)}) %collective-permute-start.5) | collective-permute-done | bytes 852000 | tf_op jit(solution)/shard_map/ppermute | solution.py:239
  97.1 0.0 copy-done.2
  97.1 17.9 %iterate2.1 = (f32[1664,128]{1,0:T(8,128)S(1)}, f32[1664,128]{1,0:T(8,128)S(1)}, f32[4096,128]{1,0:T(8,128)}, f32[8,128]{1,0:T(8,128)S(1)}) custom-call(s32[4096]{0:T(1024)S(1)} %reshape.76.refs_0_, s32[4096]{0:T(1024)S(1)} %reshape.77.refs_1_, s32[1]{0:T(128)} %bitcast.refs_2_, f32[1664,128]{1,0:T(8,128)S(1)} %bitcast.32, ...), custom_call_target="tpu_custom_call" | custom-call | tf_op jit(solution)/shard_map/iterate2/pallas_call | solution.py:284
  115.0 0.4 collective-permute-start.6
  115.4 2.0 %collective-permute-done.6 = f32[1664,128]{1,0:T(8,128)S(1)} collective-permute-done((f32[1664,128]{1,0:T(8,128)S(1)}, f32[1664,128]{1,0:T(8,128)S(1)}, u32[]{:S(2)}, u32[]{:S(2)}) %collective-permute-start.6) | collective-permute-done | bytes 852000 | tf_op jit(solution)/shard_map/ppermute | solution.py:239
  117.4 0.1 add.86
  117.5 0.0 copy-start.4
  117.5 17.0 %all_to_all.28 = f32[16,104,128]{2,1,0:T(8,128)S(1)} all-to-all(f32[16,104,128]{2,1,0:T(8,128)S(1)} %bitcast.36), channel_id=1, replica_groups={{0,2,4,6,8,10,12,14,16,18,20,22,24,26,28,30},{1,3,5,7,9,11,13,15,17,19,..., dimensions={0} | all-to-all | bytes 1703936 | tf_op jit(solution)/shard_map/all_to_all | solution.py:255
  134.6 2.5 %collective-permute-start.9 = (f32[104,128]{1,0:T(8,128)S(1)}, f32[104,128]{1,0:T(8,128)S(1)}, u32[]{:S(2)}, u32[]{:S(2)}) collective-permute-start(f32[104,128]{1,0:T(8,128)S(1)} %reduce_sum.47), channel_id=1, source_target_pairs={{0,96},{32,0},{64,32},{96,64},{1,97},{33,1},{65,33},{97,65},{2,98}... | collective-permute-start | bytes 159752 | tf_op jit(solution)/shard_map/ppermute | solution.py:259
  137.0 0.0 collective-permute-start.8
  137.0 1.3 collective-permute-start.7
  138.3 0.0 collective-permute-done.9
  138.3 3.5 %collective-permute-done.8 = f32[104,128]{1,0:T(8,128)S(1)} collective-permute-done((f32[104,128]{1,0:T(8,128)S(1)}, f32[104,128]{1,0:T(8,128)S(1)}, u32[]{:S(2)}, u32[]{:S(2)}) %collective-permute-start.8) | collective-permute-done | bytes 53280 | tf_op jit(solution)/shard_map/ppermute | solution.py:259
  141.8 0.0 collective-permute-done.7
  141.8 0.6 multiply_reduce_fusion
  142.4 1.2 broadcast_in_dim.18
  143.6 7.2 %all-to-all-start.4 = ((f32[32,1,1]{2,1,0:T(1,128)}), f32[32,1,1]{2,1,0:T(1,128)S(1)}, u32[]{:S(2)}, u32[]{:S(2)}) async-start(f32[32,1,1]{2,1,0:T(1,128)} %broadcast_in_dim.18), calls=%async_computation.4 | async-start | bytes 32768 | tf_op jit(solution)/shard_map/all_to_all | solution.py:291
  150.8 6.9 %all-to-all-done.4 = f32[32,1,1]{2,1,0:T(1,128)S(1)} async-done(((f32[32,1,1]{2,1,0:T(1,128)}), f32[32,1,1]{2,1,0:T(1,128)S(1)}, u32[]{:S(2)}, u32[]{:S(2)}) %all-to-all-start.4) | async-done | bytes 160 | tf_op jit(solution)/shard_map/all_to_all | solution.py:291
  157.7 0.6 reduce_sum.49
  159.0 0.0 copy-done.4
  159.0 0.6 fusion.3
  (6 shorter events, 0.1 us)
Async XLA Ops:
  0.6 26.6 %copy-start.5 = (s32[256,16]{0,1:T(8,128)S(1)}, s32[256,16]{0,1:T(8,128)}, u32[]{:S(2)}) copy-start(s32[256,16]{0,1:T(8,128)} %param.6) | copy-start | bytes 49156
  0.6 28.5 %copy-start.6 = (s32[256]{0:T(256)S(1)}, s32[256]{0:T(256)}, u32[]{:S(2)}) copy-start(s32[256]{0:T(256)} %param.9) | copy-start | bytes 3076
  0.6 28.8 %copy-start = (f32[256,2048]{1,0:T(8,128)S(1)}, f32[256,2048]{1,0:T(8,128)}, u32[]{:S(2)}) copy-start(f32[256,2048]{1,0:T(8,128)} %param.7) | copy-start | bytes 6291460
  2.6 21.9 %all-to-all-start = ((f32[16,104,128]{2,1,0:T(8,128)}), f32[16,104,128]{2,1,0:T(8,128)S(1)}, u32[]{:S(2)}, u32[]{:S(2)}) async-start(f32[16,104,128]{2,1,0:T(8,128)} %broadcast_in_dim.15), calls=%async_computation | async-start | bytes 1703936 | tf_op jit(solution)/shard_map/all_to_all | solution.py:248
  24.5 4.9 %collective-permute-start = (f32[1664,128]{1,0:T(8,128)S(1)}, f32[1664,128]{1,0:T(8,128)}, u32[]{:S(2)}, u32[]{:S(2)}) collective-permute-start(f32[1664,128]{1,0:T(8,128)S(1)} %bitcast.30), channel_id=1, source_target_pairs={{0,1},{1,0},{2,3},{3,2},{4,5},{5,4},{6,7},{7,6},{8,9},{9,8},{10,11... | collective-permute-start | bytes 2555912 | tf_op jit(solution)/shard_map/ppermute | solution.py:239
  29.5 1.6 copy-start.1
  46.9 2.5 %collective-permute-start.1 = (f32[1664,128]{1,0:T(8,128)S(1)}, f32[1664,128]{1,0:T(8,128)S(1)}, u32[]{:S(2)}, u32[]{:S(2)}) collective-permute-start(f32[1664,128]{1,0:T(8,128)S(1)} %get-tuple-element.9), channel_id=1, source_target_pairs={{0,1},{1,0},{2,3},{3,2},{4,5},{5,4},{6,7},{7,6},{8,9},{9,8},{10,11... | collective-permute-start | bytes 2555912 | tf_op jit(solution)/shard_map/ppermute | solution.py:239
  49.4 26.0 %copy-start.3 = (f32[12800]{0:T(1024)S(1)}, f32[12800]{0:T(1024)}, u32[]{:S(2)}) copy-start(f32[12800]{0:T(1024)} %param.10) | copy-start | bytes 153604
  67.8 29.3 %copy-start.2 = (f32[256,2048]{1,0:T(8,128)S(1)}, f32[256,2048]{1,0:T(8,128)}, u32[]{:S(2)}) copy-start(f32[256,2048]{1,0:T(8,128)} %param.8) | copy-start | bytes 6291460
  67.8 4.5 %collective-permute-start.4 = (f32[104,128]{1,0:T(8,128)S(1)}, f32[104,128]{1,0:T(8,128)S(1)}, u32[]{:S(2)}, u32[]{:S(2)}) collective-permute-start(f32[104,128]{1,0:T(8,128)S(1)} %reduce_sum.46), channel_id=1, source_target_pairs={{0,96},{32,0},{64,32},{96,64},{1,97},{33,1},{65,33},{97,65},{2,98}... | collective-permute-start | bytes 159752 | tf_op jit(solution)/shard_map/ppermute | solution.py:259
  70.6 4.8 %collective-permute-start.3 = (f32[104,128]{1,0:T(8,128)S(1)}, f32[104,128]{1,0:T(8,128)S(1)}, u32[]{:S(2)}, u32[]{:S(2)}) collective-permute-start(f32[104,128]{1,0:T(8,128)S(1)} %reduce_sum.46), channel_id=1, source_target_pairs={{0,32},{32,64},{64,96},{96,0},{1,33},{33,65},{65,97},{97,1},{2,34}... | collective-permute-start | bytes 159752 | tf_op jit(solution)/shard_map/ppermute | solution.py:259
  70.6 4.8 %collective-permute-start.2 = (f32[104,128]{1,0:T(8,128)S(1)}, f32[104,128]{1,0:T(8,128)S(1)}, u32[]{:S(2)}, u32[]{:S(2)}) collective-permute-start(f32[104,128]{1,0:T(8,128)S(1)} %reduce_sum.46), channel_id=1, source_target_pairs={{0,64},{32,96},{64,0},{96,32},{1,65},{33,97},{65,1},{97,33},{2,66}... | collective-permute-start | bytes 159752 | tf_op jit(solution)/shard_map/ppermute | solution.py:259
  90.6 6.4 %collective-permute-start.5 = (f32[1664,128]{1,0:T(8,128)S(1)}, f32[1664,128]{1,0:T(8,128)S(1)}, u32[]{:S(2)}, u32[]{:S(2)}) collective-permute-start(f32[1664,128]{1,0:T(8,128)S(1)} %bitcast.33), channel_id=1, source_target_pairs={{0,1},{1,0},{2,3},{3,2},{4,5},{5,4},{6,7},{7,6},{8,9},{9,8},{10,11... | collective-permute-start | bytes 2555912 | tf_op jit(solution)/shard_map/ppermute | solution.py:239
  115.0 2.4 %collective-permute-start.6 = (f32[1664,128]{1,0:T(8,128)S(1)}, f32[1664,128]{1,0:T(8,128)S(1)}, u32[]{:S(2)}, u32[]{:S(2)}) collective-permute-start(f32[1664,128]{1,0:T(8,128)S(1)} %get-tuple-element.13), channel_id=1, source_target_pairs={{0,1},{1,0},{2,3},{3,2},{4,5},{5,4},{6,7},{7,6},{8,9},{9,8},{10,11... | collective-permute-start | bytes 2555912 | tf_op jit(solution)/shard_map/ppermute | solution.py:239
  117.5 41.5 %copy-start.4 = (f32[12800]{0:T(1024)S(1)}, f32[12800]{0:T(1024)}, u32[]{:S(2)}) copy-start(f32[12800]{0:T(1024)} %param.11) | copy-start | bytes 153604
  134.6 3.7 %collective-permute-start.9 = (f32[104,128]{1,0:T(8,128)S(1)}, f32[104,128]{1,0:T(8,128)S(1)}, u32[]{:S(2)}, u32[]{:S(2)}) collective-permute-start(f32[104,128]{1,0:T(8,128)S(1)} %reduce_sum.47), channel_id=1, source_target_pairs={{0,96},{32,0},{64,32},{96,64},{1,97},{33,1},{65,33},{97,65},{2,98}... | collective-permute-start | bytes 159752 | tf_op jit(solution)/shard_map/ppermute | solution.py:259
  137.0 4.8 %collective-permute-start.8 = (f32[104,128]{1,0:T(8,128)S(1)}, f32[104,128]{1,0:T(8,128)S(1)}, u32[]{:S(2)}, u32[]{:S(2)}) collective-permute-start(f32[104,128]{1,0:T(8,128)S(1)} %reduce_sum.47), channel_id=1, source_target_pairs={{0,32},{32,64},{64,96},{96,0},{1,33},{33,65},{65,97},{97,1},{2,34}... | collective-permute-start | bytes 159752 | tf_op jit(solution)/shard_map/ppermute | solution.py:259
  137.0 4.8 %collective-permute-start.7 = (f32[104,128]{1,0:T(8,128)S(1)}, f32[104,128]{1,0:T(8,128)S(1)}, u32[]{:S(2)}, u32[]{:S(2)}) collective-permute-start(f32[104,128]{1,0:T(8,128)S(1)} %reduce_sum.47), channel_id=1, source_target_pairs={{0,64},{32,96},{64,0},{96,32},{1,65},{33,97},{65,1},{97,33},{2,66}... | collective-permute-start | bytes 159752 | tf_op jit(solution)/shard_map/ppermute | solution.py:259
  143.6 14.1 %all-to-all-start.4 = ((f32[32,1,1]{2,1,0:T(1,128)}), f32[32,1,1]{2,1,0:T(1,128)S(1)}, u32[]{:S(2)}, u32[]{:S(2)}) async-start(f32[32,1,1]{2,1,0:T(1,128)} %broadcast_in_dim.18), calls=%async_computation.4 | async-start | bytes 32768 | tf_op jit(solution)/shard_map/all_to_all | solution.py:291

commit v3 on v2

v3 whole, which is shorter than its diff:
```python
import jax
import jax.numpy as jnp
from jax import lax
from jax.experimental import pallas as pl
from jax.experimental.pallas import tpu as pltpu
from jax.sharding import PartitionSpec as P

BLOCK = 128
BISECT = 16
SUB = 8
DEAD = -1e30

AXES = ("grp", "shard")


def pad8(n):
    return -(-n // SUB) * SUB


def iteration_kernel(second, groups, blocks, half, item_count):
    full = 2 * half
    members = groups * SUB
    group_rows = SUB * blocks
    rows_all = groups * group_rows
    part = groups // 2
    quarter = part // 2
    part_rows = part * group_rows
    assert quarter * 4 == groups and part == BISECT and blocks % 2 == 0
    pieces = 4
    f32 = jnp.float32

    def body(*refs):
        if second:
            (gidx_in, sidx_in, ncopy, own_d, other_d, own_g, other_g, aff_in, exp_in, nlive,
             keep, send, primal_out, sumsq,
             table, work_a, work_b, acc, lo, up, peaks, sums, aff, exp, gidx, sidx, sem_in, sem_id,
             primal, sem_out) = refs
        else:
            (gidx_in, sidx_in, ncopy, own_d, other_d, aff_in, exp_in, nlive,
             keep, send,
             table, work_a, work_b, acc, lo, up, peaks, sums, aff, exp, gidx, sidx, sem_in, sem_id) = refs
        works = (work_a, work_b)

        ids_in = [pltpu.make_async_copy(src, dst, sem_id.at[k])
                  for k, (src, dst) in enumerate(((gidx_in, gidx), (sidx_in, sidx)))]
        size = part_rows // pieces
        spans = [(k * size, size) for k in range(pieces)] + [(part_rows, part_rows)]
        loads = [[pltpu.make_async_copy(src.at[pl.ds(r, n), :], dst.at[pl.ds(r, n), :], sem_in.at[k, j])
                  for j, (src, dst) in enumerate(((aff_in, aff), (exp_in, exp)))]
                 for k, (r, n) in enumerate(spans)]
        ids_in[0].start()
        for pair in loads:
            for load in pair:
                load.start()
        ids_in[1].start()

        if second:
            def square(i, s):
                r = pl.multiple_of(i * SUB, SUB)
                a = own_g[pl.ds(r, SUB), :]
                b = other_g[pl.ds(r, SUB), :]
                return s + (a * a + b * b)

            s = lax.fori_loop(0, half // SUB, square, jnp.zeros((SUB, BLOCK), f32), unroll=8)
            total = jnp.sum(jnp.sum(s, axis=1, keepdims=True), axis=0, keepdims=True)
            total = jnp.broadcast_to(total, (SUB, BLOCK))
            sumsq[...] = total
            scale = jnp.sqrt(total / item_count + 1e-6)

            def fill_table(i, c):
                r = pl.multiple_of(i * SUB, SUB)
                for d, g, off in ((own_d, own_g, 0), (other_d, other_g, half)):
                    table[pl.ds(r + off, SUB), :] = jnp.maximum(
                        d[pl.ds(r, SUB), :] + 0.5 * g[pl.ds(r, SUB), :] / scale, 0.0)
                return c
        else:
            def fill_table(i, c):
                r = pl.multiple_of(i * SUB, SUB)
                table[pl.ds(r, SUB), :] = own_d[pl.ds(r, SUB), :]
                table[pl.ds(r + half, SUB), :] = other_d[pl.ds(r, SUB), :]
                return c

        lax.fori_loop(0, half // SUB, fill_table, 0, unroll=8)

        n = ncopy[0]
        zero = jnp.zeros((SUB, BLOCK), f32)
        dead = jnp.full((SUB, BLOCK), DEAD, f32)
        vregs = full // SUB
        per_step = 2 * vregs // (2 * BISECT)
        assert per_step * BISECT == vregs

        def clear(i, c):
            acc[pl.ds(pl.multiple_of(i * SUB, SUB), SUB), :] = zero
            return c

        lax.fori_loop(2 * vregs // 16, n * vregs // 16, lambda i, c: [clear(16 * i + j, c) for j in range(16)][-1], 0)

        def clear_some(k):
            some = acc.at[pl.ds(pl.multiple_of(k * (per_step * SUB), SUB), per_step * SUB), :]
            for i in range(per_step):
                some[pl.ds(i * SUB, SUB), :] = zero

        def loop(first, last, f):
            def trip(i, c):
                f(i)
                return c

            lax.fori_loop(first, last, trip, 0)

        def picked(ids, j, g):
            return ids.at[pl.ds(j * groups, rows_all - j * groups)][g]

        def gather(h, g, first, count):
            rows = (h * part + g) * group_rows
            where = pl.multiple_of(rows + first * SUB, SUB)
            here = pl.multiple_of(g * group_rows + first * SUB, SUB)
            work = works[h].at[pl.ds(here, count * SUB), :]
            a_rows = aff.at[pl.ds(where, count * SUB), :]
            e_rows = exp.at[pl.ds(where, count * SUB), :]
            mrows = pl.ds(pl.multiple_of((h * part + g) * SUB, SUB), SUB)
            live = nlive[mrows, :] - first
            peak = peaks[mrows, :]
            for b in range(count):
                for s in range(SUB):
                    work[pl.ds(b * SUB + s, 1), :] = table[pl.ds(picked(gidx, s * blocks + b, h * part + g + first * groups), 1), :]
                now = pl.ds(b * SUB, SUB)
                v = (a_rows[now, :] - e_rows[now, :] * work[now, :]) * 2.0
                v = jnp.where(live > b, v, DEAD)
                work[now, :] = v
                peak = jnp.maximum(peak, v)
            peaks[mrows, :] = peak

        def start_bisection(h):
            for g in range(part):
                rows = pl.ds((h * part + g) * SUB, SUB)
                up[rows, :] = jnp.broadcast_to(jnp.max(peaks[rows, :], axis=1, keepdims=True), (SUB, BLOCK))
                lo[rows, :] = zero

        def fill_sums(h, q, *only):
            work = works[h].at[pl.ds(pl.multiple_of(q * (quarter * group_rows), SUB), quarter * group_rows), :]
            m0 = pl.multiple_of((h * part + q * quarter) * SUB, SUB)
            s0 = pl.multiple_of(q * (quarter * SUB), SUB)
            for g in only or range(quarter):
                rows = pl.ds(m0 + g * SUB, SUB)
                mid = (lo[rows, :] + up[rows, :]) * 0.5
                a = [None, None]
                for b in range(blocks):
                    v = jnp.clip(work[pl.ds(g * group_rows + b * SUB, SUB), :] - mid, 0.0, 1.0)
                    a[b % 2] = v if a[b % 2] is None else a[b % 2] + v
                sums[pl.ds(s0 + g * SUB, SUB), :] = a[0] + a[1]

        def lane_sums(q):
            s0 = pl.multiple_of(q * (quarter * SUB), SUB)
            return [jnp.sum(sums[pl.ds(s0 + g * SUB, SUB), :], axis=1, keepdims=True) for g in range(quarter)]

        def decide(h, q, fills):
            m0 = pl.multiple_of((h * part + q * quarter) * SUB, SUB)
            for g in range(quarter):
                rows = pl.ds(m0 + g * SUB, SUB)
                bigger = jnp.broadcast_to(fills[g], (SUB, BLOCK)) > 1.0
                low = lo[rows, :]
                high = up[rows, :]
                mid = (low + high) * 0.5
                lo[rows, :] = jnp.where(bigger, mid, low)
                up[rows, :] = jnp.where(bigger, high, mid)

        def bisect(h, beside):
            fill_sums(h, 0)

            def half_step(k):
                q = k % 2
                fills = lane_sums(q)
                steps = beside(k // 2, q)
                for g in range(quarter):
                    fill_sums(h, 1 - q, g)
                    for at, step in steps:
                        if at == g:
                            step()
                decide(h, q, fills)

            loop(0, 2 * BISECT, half_step)

        def allocate(h, g):
            rows = pl.multiple_of((h * part + g) * group_rows, SUB)
            here = pl.multiple_of(g * group_rows, SUB)
            mrows = pl.ds(pl.multiple_of((h * part + g) * SUB, SUB), SUB)
            th = up[mrows, :]
            live = nlive[mrows, :]
            for b in range(blocks):
                now = pl.ds(here + b * SUB, SUB)
                x = jnp.where(live > b, jnp.clip(works[h][now, :] - th, 0.0, 1.0), 0.0)
                if second:
                    primal[pl.ds(rows + b * SUB, SUB), :] = x
                works[h][now, :] = exp[pl.ds(rows + b * SUB, SUB), :] * x

        def scatter(h, g, first, count):
            here = g * group_rows + first
            work = works[h]
            for s in range(count):
                where = [picked(sidx, s * blocks + b, h * part + g + first * blocks * groups) for b in range(blocks)]
                added = [acc[pl.ds(i, 1), :] + work[pl.ds(here + b * SUB + s, 1), :] for b, i in enumerate(where)]
                for i, v in zip(where, added):
                    acc[pl.ds(i, 1), :] = v

        for g in range(groups):
            peaks[pl.ds(g * SUB, SUB), :] = dead
        ids_in[0].wait()
        for k in range(pieces):
            for load in loads[k]:
                load.wait()
            loop(k * (part // pieces), (k + 1) * (part // pieces), lambda g: gather(0, g, 0, blocks))
        start_bisection(0)
        for load in loads[pieces]:
            load.wait()
        bisect(0, lambda g, q: [(quarter - 1, lambda: gather(1, g, q * (blocks // 2), blocks // 2)),
                                (quarter - 1, lambda: clear_some(2 * g + q))])

        start_bisection(1)
        loop(0, part, lambda g: allocate(0, g))
        if second:
            stores = [pltpu.make_async_copy(
                primal.at[pl.ds(h * part_rows, part_rows), :],
                primal_out.at[pl.ds(h * part_rows, part_rows), :], sem_out.at[h]) for h in range(2)]
            stores[0].start()
        ids_in[1].wait()
        bisect(1, lambda g, q: [(2 * m, lambda m=m: scatter(0, g, q * (SUB // 2) + m, 1)) for m in range(SUB // 2)])
        loop(0, part, lambda g: allocate(1, g))
        if second:
            stores[1].start()
        loop(0, part, lambda g: scatter(1, g, 0, SUB))

        def finish(i, c):
            r = pl.multiple_of(i * SUB, SUB)
            for out, o in ((keep, 0), (send, half)):
                out[pl.ds(r, SUB), :] = acc[pl.ds(r + o, SUB), :] + acc[pl.ds(r + (full + o), SUB), :]
            return c

        lax.fori_loop(0, half // SUB, finish, 0, unroll=8)

        def finish_copy(t, c):
            def more(i, c):
                r = pl.multiple_of(i * SUB, SUB)
                a = pl.multiple_of(t * full + r, SUB)
                for out, o in ((keep, 0), (send, half)):
                    out[pl.ds(r, SUB), :] += acc[pl.ds(a + o, SUB), :]
                return c

            return lax.fori_loop(0, half // SUB, more, c, unroll=8)

        lax.fori_loop(2, n, finish_copy, 0)
        if second:
            for store in stores:
                store.wait()

    smem = pl.BlockSpec(memory_space=pltpu.SMEM)
    vmem = pl.BlockSpec(memory_space=pltpu.VMEM)
    left = pl.BlockSpec(memory_space=pltpu.HBM)
    outs = [jax.ShapeDtypeStruct((half, BLOCK), f32)] * 2
    out_specs = [vmem] * 2
    scratch = [
        pltpu.VMEM((full, BLOCK), f32),
        pltpu.VMEM((part_rows, BLOCK), f32),
        pltpu.VMEM((part_rows, BLOCK), f32),
        pltpu.VMEM((blocks * full, BLOCK), f32),
        pltpu.VMEM((members, BLOCK), f32),
        pltpu.VMEM((members, BLOCK), f32),
        pltpu.VMEM((members, BLOCK), f32),
        pltpu.VMEM((part * SUB, BLOCK), f32),
        pltpu.VMEM((rows_all, BLOCK), f32),
        pltpu.VMEM((rows_all, BLOCK), f32),
        pltpu.SMEM((rows_all,), jnp.int32),
        pltpu.SMEM((rows_all,), jnp.int32),
        pltpu.SemaphoreType.DMA((pieces + 1, 2)),
        pltpu.SemaphoreType.DMA((2,)),
    ]
    if second:
        outs += [jax.ShapeDtypeStruct((rows_all, BLOCK), f32), jax.ShapeDtypeStruct((SUB, BLOCK), f32)]
        out_specs += [left, vmem]
        scratch += [pltpu.VMEM((rows_all, BLOCK), f32), pltpu.SemaphoreType.DMA((2,))]
    tables = [vmem] * (4 if second else 2)
    call = pl.pallas_call(
        body,
        out_shape=outs,
        in_specs=[left, left, smem] + tables + [left, left, vmem],
        out_specs=out_specs,
        scratch_shapes=scratch,
        compiler_params=pltpu.CompilerParams(vmem_limit_bytes=48 << 20),
        name="iterate2" if second else "iterate1",
    )

    def run(gidx, sidx, ncopy, *rest):
        *tables, aff, exp, nlive = rest
        aff, exp = (pltpu.with_memory_space_constraint(x, pltpu.HBM) for x in (aff, exp))
        return call(gidx, sidx, ncopy, *tables, aff, exp, nlive)

    return run


def vmem_call(body, name, *outs):
    spec = pl.BlockSpec(memory_space=pltpu.VMEM)
    return pl.pallas_call(
        body,
        out_shape=[jax.ShapeDtypeStruct(shape, jnp.float32) for shape in outs],
        out_specs=[spec] * len(outs),
        compiler_params=pltpu.CompilerParams(vmem_limit_bytes=4 << 20),
        name=name,
    )


def spread_duals(x, chips, padded, core):
    own_rows = x.shape[0]

    def body(x, core, every):
        for p in range(chips):
            every[p, pl.ds(0, own_rows), :] = x[...]
            every[p, pl.ds(own_rows, padded - own_rows), :] = jnp.zeros((padded - own_rows, BLOCK), jnp.float32)

    return vmem_call(body, "spread_duals", (chips, padded, BLOCK))(
        x, jnp.full((SUB, BLOCK), core, jnp.int32))[0]


def sum_chips(x):
    def body(x, out):
        out[...] = jnp.sum(x[...], axis=0)

    return vmem_call(body, "sum_chips", x.shape[1:])(x)[0]


def gradient_of(plane, shifted, limit, gradient):
    own_rows = limit.shape[0]
    one, two, three = shifted
    gradient[...] = (plane[...] + two[...]) + (one[...] + three[...])
    gradient[pl.ds(0, own_rows), :] = gradient[pl.ds(0, own_rows), :] - limit[...]


def spread_gradient(plane, shifted, limit, chips):
    def body(plane, one, two, three, limit, gradient, every):
        gradient_of(plane, (one, two, three), limit, gradient)
        for p in range(chips):
            every[p] = gradient[...]

    return vmem_call(body, "spread_gradient", plane.shape, (chips, *plane.shape))(plane, *shifted, limit)


def last_gradient(plane, shifted, limit, shards):
    def body(plane, one, two, three, limit, gradient, parts):
        gradient_of(plane, (one, two, three), limit, gradient)
        g = gradient[...]
        part = jnp.sum(jnp.sum(g * g, axis=0, keepdims=True), axis=1, keepdims=True)
        parts[...] = jnp.broadcast_to(part[None], parts.shape)

    return vmem_call(body, "last_gradient", plane.shape, (shards, 1, BLOCK))(plane, *shifted, limit)


def last_duals(duals, first, sumsq, second, parts, item_count):
    own_rows = duals.shape[0]

    def body(duals, first, sumsq, second, parts, out):
        own = pl.ds(0, own_rows)
        scale = jnp.sqrt(sumsq[0:1, :] / item_count + 1e-6)
        lam = jnp.maximum(duals[...] + 0.5 * first[own, :] / scale, 0.0)
        scale = jnp.sqrt(jnp.sum(parts[...], axis=0) / item_count + 1e-6)
        out[...] = jnp.maximum(lam + 0.5 * second[own, :] / scale, 0.0)

    return vmem_call(body, "last_duals", duals.shape)(duals, first, sumsq, second, parts)[0]


def local(candidates, affinity, exposure, lengths, item_limit, item_duals, *, grp_size, shard_size):
    chips = shard_size // 2
    same_core = [[2 * p + c for p in range(chips)] for c in range(2)]
    swap = [(g * shard_size + s, g * shard_size + (s ^ 1)) for g in range(grp_size) for s in range(shard_size)]
    members, slots = affinity.shape
    blocks = slots // BLOCK
    groups = members // SUB
    own_items = item_limit.shape[0]
    item_count = own_items * shard_size
    own_rows = own_items // BLOCK
    padded = pad8(own_rows)
    half = chips * padded
    full = 2 * half
    core = lax.axis_index("shard") % 2

    def swap_cores(x):
        return lax.ppermute(x, AXES, swap)

    def as_rows(x):
        return x.reshape(groups, SUB, blocks, BLOCK).transpose(0, 2, 1, 3).reshape(-1, BLOCK)

    def gather_halves(every):
        every = lax.all_to_all(
            every, "shard", 0, 0, axis_index_groups=same_core, tiled=True).reshape(half, BLOCK)
        return every, swap_cores(every)

    def reduce_loads(keep, send):
        chip = keep + swap_cores(send)
        plane = sum_chips(lax.all_to_all(
            chip.reshape(chips, padded, BLOCK), "shard", 0, 0,
            axis_index_groups=same_core, tiled=True))
        return plane, [
            lax.ppermute(plane, "grp", [(g, (g + d) % grp_size) for g in range(grp_size)])
            for d in range(1, grp_size)
        ]

    shard_of = candidates // own_rows
    gidx = (jnp.where(shard_of % 2 == core, 0, half) + (shard_of // 2) * padded + candidates % own_rows).reshape(-1)
    batch = gidx.reshape(-1, blocks)
    earlier = jnp.arange(blocks)[:, None] > jnp.arange(blocks)[None, :]
    copy = jnp.sum((batch[:, :, None] == batch[:, None, :]) & earlier, axis=2, dtype=jnp.int32)
    sidx = (batch + full * copy).reshape(groups, -1).T.reshape(-1)
    gidx = gidx.reshape(groups, -1).T.reshape(-1)
    ncopy = (jnp.max(copy) + 1).reshape(1)

    aff = as_rows(affinity)
    exp = as_rows(exposure)
    nlive = jnp.broadcast_to((lengths // BLOCK)[:, None], (members, BLOCK))
    limit = item_limit.reshape(own_rows, BLOCK)
    duals = item_duals.reshape(own_rows, BLOCK)

    own_d, other_d = gather_halves(spread_duals(duals, chips, padded, core))
    keep, send = iteration_kernel(False, groups, blocks, half, item_count)(
        gidx, sidx, ncopy, own_d, other_d, aff, exp, nlive)
    first, every = spread_gradient(*reduce_loads(keep, send), limit, chips)

    own_g, other_g = gather_halves(every)
    keep, send, primal, sumsq = iteration_kernel(True, groups, blocks, half, item_count)(
        gidx, sidx, ncopy, own_d, other_d, own_g, other_g, aff, exp, nlive)
    second, parts = last_gradient(*reduce_loads(keep, send), limit, shard_size)
    parts = lax.all_to_all(parts, "shard", 0, 0, tiled=True)
    duals = last_duals(duals, first, sumsq, second, parts, item_count)

    primal = primal.reshape(groups, blocks, SUB, BLOCK).transpose(0, 2, 1, 3).reshape(members, slots)
    return primal, duals.reshape(-1)


def solution(mesh):
    placed = (
        P(("grp", "shard"), None),
        P(("grp", "shard"), None),
        P(("grp", "shard"), None),
        P(("grp", "shard")),
        P("shard"),
        P("shard"),
    )

    def run(*args):
        return local(*args, grp_size=mesh.shape["grp"], shard_size=mesh.shape["shard"])

    return jax.shard_map(
        run,
        mesh=mesh,
        in_specs=placed,
        out_specs=(P(("grp", "shard"), None), P("shard")),
        check_vma=False,
    )
```

time: 160 us -> 143 us (0.89)
  blocking collectives: 49.3 us -> 85.2 us
  starting transfers between devices: 31.8 us -> 12.6 us
  waiting for transfers between devices: 33.2 us -> 14.2 us
  Pallas kernels: 33.7 us -> 26.9 us
  local copies, waits for them, and re-layouts: 5.25 us -> 1.67 us
  other arithmetic: 4.18 us -> 1.02 us
    all_to_all x1 -> x3, blocking collectives: 15.2 us -> 51.2 us  [the longest x2 37.2 us: gather_halves(): lax.all_to_all(every, 'shard', 0, 0, axis_index_groups=same_core, tiled=T...]
    all_to_all x2 -> x0, waiting for transfers between devices: 20.3 us -> none  [the longest x1 13.4 us: gather_halves(): lax.all_to_all(jnp.broadcast_to(x[None], (chips, padded, BLOCK)), 'shard'...]
    all_to_all x2 -> x0, starting transfers between devices: 15.6 us -> none  [the longest x1 8.42 us: gather_halves(): lax.all_to_all(jnp.broadcast_to(x[None], (chips, padded, BLOCK)), 'shard'...]
    pallas_call x2 -> x8, Pallas kernels: 33.7 us -> 26.9 us  [the longest x2 25.8 us: run(): return call(gidx, sidx, ncopy, *tables, aff, exp, nlive)]
    ppermute x6, starting transfers between devices: 8.18 us -> 5.65 us  [reduce_loads(): lax.ppermute(plane, 'grp', [(g, (g + d) % grp_size) for g in range(grp_si...]
    reduce_sum x4 -> x0, other arithmetic: 2.51 us -> none  [the longest x2 1.26 us: reduce_loads(): plane = lax.all_to_all(chip.reshape(chips, padded, BLOCK), 'shard', 0, 0,...]
    broadcast_in_dim x3 -> x1, local copies, waits for them, and re-layouts: 2.18 us -> 0.01 us  [spread_duals(): jnp.full((SUB, BLOCK), core, jnp.int32)]
  transfers between devices with their start and end apart: 12 -> 10, of which waited for: 8 -> 9; matrix products, arithmetic and copies ran while one was open for 1% -> 1% of each run, Pallas kernels for 0% -> 0%
where the time goes in v3:
time: 143 us
  blocking collectives  85.2 us (60%)
  Pallas kernels  26.9 us (19%)
  waiting for transfers between devices  14.2 us (10%)
  starting transfers between devices  12.6 us (9%)
  local copies, waits for them, and re-layouts  1.67 us (1%)
  between operations  1.44 us (1%)
    all_to_all x2, blocking collectives, gather_halves(): lax.all_to_all(every, 'shard', 0, 0, axis_index_groups=same_core, tiled=T...  37.2 us
    all_to_all x2, blocking collectives, reduce_loads(): lax.all_to_all(chip.reshape(chips, padded, BLOCK), 'shard', 0, 0, axis_in...  34.1 us
    pallas_call x2, Pallas kernels, run(): return call(gidx, sidx, ncopy, *tables, aff, exp, nlive)  25.8 us
    all_to_all x1, blocking collectives, local(): parts = lax.all_to_all(parts, 'shard', 0, 0, tiled=True)  13.9 us
    ppermute x6, waiting for transfers between devices, reduce_loads(): lax.ppermute(plane, 'grp', [(g, (g + d) % grp_size) for g in range(grp_si...  7.93 us
    ppermute x4, starting transfers between devices, swap_cores(): return lax.ppermute(x, AXES, swap)  6.95 us
    ppermute x4, waiting for transfers between devices, swap_cores(): return lax.ppermute(x, AXES, swap)  6.31 us
    ppermute x6, starting transfers between devices, reduce_loads(): lax.ppermute(plane, 'grp', [(g, (g + d) % grp_size) for g in range(grp_si...  5.65 us
  transfers between devices with their start and end apart: 10, of which 9 were waited for; matrix products, arithmetic and copies ran while one was open for 1% of the time, Pallas kernels for 0%

profile of v3, /device:TPU:1, one launch (start us, length us, event | category | flops | bytes accessed | tf_op | source)
XLA Modules:
  0.0 143.1 jit_solution(13048946796479014423)
XLA Ops:
  0.6 0.0 copy-start.3
  0.6 0.0 copy-start.4
  0.7 0.0 copy-start
  0.7 0.8 copy-done
  1.5 0.1 spread_duals.1
  1.5 22.1 %all_to_all.25 = f32[16,104,128]{2,1,0:T(8,128)S(1)} all-to-all(f32[16,104,128]{2,1,0:T(8,128)S(1)} %spread_duals.1), channel_id=1, replica_groups={{0,2,4,6,8,10,12,14,16,18,20,22,24,26,28,30},{1,3,5,7,9,11,13,15,17,19,..., dimensions={0} | all-to-all | bytes 1703936 | tf_op jit(solution)/shard_map/all_to_all | solution.py:390
  23.7 1.8 %collective-permute-start = (f32[1664,128]{1,0:T(8,128)S(1)}, f32[1664,128]{1,0:T(8,128)S(1)}, u32[]{:S(2)}, u32[]{:S(2)}) collective-permute-start(f32[1664,128]{1,0:T(8,128)S(1)} %bitcast.25), channel_id=1, source_target_pairs={{0,1},{1,0},{2,3},{3,2},{4,5},{5,4},{6,7},{7,6},{8,9},{9,8},{10,11... | collective-permute-start | bytes 2555912 | tf_op jit(solution)/shard_map/ppermute | solution.py:384
  25.5 0.0 copy-done.3
  25.5 0.1 copy.16
  25.7 0.1 convert_reduce_fusion
  25.8 0.6 fusion.7
  27.1 0.1 copy.18
  27.2 0.1 reshape.71
  27.3 0.1 copy.19
  27.4 0.1 reshape.72.refs_1_
  27.5 0.1 reshape_reshape.3
  27.6 0.1 copy.17
  27.7 0.1 reshape.70.refs_0_
  27.8 0.0 copy-done.4
  27.8 0.0 collective-permute-done.refs_4_
  27.8 0.1 broadcast_in_dim.20.refs_7_.refs_9_
  27.9 12.9 %iterate1.1 = (f32[1664,128]{1,0:T(8,128)S(1)}, f32[1664,128]{1,0:T(8,128)S(1)}) custom-call(s32[4096]{0:T(1024)S(1)} %reshape.70.refs_0_, s32[4096]{0:T(1024)S(1)} %reshape.72.refs_1_, s32[1]{0:T(128)} %bitcast.2.refs_2_, f32[1664,128]{1,0:T(8,128)S(1)} %bitcast.26, f32[1664,128]{1,0:T(8,128)S(1)} %collective-permute-done.refs_4_, f32[4096,128]{1,0:T(8,128)} %bitcast.34, ...), custom_call_target="tpu_custom_call" | custom-call | tf_op jit(solution)/shard_map/iterate1/pallas_call | solution.py:294
  40.8 0.2 collective-permute-start.1
  40.9 2.3 %collective-permute-done.1 = f32[1664,128]{1,0:T(8,128)S(1)} collective-permute-done((f32[1664,128]{1,0:T(8,128)S(1)}, f32[1664,128]{1,0:T(8,128)S(1)}, u32[]{:S(2)}, u32[]{:S(2)}) %collective-permute-start.1) | collective-permute-done | bytes 852000 | tf_op jit(solution)/shard_map/ppermute | solution.py:384
  43.2 0.0 copy-start.2
  43.2 0.1 add.42
  43.3 17.1 %all_to_all.26.x = f32[16,104,128]{2,1,0:T(8,128)S(1)} all-to-all(f32[16,104,128]{2,1,0:T(8,128)S(1)} %bitcast.38), channel_id=1, replica_groups={{0,2,4,6,8,10,12,14,16,18,20,22,24,26,28,30},{1,3,5,7,9,11,13,15,17,19,..., dimensions={0} | all-to-all | bytes 1703936 | tf_op jit(solution)/shard_map/all_to_all | solution.py:396
  60.4 2.8 %collective-permute-start.4 = (f32[104,128]{1,0:T(8,128)S(1)}, f32[104,128]{1,0:T(8,128)S(1)}, u32[]{:S(2)}, u32[]{:S(2)}) collective-permute-start(f32[104,128]{1,0:T(8,128)S(1)} %sum_chips.2.plane), channel_id=1, source_target_pairs={{0,96},{32,0},{64,32},{96,64},{1,97},{33,1},{65,33},{97,65},{2,98}... | collective-permute-start | bytes 159752 | tf_op jit(solution)/shard_map/ppermute | solution.py:400
  63.2 0.3 collective-permute-start.3
  63.6 0.7 collective-permute-start.2
  64.3 0.2 collective-permute-done.4.three
  64.5 3.3 %collective-permute-done.3.two = f32[104,128]{1,0:T(8,128)S(1)} collective-permute-done((f32[104,128]{1,0:T(8,128)S(1)}, f32[104,128]{1,0:T(8,128)S(1)}, u32[]{:S(2)}, u32[]{:S(2)}) %collective-permute-start.3) | collective-permute-done | bytes 53280 | tf_op jit(solution)/shard_map/ppermute | solution.py:400
  67.8 0.5 collective-permute-done.2.one
  68.3 0.0 copy-done.2
  68.3 0.1 spread_gradient.1
  68.4 15.1 %all_to_all.27 = f32[16,104,128]{2,1,0:T(8,128)S(1)} all-to-all(f32[16,104,128]{2,1,0:T(8,128)S(1)} %get-tuple-element.14), channel_id=1, replica_groups={{0,2,4,6,8,10,12,14,16,18,20,22,24,26,28,30},{1,3,5,7,9,11,13,15,17,19,..., dimensions={0} | all-to-all | bytes 1703936 | tf_op jit(solution)/shard_map/all_to_all | solution.py:390
  83.5 4.5 %collective-permute-start.5 = (f32[1664,128]{1,0:T(8,128)S(1)}, f32[1664,128]{1,0:T(8,128)S(1)}, u32[]{:S(2)}, u32[]{:S(2)}) collective-permute-start(f32[1664,128]{1,0:T(8,128)S(1)} %bitcast.28), channel_id=1, source_target_pairs={{0,1},{1,0},{2,3},{3,2},{4,5},{5,4},{6,7},{7,6},{8,9},{9,8},{10,11... | collective-permute-start | bytes 2555912 | tf_op jit(solution)/shard_map/ppermute | solution.py:384
  88.0 2.0 %collective-permute-done.5.refs_6_ = f32[1664,128]{1,0:T(8,128)S(1)} collective-permute-done((f32[1664,128]{1,0:T(8,128)S(1)}, f32[1664,128]{1,0:T(8,128)S(1)}, u32[]{:S(2)}, u32[]{:S(2)}) %collective-permute-start.5) | collective-permute-done | bytes 852000 | tf_op jit(solution)/shard_map/ppermute | solution.py:384
  90.0 13.0 %iterate2.1 = (f32[1664,128]{1,0:T(8,128)S(1)}, f32[1664,128]{1,0:T(8,128)S(1)}, f32[4096,128]{1,0:T(8,128)}, f32[8,128]{1,0:T(8,128)S(1)}) custom-call(s32[4096]{0:T(1024)S(1)} %reshape.70.refs_0_, s32[4096]{0:T(1024)S(1)} %reshape.72.refs_1_, s32[1]{0:T(128)} %bitcast.2.refs_2_, f32[1664,128]{1,0:T(8,128)S(1)} %bitcast.27, ...), custom_call_target="tpu_custom_call" | custom-call | tf_op jit(solution)/shard_map/iterate2/pallas_call | solution.py:294
  102.9 0.5 collective-permute-start.6
  103.4 2.0 %collective-permute-done.6 = f32[1664,128]{1,0:T(8,128)S(1)} collective-permute-done((f32[1664,128]{1,0:T(8,128)S(1)}, f32[1664,128]{1,0:T(8,128)S(1)}, u32[]{:S(2)}, u32[]{:S(2)}) %collective-permute-start.6) | collective-permute-done | bytes 852000 | tf_op jit(solution)/shard_map/ppermute | solution.py:384
  105.4 0.1 add.43
  105.5 0.0 copy-start.1
  105.5 17.0 %all_to_all.28.x = f32[16,104,128]{2,1,0:T(8,128)S(1)} all-to-all(f32[16,104,128]{2,1,0:T(8,128)S(1)} %bitcast.39), channel_id=1, replica_groups={{0,2,4,6,8,10,12,14,16,18,20,22,24,26,28,30},{1,3,5,7,9,11,13,15,17,19,..., dimensions={0} | all-to-all | bytes 1703936 | tf_op jit(solution)/shard_map/all_to_all | solution.py:396
  122.6 0.7 collective-permute-start.9
  123.2 0.4 collective-permute-start.8
  123.6 0.8 collective-permute-start.7
  124.4 1.2 collective-permute-done.9.three
  125.6 2.1 %collective-permute-done.8.two = f32[104,128]{1,0:T(8,128)S(1)} collective-permute-done((f32[104,128]{1,0:T(8,128)S(1)}, f32[104,128]{1,0:T(8,128)S(1)}, u32[]{:S(2)}, u32[]{:S(2)}) %collective-permute-start.8) | collective-permute-done | bytes 53280 | tf_op jit(solution)/shard_map/ppermute | solution.py:400
  127.8 0.5 collective-permute-done.7.one
  128.3 0.1 last_gradient.1
  128.4 13.9 %all_to_all.29.parts = f32[32,1,128]{2,1,0:T(1,128)S(1)} all-to-all(f32[32,1,128]{2,1,0:T(1,128)S(1)} %get-tuple-element.21), channel_id=1, replica_groups=mesh['grp'=4,'shard'=32] {'shard'}, dimensions={0} | all-to-all | bytes 32768 | tf_op jit(solution)/shard_map/all_to_all | solution.py:428
  142.4 0.0 copy-done.1
  142.4 0.7 last_duals.1
  (6 shorter events, 0.2 us)
Async XLA Ops:
  0.6 24.9 %copy-start.3 = (s32[256,16]{0,1:T(8,128)S(1)}, s32[256,16]{0,1:T(8,128)}, u32[]{:S(2)}) copy-start(s32[256,16]{0,1:T(8,128)} %param.6) | copy-start | bytes 49156
  0.6 27.1 %copy-start.4 = (s32[256]{0:T(256)S(1)}, s32[256]{0:T(256)}, u32[]{:S(2)}) copy-start(s32[256]{0:T(256)} %param.9) | copy-start | bytes 3076
  0.7 0.8 copy-start
  23.7 4.1 %collective-permute-start = (f32[1664,128]{1,0:T(8,128)S(1)}, f32[1664,128]{1,0:T(8,128)S(1)}, u32[]{:S(2)}, u32[]{:S(2)}) collective-permute-start(f32[1664,128]{1,0:T(8,128)S(1)} %bitcast.25), channel_id=1, source_target_pairs={{0,1},{1,0},{2,3},{3,2},{4,5},{5,4},{6,7},{7,6},{8,9},{9,8},{10,11... | collective-permute-start | bytes 2555912 | tf_op jit(solution)/shard_map/ppermute | solution.py:384
  40.8 2.5 %collective-permute-start.1 = (f32[1664,128]{1,0:T(8,128)S(1)}, f32[1664,128]{1,0:T(8,128)S(1)}, u32[]{:S(2)}, u32[]{:S(2)}) collective-permute-start(f32[1664,128]{1,0:T(8,128)S(1)} %get-tuple-element.13), channel_id=1, source_target_pairs={{0,1},{1,0},{2,3},{3,2},{4,5},{5,4},{6,7},{7,6},{8,9},{9,8},{10,11... | collective-permute-start | bytes 2555912 | tf_op jit(solution)/shard_map/ppermute | solution.py:384
  43.2 25.1 %copy-start.2 = (f32[12800]{0:T(1024)S(1)}, f32[12800]{0:T(1024)}, u32[]{:S(2)}) copy-start(f32[12800]{0:T(1024)} %param.10) | copy-start | bytes 153604
  60.4 4.0 %collective-permute-start.4 = (f32[104,128]{1,0:T(8,128)S(1)}, f32[104,128]{1,0:T(8,128)S(1)}, u32[]{:S(2)}, u32[]{:S(2)}) collective-permute-start(f32[104,128]{1,0:T(8,128)S(1)} %sum_chips.2.plane), channel_id=1, source_target_pairs={{0,96},{32,0},{64,32},{96,64},{1,97},{33,1},{65,33},{97,65},{2,98}... | collective-permute-start | bytes 159752 | tf_op jit(solution)/shard_map/ppermute | solution.py:400
  63.2 4.5 %collective-permute-start.3 = (f32[104,128]{1,0:T(8,128)S(1)}, f32[104,128]{1,0:T(8,128)S(1)}, u32[]{:S(2)}, u32[]{:S(2)}) collective-permute-start(f32[104,128]{1,0:T(8,128)S(1)} %sum_chips.2.plane), channel_id=1, source_target_pairs={{0,64},{32,96},{64,0},{96,32},{1,65},{33,97},{65,1},{97,33},{2,66}... | collective-permute-start | bytes 159752 | tf_op jit(solution)/shard_map/ppermute | solution.py:400
  63.6 4.7 %collective-permute-start.2 = (f32[104,128]{1,0:T(8,128)S(1)}, f32[104,128]{1,0:T(8,128)S(1)}, u32[]{:S(2)}, u32[]{:S(2)}) collective-permute-start(f32[104,128]{1,0:T(8,128)S(1)} %sum_chips.2.plane), channel_id=1, source_target_pairs={{0,32},{32,64},{64,96},{96,0},{1,33},{33,65},{65,97},{97,1},{2,34}... | collective-permute-start | bytes 159752 | tf_op jit(solution)/shard_map/ppermute | solution.py:400
  83.5 6.5 %collective-permute-start.5 = (f32[1664,128]{1,0:T(8,128)S(1)}, f32[1664,128]{1,0:T(8,128)S(1)}, u32[]{:S(2)}, u32[]{:S(2)}) collective-permute-start(f32[1664,128]{1,0:T(8,128)S(1)} %bitcast.28), channel_id=1, source_target_pairs={{0,1},{1,0},{2,3},{3,2},{4,5},{5,4},{6,7},{7,6},{8,9},{9,8},{10,11... | collective-permute-start | bytes 2555912 | tf_op jit(solution)/shard_map/ppermute | solution.py:384
  102.9 2.5 %collective-permute-start.6 = (f32[1664,128]{1,0:T(8,128)S(1)}, f32[1664,128]{1,0:T(8,128)S(1)}, u32[]{:S(2)}, u32[]{:S(2)}) collective-permute-start(f32[1664,128]{1,0:T(8,128)S(1)} %get-tuple-element.19), channel_id=1, source_target_pairs={{0,1},{1,0},{2,3},{3,2},{4,5},{5,4},{6,7},{7,6},{8,9},{9,8},{10,11... | collective-permute-start | bytes 2555912 | tf_op jit(solution)/shard_map/ppermute | solution.py:384
  105.5 36.9 %copy-start.1 = (f32[12800]{0:T(1024)S(1)}, f32[12800]{0:T(1024)}, u32[]{:S(2)}) copy-start(f32[12800]{0:T(1024)} %param.11) | copy-start | bytes 153604
  122.6 3.1 %collective-permute-start.9 = (f32[104,128]{1,0:T(8,128)S(1)}, f32[104,128]{1,0:T(8,128)S(1)}, u32[]{:S(2)}, u32[]{:S(2)}) collective-permute-start(f32[104,128]{1,0:T(8,128)S(1)} %sum_chips.3.plane), channel_id=1, source_target_pairs={{0,96},{32,0},{64,32},{96,64},{1,97},{33,1},{65,33},{97,65},{2,98}... | collective-permute-start | bytes 159752 | tf_op jit(solution)/shard_map/ppermute | solution.py:400
  123.2 4.5 %collective-permute-start.8 = (f32[104,128]{1,0:T(8,128)S(1)}, f32[104,128]{1,0:T(8,128)S(1)}, u32[]{:S(2)}, u32[]{:S(2)}) collective-permute-start(f32[104,128]{1,0:T(8,128)S(1)} %sum_chips.3.plane), channel_id=1, source_target_pairs={{0,64},{32,96},{64,0},{96,32},{1,65},{33,97},{65,1},{97,33},{2,66}... | collective-permute-start | bytes 159752 | tf_op jit(solution)/shard_map/ppermute | solution.py:400
  123.6 4.7 %collective-permute-start.7 = (f32[104,128]{1,0:T(8,128)S(1)}, f32[104,128]{1,0:T(8,128)S(1)}, u32[]{:S(2)}, u32[]{:S(2)}) collective-permute-start(f32[104,128]{1,0:T(8,128)S(1)} %sum_chips.3.plane), channel_id=1, source_target_pairs={{0,32},{32,64},{64,96},{96,0},{1,33},{33,65},{65,97},{97,1},{2,34}... | collective-permute-start | bytes 159752 | tf_op jit(solution)/shard_map/ppermute | solution.py:400

commit v4 on v3

--- a/solution.py
+++ b/solution.py
@@ -11,10 +11,6 @@
 DEAD = -1e30
 
 AXES = ("grp", "shard")
-
-
-def pad8(n):
-    return -(-n // SUB) * SUB
 
 
 def iteration_kernel(second, groups, blocks, half, item_count):
@@ -307,45 +303,50 @@
     )
 
 
-def spread_duals(x, chips, padded, core):
+def spread_duals(x, chips, core):
     own_rows = x.shape[0]
 
     def body(x, core, every):
         for p in range(chips):
-            every[p, pl.ds(0, own_rows), :] = x[...]
-            every[p, pl.ds(own_rows, padded - own_rows), :] = jnp.zeros((padded - own_rows, BLOCK), jnp.float32)
-
-    return vmem_call(body, "spread_duals", (chips, padded, BLOCK))(
+            every[pl.ds(p * own_rows, own_rows), :] = x[...]
+
+    return vmem_call(body, "spread_duals", (chips * own_rows, BLOCK))(
         x, jnp.full((SUB, BLOCK), core, jnp.int32))[0]
 
 
-def sum_chips(x):
+def sum_chips(x, chips):
+    own_rows = x.shape[0] // chips
+
     def body(x, out):
-        out[...] = jnp.sum(x[...], axis=0)
-
-    return vmem_call(body, "sum_chips", x.shape[1:])(x)[0]
-
-
-def gradient_of(plane, shifted, limit, gradient):
-    own_rows = limit.shape[0]
+        parts = [x[pl.ds(p * own_rows, own_rows), :] for p in range(chips)]
+        while len(parts) > 1:
+            parts = [a + b for a, b in zip(parts[::2], parts[1::2])]
+        out[...] = parts[0]
+
+    return vmem_call(body, "sum_chips", (own_rows, BLOCK))(x)[0]
+
+
+def gradient_of(plane, shifted, limit):
     one, two, three = shifted
-    gradient[...] = (plane[...] + two[...]) + (one[...] + three[...])
-    gradient[pl.ds(0, own_rows), :] = gradient[pl.ds(0, own_rows), :] - limit[...]
+    return ((plane[...] + two[...]) + (one[...] + three[...])) - limit[...]
 
 
 def spread_gradient(plane, shifted, limit, chips):
+    own_rows = plane.shape[0]
+
     def body(plane, one, two, three, limit, gradient, every):
-        gradient_of(plane, (one, two, three), limit, gradient)
+        g = gradient_of(plane, (one, two, three), limit)
+        gradient[...] = g
         for p in range(chips):
-            every[p] = gradient[...]
-
-    return vmem_call(body, "spread_gradient", plane.shape, (chips, *plane.shape))(plane, *shifted, limit)
+            every[pl.ds(p * own_rows, own_rows), :] = g
+
+    return vmem_call(body, "spread_gradient", plane.shape, (chips * own_rows, BLOCK))(plane, *shifted, limit)
 
 
 def last_gradient(plane, shifted, limit, shards):
     def body(plane, one, two, three, limit, gradient, parts):
-        gradient_of(plane, (one, two, three), limit, gradient)
-        g = gradient[...]
+        g = gradient_of(plane, (one, two, three), limit)
+        gradient[...] = g
         part = jnp.sum(jnp.sum(g * g, axis=0, keepdims=True), axis=1, keepdims=True)
         parts[...] = jnp.broadcast_to(part[None], parts.shape)
 
@@ -353,14 +354,11 @@
 
 
 def last_duals(duals, first, sumsq, second, parts, item_count):
-    own_rows = duals.shape[0]
-
     def body(duals, first, sumsq, second, parts, out):
-        own = pl.ds(0, own_rows)
         scale = jnp.sqrt(sumsq[0:1, :] / item_count + 1e-6)
-        lam = jnp.maximum(duals[...] + 0.5 * first[own, :] / scale, 0.0)
+        lam = jnp.maximum(duals[...] + 0.5 * first[...] / scale, 0.0)
         scale = jnp.sqrt(jnp.sum(parts[...], axis=0) / item_count + 1e-6)
-        out[...] = jnp.maximum(lam + 0.5 * second[own, :] / scale, 0.0)
+        out[...] = jnp.maximum(lam + 0.5 * second[...] / scale, 0.0)
 
     return vmem_call(body, "last_duals", duals.shape)(duals, first, sumsq, second, parts)[0]
 
@@ -375,8 +373,7 @@
     own_items = item_limit.shape[0]
     item_count = own_items * shard_size
     own_rows = own_items // BLOCK
-    padded = pad8(own_rows)
-    half = chips * padded
+    half = chips * own_rows
     full = 2 * half
     core = lax.axis_index("shard") % 2
 
@@ -386,23 +383,25 @@
     def as_rows(x):
         return x.reshape(groups, SUB, blocks, BLOCK).transpose(0, 2, 1, 3).reshape(-1, BLOCK)
 
+    def exchange(x):
+        x = x.reshape(chips, 1, own_items)
+        return lax.all_to_all(
+            x, "shard", 0, 0, axis_index_groups=same_core, tiled=True).reshape(half, BLOCK)
+
     def gather_halves(every):
-        every = lax.all_to_all(
-            every, "shard", 0, 0, axis_index_groups=same_core, tiled=True).reshape(half, BLOCK)
+        every = exchange(every)
         return every, swap_cores(every)
 
     def reduce_loads(keep, send):
         chip = keep + swap_cores(send)
-        plane = sum_chips(lax.all_to_all(
-            chip.reshape(chips, padded, BLOCK), "shard", 0, 0,
-            axis_index_groups=same_core, tiled=True))
+        plane = sum_chips(exchange(chip), chips)
         return plane, [
             lax.ppermute(plane, "grp", [(g, (g + d) % grp_size) for g in range(grp_size)])
             for d in range(1, grp_size)
         ]
 
     shard_of = candidates // own_rows
-    gidx = (jnp.where(shard_of % 2 == core, 0, half) + (shard_of // 2) * padded + candidates % own_rows).reshape(-1)
+    gidx = (jnp.where(shard_of % 2 == core, 0, half) + (shard_of // 2) * own_rows + candidates % own_rows).reshape(-1)
     batch = gidx.reshape(-1, blocks)
     earlier = jnp.arange(blocks)[:, None] > jnp.arange(blocks)[None, :]
     copy = jnp.sum((batch[:, :, None] == batch[:, None, :]) & earlier, axis=2, dtype=jnp.int32)
@@ -416,7 +415,7 @@
     limit = item_limit.reshape(own_rows, BLOCK)
     duals = item_duals.reshape(own_rows, BLOCK)
 
-    own_d, other_d = gather_halves(spread_duals(duals, chips, padded, core))
+    own_d, other_d = gather_halves(spread_duals(duals, chips, core))
     keep, send = iteration_kernel(False, groups, blocks, half, item_count)(
         gidx, sidx, ncopy, own_d, other_d, aff, exp, nlive)
     first, every = spread_gradient(*reduce_loads(keep, send), limit, chips)

time: 143 us -> 142 us (level)
  no operation moved by 1% of the time
where the time goes in v4:
time: 142 us; the launch traced here: 141 us
  blocking collectives  83.8 us (59%)
  Pallas kernels  26.8 us (19%)
  waiting for transfers between devices  14.1 us (10%)
  starting transfers between devices  12.4 us (9%)
  local copies, waits for them, and re-layouts  1.67 us (1%)
  between operations  1.43 us (1%)
    all_to_all x4, blocking collectives, exchange(): lax.all_to_all(x, 'shard', 0, 0, axis_index_groups=same_core, tiled=True)  70.2 us
    pallas_call x2, Pallas kernels, run(): return call(gidx, sidx, ncopy, *tables, aff, exp, nlive)  25.8 us
    all_to_all x1, blocking collectives, local(): parts = lax.all_to_all(parts, 'shard', 0, 0, tiled=True)  13.6 us
    ppermute x6, waiting for transfers between devices, reduce_loads(): lax.ppermute(plane, 'grp', [(g, (g + d) % grp_size) for g in range(grp_si...  7.89 us
    ppermute x4, starting transfers between devices, swap_cores(): return lax.ppermute(x, AXES, swap)  6.78 us
    ppermute x4, waiting for transfers between devices, swap_cores(): return lax.ppermute(x, AXES, swap)  6.25 us
    ppermute x6, starting transfers between devices, reduce_loads(): lax.ppermute(plane, 'grp', [(g, (g + d) % grp_size) for g in range(grp_si...  5.63 us
  transfers between devices with their start and end apart: 10, of which 9 were waited for; matrix products, arithmetic and copies ran while one was open for 1% of the time, Pallas kernels for 0%

profile of v4, /device:TPU:1, one launch (start us, length us, event | category | flops | bytes accessed | tf_op | source)
XLA Modules:
  0.0 141.3 jit_solution(2481302997169591911)
XLA Ops:
  0.6 0.0 copy-start.3
  0.6 0.0 copy-start.4
  0.7 0.0 copy-start.1
  0.7 0.8 copy-done.1
  1.5 0.1 spread_duals.1
  1.5 21.8 %all_to_all.25 = f32[16,1,12800]{2,1,0:T(1,128)S(1)} all-to-all(f32[16,1,12800]{2,1,0:T(1,128)S(1)} %bitcast.32), channel_id=1, replica_groups={{0,2,4,6,8,10,12,14,16,18,20,22,24,26,28,30},{1,3,5,7,9,11,13,15,17,19,..., dimensions={0} | all-to-all | bytes 1638400 | tf_op jit(solution)/shard_map/all_to_all | solution.py:388
  23.4 1.8 %collective-permute-start = (f32[1600,128]{1,0:T(8,128)S(1)}, f32[1600,128]{1,0:T(8,128)S(1)}, u32[]{:S(2)}, u32[]{:S(2)}) collective-permute-start(f32[1600,128]{1,0:T(8,128)S(1)} %bitcast.29), channel_id=1, source_target_pairs={{0,1},{1,0},{2,3},{3,2},{4,5},{5,4},{6,7},{7,6},{8,9},{9,8},{10,11... | collective-permute-start | bytes 2457608 | tf_op jit(solution)/shard_map/ppermute | solution.py:381
  25.2 0.0 copy-done.3
  25.2 0.1 copy.26
  25.3 0.1 convert_reduce_fusion
  25.5 0.6 fusion.7
  26.7 0.1 copy.28
  26.8 0.1 reshape.83
  27.0 0.1 copy.29
  27.1 0.1 reshape.84.refs_1_
  27.1 0.1 reshape_reshape.3
  27.2 0.1 copy.27
  27.3 0.1 reshape.82.refs_0_
  27.4 0.0 copy-done.4
  27.4 0.0 collective-permute-done.refs_4_
  27.5 0.1 broadcast_in_dim.20.refs_7_.refs_9_
  27.6 12.9 %iterate1.1 = (f32[1600,128]{1,0:T(8,128)S(1)}, f32[1600,128]{1,0:T(8,128)S(1)}) custom-call(s32[4096]{0:T(1024)S(1)} %reshape.82.refs_0_, s32[4096]{0:T(1024)S(1)} %reshape.84.refs_1_, s32[1]{0:T(128)} %bitcast.2.refs_2_, f32[1600,128]{1,0:T(8,128)S(1)} %bitcast.30, f32[1600,128]{1,0:T(8,128)S(1)} %collective-permute-done.refs_4_, f32[4096,128]{1,0:T(8,128)} %bitcast.42, ...), custom_call_target="tpu_custom_call" | custom-call | tf_op jit(solution)/shard_map/iterate1/pallas_call | solution.py:290
  40.4 0.1 collective-permute-start.1
  40.5 2.3 %collective-permute-done.1 = f32[1600,128]{1,0:T(8,128)S(1)} collective-permute-done((f32[1600,128]{1,0:T(8,128)S(1)}, f32[1600,128]{1,0:T(8,128)S(1)}, u32[]{:S(2)}, u32[]{:S(2)}) %collective-permute-start.1) | collective-permute-done | bytes 819232 | tf_op jit(solution)/shard_map/ppermute | solution.py:381
  42.8 0.0 copy-start
  42.8 0.1 add.42
  43.0 16.9 %all_to_all.26 = f32[16,1,12800]{2,1,0:T(1,128)S(1)} all-to-all(f32[16,1,12800]{2,1,0:T(1,128)S(1)} %bitcast.46), channel_id=1, replica_groups={{0,2,4,6,8,10,12,14,16,18,20,22,24,26,28,30},{1,3,5,7,9,11,13,15,17,19,..., dimensions={0} | all-to-all | bytes 1638400 | tf_op jit(solution)/shard_map/all_to_all | solution.py:388
  59.9 2.8 %collective-permute-start.4 = (f32[100,128]{1,0:T(8,128)S(1)}, f32[100,128]{1,0:T(8,128)S(1)}, u32[]{:S(2)}, u32[]{:S(2)}) collective-permute-start(f32[100,128]{1,0:T(8,128)S(1)} %sum_chips.2.plane), channel_id=1, source_target_pairs={{0,96},{32,0},{64,32},{96,64},{1,97},{33,1},{65,33},{97,65},{2,98}... | collective-permute-start | bytes 153608 | tf_op jit(solution)/shard_map/ppermute | solution.py:399
  62.7 0.3 collective-permute-start.3
  63.0 0.7 collective-permute-start.2
  63.7 0.1 collective-permute-done.4.three
  63.9 3.3 %collective-permute-done.3.two = f32[100,128]{1,0:T(8,128)S(1)} collective-permute-done((f32[100,128]{1,0:T(8,128)S(1)}, f32[100,128]{1,0:T(8,128)S(1)}, u32[]{:S(2)}, u32[]{:S(2)}) %collective-permute-start.3) | collective-permute-done | bytes 51232 | tf_op jit(solution)/shard_map/ppermute | solution.py:399
  67.2 0.5 collective-permute-done.2.one
  67.7 0.0 copy-done
  67.7 0.1 spread_gradient.1
  67.8 14.6 %all_to_all.27 = f32[16,1,12800]{2,1,0:T(1,128)S(1)} all-to-all(f32[16,1,12800]{2,1,0:T(1,128)S(1)} %bitcast.37), channel_id=1, replica_groups={{0,2,4,6,8,10,12,14,16,18,20,22,24,26,28,30},{1,3,5,7,9,11,13,15,17,19,..., dimensions={0} | all-to-all | bytes 1638400 | tf_op jit(solution)/shard_map/all_to_all | solution.py:388
  82.4 4.4 %collective-permute-start.5 = (f32[1600,128]{1,0:T(8,128)S(1)}, f32[1600,128]{1,0:T(8,128)S(1)}, u32[]{:S(2)}, u32[]{:S(2)}) collective-permute-start(f32[1600,128]{1,0:T(8,128)S(1)} %bitcast.35), channel_id=1, source_target_pairs={{0,1},{1,0},{2,3},{3,2},{4,5},{5,4},{6,7},{7,6},{8,9},{9,8},{10,11... | collective-permute-start | bytes 2457608 | tf_op jit(solution)/shard_map/ppermute | solution.py:381
  86.8 2.0 %collective-permute-done.5.refs_6_ = f32[1600,128]{1,0:T(8,128)S(1)} collective-permute-done((f32[1600,128]{1,0:T(8,128)S(1)}, f32[1600,128]{1,0:T(8,128)S(1)}, u32[]{:S(2)}, u32[]{:S(2)}) %collective-permute-start.5) | collective-permute-done | bytes 819232 | tf_op jit(solution)/shard_map/ppermute | solution.py:381
  88.8 13.0 %iterate2.1 = (f32[1600,128]{1,0:T(8,128)S(1)}, f32[1600,128]{1,0:T(8,128)S(1)}, f32[4096,128]{1,0:T(8,128)}, f32[8,128]{1,0:T(8,128)S(1)}) custom-call(s32[4096]{0:T(1024)S(1)} %reshape.82.refs_0_, s32[4096]{0:T(1024)S(1)} %reshape.84.refs_1_, s32[1]{0:T(128)} %bitcast.2.refs_2_, f32[1600,128]{1,0:T(8,128)S(1)} %bitcast.31, ...), custom_call_target="tpu_custom_call" | custom-call | tf_op jit(solution)/shard_map/iterate2/pallas_call | solution.py:290
  101.8 0.4 collective-permute-start.6
  102.2 2.0 %collective-permute-done.6 = f32[1600,128]{1,0:T(8,128)S(1)} collective-permute-done((f32[1600,128]{1,0:T(8,128)S(1)}, f32[1600,128]{1,0:T(8,128)S(1)}, u32[]{:S(2)}, u32[]{:S(2)}) %collective-permute-start.6) | collective-permute-done | bytes 819232 | tf_op jit(solution)/shard_map/ppermute | solution.py:381
  104.2 0.0 copy-start.2
  104.2 0.1 add.43
  104.3 16.8 %all_to_all.28 = f32[16,1,12800]{2,1,0:T(1,128)S(1)} all-to-all(f32[16,1,12800]{2,1,0:T(1,128)S(1)} %bitcast.47), channel_id=1, replica_groups={{0,2,4,6,8,10,12,14,16,18,20,22,24,26,28,30},{1,3,5,7,9,11,13,15,17,19,..., dimensions={0} | all-to-all | bytes 1638400 | tf_op jit(solution)/shard_map/all_to_all | solution.py:388
  121.2 0.6 collective-permute-start.9
  121.8 0.4 collective-permute-start.8
  122.2 0.8 collective-permute-start.7
  123.0 1.3 collective-permute-done.9.three
  124.2 2.1 %collective-permute-done.8.two = f32[100,128]{1,0:T(8,128)S(1)} collective-permute-done((f32[100,128]{1,0:T(8,128)S(1)}, f32[100,128]{1,0:T(8,128)S(1)}, u32[]{:S(2)}, u32[]{:S(2)}) %collective-permute-start.8) | collective-permute-done | bytes 51232 | tf_op jit(solution)/shard_map/ppermute | solution.py:399
  126.3 0.5 collective-permute-done.7.one
  126.9 0.1 last_gradient.1
  127.0 13.6 %all_to_all.29.parts = f32[32,1,128]{2,1,0:T(1,128)S(1)} all-to-all(f32[32,1,128]{2,1,0:T(1,128)S(1)} %get-tuple-element.21), channel_id=1, replica_groups=mesh['grp'=4,'shard'=32] {'shard'}, dimensions={0} | all-to-all | bytes 32768 | tf_op jit(solution)/shard_map/all_to_all | solution.py:427
  140.6 0.0 copy-done.2
  140.6 0.7 last_duals.1
  (6 shorter events, 0.1 us)
Async XLA Ops:
  0.6 24.5 %copy-start.3 = (s32[256,16]{0,1:T(8,128)S(1)}, s32[256,16]{0,1:T(8,128)}, u32[]{:S(2)}) copy-start(s32[256,16]{0,1:T(8,128)} %param.6) | copy-start | bytes 49156
  0.6 26.8 %copy-start.4 = (s32[256]{0:T(256)S(1)}, s32[256]{0:T(256)}, u32[]{:S(2)}) copy-start(s32[256]{0:T(256)} %param.9) | copy-start | bytes 3076
  0.7 0.8 copy-start.1
  23.4 4.1 %collective-permute-start = (f32[1600,128]{1,0:T(8,128)S(1)}, f32[1600,128]{1,0:T(8,128)S(1)}, u32[]{:S(2)}, u32[]{:S(2)}) collective-permute-start(f32[1600,128]{1,0:T(8,128)S(1)} %bitcast.29), channel_id=1, source_target_pairs={{0,1},{1,0},{2,3},{3,2},{4,5},{5,4},{6,7},{7,6},{8,9},{9,8},{10,11... | collective-permute-start | bytes 2457608 | tf_op jit(solution)/shard_map/ppermute | solution.py:381
  40.4 2.4 %collective-permute-start.1 = (f32[1600,128]{1,0:T(8,128)S(1)}, f32[1600,128]{1,0:T(8,128)S(1)}, u32[]{:S(2)}, u32[]{:S(2)}) collective-permute-start(f32[1600,128]{1,0:T(8,128)S(1)} %get-tuple-element.13), channel_id=1, source_target_pairs={{0,1},{1,0},{2,3},{3,2},{4,5},{5,4},{6,7},{7,6},{8,9},{9,8},{10,11... | collective-permute-start | bytes 2457608 | tf_op jit(solution)/shard_map/ppermute | solution.py:381
  42.8 24.9 %copy-start = (f32[12800]{0:T(1024)S(1)}, f32[12800]{0:T(1024)}, u32[]{:S(2)}) copy-start(f32[12800]{0:T(1024)} %param.10) | copy-start | bytes 153604
  59.9 4.0 %collective-permute-start.4 = (f32[100,128]{1,0:T(8,128)S(1)}, f32[100,128]{1,0:T(8,128)S(1)}, u32[]{:S(2)}, u32[]{:S(2)}) collective-permute-start(f32[100,128]{1,0:T(8,128)S(1)} %sum_chips.2.plane), channel_id=1, source_target_pairs={{0,96},{32,0},{64,32},{96,64},{1,97},{33,1},{65,33},{97,65},{2,98}... | collective-permute-start | bytes 153608 | tf_op jit(solution)/shard_map/ppermute | solution.py:399
  62.7 4.5 %collective-permute-start.3 = (f32[100,128]{1,0:T(8,128)S(1)}, f32[100,128]{1,0:T(8,128)S(1)}, u32[]{:S(2)}, u32[]{:S(2)}) collective-permute-start(f32[100,128]{1,0:T(8,128)S(1)} %sum_chips.2.plane), channel_id=1, source_target_pairs={{0,64},{32,96},{64,0},{96,32},{1,65},{33,97},{65,1},{97,33},{2,66}... | collective-permute-start | bytes 153608 | tf_op jit(solution)/shard_map/ppermute | solution.py:399
  63.0 4.7 %collective-permute-start.2 = (f32[100,128]{1,0:T(8,128)S(1)}, f32[100,128]{1,0:T(8,128)S(1)}, u32[]{:S(2)}, u32[]{:S(2)}) collective-permute-start(f32[100,128]{1,0:T(8,128)S(1)} %sum_chips.2.plane), channel_id=1, source_target_pairs={{0,32},{32,64},{64,96},{96,0},{1,33},{33,65},{65,97},{97,1},{2,34}... | collective-permute-start | bytes 153608 | tf_op jit(solution)/shard_map/ppermute | solution.py:399
  82.4 6.4 %collective-permute-start.5 = (f32[1600,128]{1,0:T(8,128)S(1)}, f32[1600,128]{1,0:T(8,128)S(1)}, u32[]{:S(2)}, u32[]{:S(2)}) collective-permute-start(f32[1600,128]{1,0:T(8,128)S(1)} %bitcast.35), channel_id=1, source_target_pairs={{0,1},{1,0},{2,3},{3,2},{4,5},{5,4},{6,7},{7,6},{8,9},{9,8},{10,11... | collective-permute-start | bytes 2457608 | tf_op jit(solution)/shard_map/ppermute | solution.py:381
  101.8 2.4 %collective-permute-start.6 = (f32[1600,128]{1,0:T(8,128)S(1)}, f32[1600,128]{1,0:T(8,128)S(1)}, u32[]{:S(2)}, u32[]{:S(2)}) collective-permute-start(f32[1600,128]{1,0:T(8,128)S(1)} %get-tuple-element.19), channel_id=1, source_target_pairs={{0,1},{1,0},{2,3},{3,2},{4,5},{5,4},{6,7},{7,6},{8,9},{9,8},{10,11... | collective-permute-start | bytes 2457608 | tf_op jit(solution)/shard_map/ppermute | solution.py:381
  104.2 36.4 %copy-start.2 = (f32[12800]{0:T(1024)S(1)}, f32[12800]{0:T(1024)}, u32[]{:S(2)}) copy-start(f32[12800]{0:T(1024)} %param.11) | copy-start | bytes 153604
  121.2 3.1 %collective-permute-start.9 = (f32[100,128]{1,0:T(8,128)S(1)}, f32[100,128]{1,0:T(8,128)S(1)}, u32[]{:S(2)}, u32[]{:S(2)}) collective-permute-start(f32[100,128]{1,0:T(8,128)S(1)} %sum_chips.3.plane), channel_id=1, source_target_pairs={{0,96},{32,0},{64,32},{96,64},{1,97},{33,1},{65,33},{97,65},{2,98}... | collective-permute-start | bytes 153608 | tf_op jit(solution)/shard_map/ppermute | solution.py:399
  121.8 4.5 %collective-permute-start.8 = (f32[100,128]{1,0:T(8,128)S(1)}, f32[100,128]{1,0:T(8,128)S(1)}, u32[]{:S(2)}, u32[]{:S(2)}) collective-permute-start(f32[100,128]{1,0:T(8,128)S(1)} %sum_chips.3.plane), channel_id=1, source_target_pairs={{0,64},{32,96},{64,0},{96,32},{1,65},{33,97},{65,1},{97,33},{2,66}... | collective-permute-start | bytes 153608 | tf_op jit(solution)/shard_map/ppermute | solution.py:399
  122.2 4.7 %collective-permute-start.7 = (f32[100,128]{1,0:T(8,128)S(1)}, f32[100,128]{1,0:T(8,128)S(1)}, u32[]{:S(2)}, u32[]{:S(2)}) collective-permute-start(f32[100,128]{1,0:T(8,128)S(1)} %sum_chips.3.plane), channel_id=1, source_target_pairs={{0,32},{32,64},{64,96},{96,0},{1,33},{33,65},{65,97},{97,1},{2,34}... | collective-permute-start | bytes 153608 | tf_op jit(solution)/shard_map/ppermute | solution.py:399

commit v5 on v4

--- a/solution.py
+++ b/solution.py
@@ -8,6 +8,7 @@
 BLOCK = 128
 BISECT = 16
 SUB = 8
+COPIES = 8
 DEAD = -1e30
 
 AXES = ("grp", "shard")
@@ -29,13 +30,14 @@
         if second:
             (gidx_in, sidx_in, ncopy, own_d, other_d, own_g, other_g, aff_in, exp_in, nlive,
              keep, send, primal_out, sumsq,
-             table, work_a, work_b, acc, lo, up, peaks, sums, aff, exp, gidx, sidx, sem_in, sem_id,
+             table, work_a, work_b, acc_even, acc_odd, lo, up, peaks, sums, aff, exp, gidx, sidx, sem_in, sem_id,
              primal, sem_out) = refs
         else:
             (gidx_in, sidx_in, ncopy, own_d, other_d, aff_in, exp_in, nlive,
              keep, send,
-             table, work_a, work_b, acc, lo, up, peaks, sums, aff, exp, gidx, sidx, sem_in, sem_id) = refs
+             table, work_a, work_b, acc_even, acc_odd, lo, up, peaks, sums, aff, exp, gidx, sidx, sem_in, sem_id) = refs
         works = (work_a, work_b)
+        accs = (acc_even, acc_odd)
 
         ids_in = [pltpu.make_async_copy(src, dst, sem_id.at[k])
                   for k, (src, dst) in enumerate(((gidx_in, gidx), (sidx_in, sidx)))]
@@ -79,22 +81,26 @@
         lax.fori_loop(0, half // SUB, fill_table, 0, unroll=8)
 
         n = ncopy[0]
+        fits = n <= COPIES
+        used = jnp.where(fits, n, 1)
         zero = jnp.zeros((SUB, BLOCK), f32)
         dead = jnp.full((SUB, BLOCK), DEAD, f32)
         vregs = full // SUB
-        per_step = 2 * vregs // (2 * BISECT)
-        assert per_step * BISECT == vregs
-
-        def clear(i, c):
-            acc[pl.ds(pl.multiple_of(i * SUB, SUB), SUB), :] = zero
+        per_step = vregs // (2 * BISECT)
+        assert per_step * 2 * BISECT <= vregs and vregs % 16 == 0
+
+        def clear(first, count):
+            for acc in accs:
+                some = acc.at[pl.ds(pl.multiple_of(first * SUB, SUB), count * SUB), :]
+                for i in range(count):
+                    some[pl.ds(i * SUB, SUB), :] = zero
+
+        def clear_16(i, c):
+            clear(16 * i, 16)
             return c
 
-        lax.fori_loop(2 * vregs // 16, n * vregs // 16, lambda i, c: [clear(16 * i + j, c) for j in range(16)][-1], 0)
-
-        def clear_some(k):
-            some = acc.at[pl.ds(pl.multiple_of(k * (per_step * SUB), SUB), per_step * SUB), :]
-            for i in range(per_step):
-                some[pl.ds(i * SUB, SUB), :] = zero
+        lax.fori_loop(vregs // 16, used * vregs // 16, clear_16, 0)
+        clear(per_step * 2 * BISECT, vregs - per_step * 2 * BISECT)
 
         def loop(first, last, f):
             def trip(i, c):
@@ -189,11 +195,12 @@
                     primal[pl.ds(rows + b * SUB, SUB), :] = x
                 works[h][now, :] = exp[pl.ds(rows + b * SUB, SUB), :] * x
 
-        def scatter(h, g, first, count):
+        def scatter(h, g, first, count, parity=0):
             here = g * group_rows + first
             work = works[h]
             for s in range(count):
                 where = [picked(sidx, s * blocks + b, h * part + g + first * blocks * groups) for b in range(blocks)]
+                acc = accs[(s + parity) % 2]
                 added = [acc[pl.ds(i, 1), :] + work[pl.ds(here + b * SUB + s, 1), :] for b, i in enumerate(where)]
                 for i, v in zip(where, added):
                     acc[pl.ds(i, 1), :] = v
@@ -209,7 +216,7 @@
         for load in loads[pieces]:
             load.wait()
         bisect(0, lambda g, q: [(quarter - 1, lambda: gather(1, g, q * (blocks // 2), blocks // 2)),
-                                (quarter - 1, lambda: clear_some(2 * g + q))])
+                                (quarter - 1, lambda: clear((2 * g + q) * per_step, per_step))])
 
         start_bisection(1)
         loop(0, part, lambda g: allocate(0, g))
@@ -219,16 +226,39 @@
                 primal_out.at[pl.ds(h * part_rows, part_rows), :], sem_out.at[h]) for h in range(2)]
             stores[0].start()
         ids_in[1].wait()
-        bisect(1, lambda g, q: [(2 * m, lambda m=m: scatter(0, g, q * (SUB // 2) + m, 1)) for m in range(SUB // 2)])
+        @pl.when(fits)
+        def _():
+            bisect(1, lambda g, q: [(2 * m, lambda m=m: scatter(0, g, q * (SUB // 2) + m, 1, m)) for m in range(SUB // 2)])
+
+        @pl.when(jnp.logical_not(fits))
+        def _():
+            bisect(1, lambda g, q: [])
+
         loop(0, part, lambda g: allocate(1, g))
         if second:
             stores[1].start()
-        loop(0, part, lambda g: scatter(1, g, 0, SUB))
+
+        @pl.when(fits)
+        def _():
+            loop(0, part, lambda g: scatter(1, g, 0, SUB))
+
+        @pl.when(jnp.logical_not(fits))
+        def _():
+            def one(h, k):
+                g = k // group_rows
+                j = k - g * group_rows
+                s = j // blocks
+                i = gidx[j * groups + h * part + g]
+                r = g * group_rows + (j - s * blocks) * SUB + s
+                acc_even[pl.ds(i, 1), :] = acc_even[pl.ds(i, 1), :] + works[h][pl.ds(r, 1), :]
+
+            for h in range(2):
+                loop(0, part_rows, lambda k: one(h, k))
 
         def finish(i, c):
             r = pl.multiple_of(i * SUB, SUB)
             for out, o in ((keep, 0), (send, half)):
-                out[pl.ds(r, SUB), :] = acc[pl.ds(r + o, SUB), :] + acc[pl.ds(r + (full + o), SUB), :]
+                out[pl.ds(r, SUB), :] = acc_even[pl.ds(r + o, SUB), :] + acc_odd[pl.ds(r + o, SUB), :]
             return c
 
         lax.fori_loop(0, half // SUB, finish, 0, unroll=8)
@@ -238,12 +268,12 @@
                 r = pl.multiple_of(i * SUB, SUB)
                 a = pl.multiple_of(t * full + r, SUB)
                 for out, o in ((keep, 0), (send, half)):
-                    out[pl.ds(r, SUB), :] += acc[pl.ds(a + o, SUB), :]
+                    out[pl.ds(r, SUB), :] += acc_even[pl.ds(a + o, SUB), :] + acc_odd[pl.ds(a + o, SUB), :]
                 return c
 
             return lax.fori_loop(0, half // SUB, more, c, unroll=8)
 
-        lax.fori_loop(2, n, finish_copy, 0)
+        lax.fori_loop(1, used, finish_copy, 0)
         if second:
             for store in stores:
                 store.wait()
@@ -257,7 +287,8 @@
         pltpu.VMEM((full, BLOCK), f32),
         pltpu.VMEM((part_rows, BLOCK), f32),
         pltpu.VMEM((part_rows, BLOCK), f32),
-        pltpu.VMEM((blocks * full, BLOCK), f32),
+        pltpu.VMEM((COPIES * full, BLOCK), f32),
+        pltpu.VMEM((COPIES * full, BLOCK), f32),
         pltpu.VMEM((members, BLOCK), f32),
         pltpu.VMEM((members, BLOCK), f32),
         pltpu.VMEM((members, BLOCK), f32),

time: 142 us -> 140 us (0.986)
  Pallas kernels: 26.8 us -> 24.9 us
    pallas_call x2, Pallas kernels: 25.8 us -> 23.9 us  [run(): return call(gidx, sidx, ncopy, *tables, aff, exp, nlive)]
where the time goes in v5:
time: 140 us; the launch traced here: 139 us
  blocking collectives  83.8 us (60%)
  Pallas kernels  24.9 us (18%)
  waiting for transfers between devices  14.1 us (10%)
  starting transfers between devices  12.5 us (9%)
  local copies, waits for them, and re-layouts  1.67 us (1%)
  between operations  1.43 us (1%)
    all_to_all x4, blocking collectives, exchange(): lax.all_to_all(x, 'shard', 0, 0, axis_index_groups=same_core, tiled=True)  70.1 us
    pallas_call x2, Pallas kernels, run(): return call(gidx, sidx, ncopy, *tables, aff, exp, nlive)  23.9 us
    all_to_all x1, blocking collectives, local(): parts = lax.all_to_all(parts, 'shard', 0, 0, tiled=True)  13.6 us
    ppermute x6, waiting for transfers between devices, reduce_loads(): lax.ppermute(plane, 'grp', [(g, (g + d) % grp_size) for g in range(grp_si...  7.88 us
    ppermute x4, starting transfers between devices, swap_cores(): return lax.ppermute(x, AXES, swap)  6.86 us
    ppermute x4, waiting for transfers between devices, swap_cores(): return lax.ppermute(x, AXES, swap)  6.19 us
    ppermute x6, starting transfers between devices, reduce_loads(): lax.ppermute(plane, 'grp', [(g, (g + d) % grp_size) for g in range(grp_si...  5.66 us
  transfers between devices with their start and end apart: 10, of which 9 were waited for; matrix products, arithmetic and copies ran while one was open for 1% of the time, Pallas kernels for 0%

profile of v5, /device:TPU:1, one launch (start us, length us, event | category | flops | bytes accessed | tf_op | source)
XLA Modules:
  0.0 139.4 jit_solution(411584634542131950)
XLA Ops:
  0.6 0.0 copy-start.3
  0.6 0.0 copy-start.4
  0.7 0.0 copy-start.1
  0.7 0.8 copy-done.1
  1.5 0.1 spread_duals.1
  1.5 21.8 %all_to_all.25 = f32[16,1,12800]{2,1,0:T(1,128)S(1)} all-to-all(f32[16,1,12800]{2,1,0:T(1,128)S(1)} %bitcast.32), channel_id=1, replica_groups={{0,2,4,6,8,10,12,14,16,18,20,22,24,26,28,30},{1,3,5,7,9,11,13,15,17,19,..., dimensions={0} | all-to-all | bytes 1638400 | tf_op jit(solution)/shard_map/all_to_all | solution.py:419
  23.4 1.8 %collective-permute-start = (f32[1600,128]{1,0:T(8,128)S(1)}, f32[1600,128]{1,0:T(8,128)S(1)}, u32[]{:S(2)}, u32[]{:S(2)}) collective-permute-start(f32[1600,128]{1,0:T(8,128)S(1)} %bitcast.29), channel_id=1, source_target_pairs={{0,1},{1,0},{2,3},{3,2},{4,5},{5,4},{6,7},{7,6},{8,9},{9,8},{10,11... | collective-permute-start | bytes 2457608 | tf_op jit(solution)/shard_map/ppermute | solution.py:412
  25.2 0.0 copy-done.3
  25.2 0.1 copy.26
  25.3 0.1 convert_reduce_fusion
  25.5 0.6 fusion.7
  26.7 0.1 copy.28
  26.8 0.1 reshape.83
  27.0 0.1 copy.29
  27.1 0.1 reshape.84.refs_1_
  27.1 0.1 reshape_reshape.3
  27.2 0.1 copy.27
  27.3 0.1 reshape.82.refs_0_
  27.4 0.0 copy-done.4
  27.4 0.0 collective-permute-done.refs_4_
  27.5 0.1 broadcast_in_dim.20.refs_7_.refs_9_
  27.6 11.9 %iterate1.1 = (f32[1600,128]{1,0:T(8,128)S(1)}, f32[1600,128]{1,0:T(8,128)S(1)}) custom-call(s32[4096]{0:T(1024)S(1)} %reshape.82.refs_0_, s32[4096]{0:T(1024)S(1)} %reshape.84.refs_1_, s32[1]{0:T(128)} %bitcast.2.refs_2_, f32[1600,128]{1,0:T(8,128)S(1)} %bitcast.30, f32[1600,128]{1,0:T(8,128)S(1)} %collective-permute-done.refs_4_, f32[4096,128]{1,0:T(8,128)} %bitcast.42, ...), custom_call_target="tpu_custom_call" | custom-call | tf_op jit(solution)/shard_map/iterate1/pallas_call | solution.py:321
  39.5 0.1 collective-permute-start.1
  39.6 2.3 %collective-permute-done.1 = f32[1600,128]{1,0:T(8,128)S(1)} collective-permute-done((f32[1600,128]{1,0:T(8,128)S(1)}, f32[1600,128]{1,0:T(8,128)S(1)}, u32[]{:S(2)}, u32[]{:S(2)}) %collective-permute-start.1) | collective-permute-done | bytes 819232 | tf_op jit(solution)/shard_map/ppermute | solution.py:412
  41.9 0.0 copy-start
  41.9 0.1 add.42
  42.0 16.9 %all_to_all.26 = f32[16,1,12800]{2,1,0:T(1,128)S(1)} all-to-all(f32[16,1,12800]{2,1,0:T(1,128)S(1)} %bitcast.46), channel_id=1, replica_groups={{0,2,4,6,8,10,12,14,16,18,20,22,24,26,28,30},{1,3,5,7,9,11,13,15,17,19,..., dimensions={0} | all-to-all | bytes 1638400 | tf_op jit(solution)/shard_map/all_to_all | solution.py:419
  58.9 2.8 %collective-permute-start.4 = (f32[100,128]{1,0:T(8,128)S(1)}, f32[100,128]{1,0:T(8,128)S(1)}, u32[]{:S(2)}, u32[]{:S(2)}) collective-permute-start(f32[100,128]{1,0:T(8,128)S(1)} %sum_chips.2.plane), channel_id=1, source_target_pairs={{0,96},{32,0},{64,32},{96,64},{1,97},{33,1},{65,33},{97,65},{2,98}... | collective-permute-start | bytes 153608 | tf_op jit(solution)/shard_map/ppermute | solution.py:430
  61.7 0.4 collective-permute-start.3
  62.1 0.7 collective-permute-start.2
  62.8 0.2 collective-permute-done.4.three
  62.9 3.3 %collective-permute-done.3.two = f32[100,128]{1,0:T(8,128)S(1)} collective-permute-done((f32[100,128]{1,0:T(8,128)S(1)}, f32[100,128]{1,0:T(8,128)S(1)}, u32[]{:S(2)}, u32[]{:S(2)}) %collective-permute-start.3) | collective-permute-done | bytes 51232 | tf_op jit(solution)/shard_map/ppermute | solution.py:430
  66.3 0.5 collective-permute-done.2.one
  66.8 0.0 copy-done
  66.8 0.1 spread_gradient.1
  66.8 14.6 %all_to_all.27 = f32[16,1,12800]{2,1,0:T(1,128)S(1)} all-to-all(f32[16,1,12800]{2,1,0:T(1,128)S(1)} %bitcast.37), channel_id=1, replica_groups={{0,2,4,6,8,10,12,14,16,18,20,22,24,26,28,30},{1,3,5,7,9,11,13,15,17,19,..., dimensions={0} | all-to-all | bytes 1638400 | tf_op jit(solution)/shard_map/all_to_all | solution.py:419
  81.5 4.4 %collective-permute-start.5 = (f32[1600,128]{1,0:T(8,128)S(1)}, f32[1600,128]{1,0:T(8,128)S(1)}, u32[]{:S(2)}, u32[]{:S(2)}) collective-permute-start(f32[1600,128]{1,0:T(8,128)S(1)} %bitcast.35), channel_id=1, source_target_pairs={{0,1},{1,0},{2,3},{3,2},{4,5},{5,4},{6,7},{7,6},{8,9},{9,8},{10,11... | collective-permute-start | bytes 2457608 | tf_op jit(solution)/shard_map/ppermute | solution.py:412
  85.9 2.0 %collective-permute-done.5.refs_6_ = f32[1600,128]{1,0:T(8,128)S(1)} collective-permute-done((f32[1600,128]{1,0:T(8,128)S(1)}, f32[1600,128]{1,0:T(8,128)S(1)}, u32[]{:S(2)}, u32[]{:S(2)}) %collective-permute-start.5) | collective-permute-done | bytes 819232 | tf_op jit(solution)/shard_map/ppermute | solution.py:412
  87.9 12.0 %iterate2.1 = (f32[1600,128]{1,0:T(8,128)S(1)}, f32[1600,128]{1,0:T(8,128)S(1)}, f32[4096,128]{1,0:T(8,128)}, f32[8,128]{1,0:T(8,128)S(1)}) custom-call(s32[4096]{0:T(1024)S(1)} %reshape.82.refs_0_, s32[4096]{0:T(1024)S(1)} %reshape.84.refs_1_, s32[1]{0:T(128)} %bitcast.2.refs_2_, f32[1600,128]{1,0:T(8,128)S(1)} %bitcast.31, ...), custom_call_target="tpu_custom_call" | custom-call | tf_op jit(solution)/shard_map/iterate2/pallas_call | solution.py:321
  99.9 0.5 collective-permute-start.6
  100.4 2.0 %collective-permute-done.6 = f32[1600,128]{1,0:T(8,128)S(1)} collective-permute-done((f32[1600,128]{1,0:T(8,128)S(1)}, f32[1600,128]{1,0:T(8,128)S(1)}, u32[]{:S(2)}, u32[]{:S(2)}) %collective-permute-start.6) | collective-permute-done | bytes 819232 | tf_op jit(solution)/shard_map/ppermute | solution.py:412
  102.3 0.0 copy-start.2
  102.3 0.1 add.43
  102.4 16.8 %all_to_all.28 = f32[16,1,12800]{2,1,0:T(1,128)S(1)} all-to-all(f32[16,1,12800]{2,1,0:T(1,128)S(1)} %bitcast.47), channel_id=1, replica_groups={{0,2,4,6,8,10,12,14,16,18,20,22,24,26,28,30},{1,3,5,7,9,11,13,15,17,19,..., dimensions={0} | all-to-all | bytes 1638400 | tf_op jit(solution)/shard_map/all_to_all | solution.py:419
  119.3 0.6 collective-permute-start.9
  119.9 0.4 collective-permute-start.8
  120.3 0.8 collective-permute-start.7
  121.1 1.2 collective-permute-done.9.three
  122.3 2.1 %collective-permute-done.8.two = f32[100,128]{1,0:T(8,128)S(1)} collective-permute-done((f32[100,128]{1,0:T(8,128)S(1)}, f32[100,128]{1,0:T(8,128)S(1)}, u32[]{:S(2)}, u32[]{:S(2)}) %collective-permute-start.8) | collective-permute-done | bytes 51232 | tf_op jit(solution)/shard_map/ppermute | solution.py:430
  124.4 0.5 collective-permute-done.7.one
  125.0 0.1 last_gradient.1
  125.1 13.6 %all_to_all.29.parts = f32[32,1,128]{2,1,0:T(1,128)S(1)} all-to-all(f32[32,1,128]{2,1,0:T(1,128)S(1)} %get-tuple-element.21), channel_id=1, replica_groups=mesh['grp'=4,'shard'=32] {'shard'}, dimensions={0} | all-to-all | bytes 32768 | tf_op jit(solution)/shard_map/all_to_all | solution.py:458
  138.7 0.0 copy-done.2
  138.7 0.7 last_duals.1
  (6 shorter events, 0.1 us)
Async XLA Ops:
  0.6 24.5 %copy-start.3 = (s32[256,16]{0,1:T(8,128)S(1)}, s32[256,16]{0,1:T(8,128)}, u32[]{:S(2)}) copy-start(s32[256,16]{0,1:T(8,128)} %param.6) | copy-start | bytes 49156
  0.6 26.8 %copy-start.4 = (s32[256]{0:T(256)S(1)}, s32[256]{0:T(256)}, u32[]{:S(2)}) copy-start(s32[256]{0:T(256)} %param.9) | copy-start | bytes 3076
  0.7 0.8 copy-start.1
  23.4 4.1 %collective-permute-start = (f32[1600,128]{1,0:T(8,128)S(1)}, f32[1600,128]{1,0:T(8,128)S(1)}, u32[]{:S(2)}, u32[]{:S(2)}) collective-permute-start(f32[1600,128]{1,0:T(8,128)S(1)} %bitcast.29), channel_id=1, source_target_pairs={{0,1},{1,0},{2,3},{3,2},{4,5},{5,4},{6,7},{7,6},{8,9},{9,8},{10,11... | collective-permute-start | bytes 2457608 | tf_op jit(solution)/shard_map/ppermute | solution.py:412
  39.5 2.4 %collective-permute-start.1 = (f32[1600,128]{1,0:T(8,128)S(1)}, f32[1600,128]{1,0:T(8,128)S(1)}, u32[]{:S(2)}, u32[]{:S(2)}) collective-permute-start(f32[1600,128]{1,0:T(8,128)S(1)} %get-tuple-element.13), channel_id=1, source_target_pairs={{0,1},{1,0},{2,3},{3,2},{4,5},{5,4},{6,7},{7,6},{8,9},{9,8},{10,11... | collective-permute-start | bytes 2457608 | tf_op jit(solution)/shard_map/ppermute | solution.py:412
  41.9 24.9 %copy-start = (f32[12800]{0:T(1024)S(1)}, f32[12800]{0:T(1024)}, u32[]{:S(2)}) copy-start(f32[12800]{0:T(1024)} %param.10) | copy-start | bytes 153604
  58.9 4.0 %collective-permute-start.4 = (f32[100,128]{1,0:T(8,128)S(1)}, f32[100,128]{1,0:T(8,128)S(1)}, u32[]{:S(2)}, u32[]{:S(2)}) collective-permute-start(f32[100,128]{1,0:T(8,128)S(1)} %sum_chips.2.plane), channel_id=1, source_target_pairs={{0,96},{32,0},{64,32},{96,64},{1,97},{33,1},{65,33},{97,65},{2,98}... | collective-permute-start | bytes 153608 | tf_op jit(solution)/shard_map/ppermute | solution.py:430
  61.7 4.5 %collective-permute-start.3 = (f32[100,128]{1,0:T(8,128)S(1)}, f32[100,128]{1,0:T(8,128)S(1)}, u32[]{:S(2)}, u32[]{:S(2)}) collective-permute-start(f32[100,128]{1,0:T(8,128)S(1)} %sum_chips.2.plane), channel_id=1, source_target_pairs={{0,64},{32,96},{64,0},{96,32},{1,65},{33,97},{65,1},{97,33},{2,66}... | collective-permute-start | bytes 153608 | tf_op jit(solution)/shard_map/ppermute | solution.py:430
  62.1 4.7 %collective-permute-start.2 = (f32[100,128]{1,0:T(8,128)S(1)}, f32[100,128]{1,0:T(8,128)S(1)}, u32[]{:S(2)}, u32[]{:S(2)}) collective-permute-start(f32[100,128]{1,0:T(8,128)S(1)} %sum_chips.2.plane), channel_id=1, source_target_pairs={{0,32},{32,64},{64,96},{96,0},{1,33},{33,65},{65,97},{97,1},{2,34}... | collective-permute-start | bytes 153608 | tf_op jit(solution)/shard_map/ppermute | solution.py:430
  81.5 6.4 %collective-permute-start.5 = (f32[1600,128]{1,0:T(8,128)S(1)}, f32[1600,128]{1,0:T(8,128)S(1)}, u32[]{:S(2)}, u32[]{:S(2)}) collective-permute-start(f32[1600,128]{1,0:T(8,128)S(1)} %bitcast.35), channel_id=1, source_target_pairs={{0,1},{1,0},{2,3},{3,2},{4,5},{5,4},{6,7},{7,6},{8,9},{9,8},{10,11... | collective-permute-start | bytes 2457608 | tf_op jit(solution)/shard_map/ppermute | solution.py:412
  99.9 2.4 %collective-permute-start.6 = (f32[1600,128]{1,0:T(8,128)S(1)}, f32[1600,128]{1,0:T(8,128)S(1)}, u32[]{:S(2)}, u32[]{:S(2)}) collective-permute-start(f32[1600,128]{1,0:T(8,128)S(1)} %get-tuple-element.19), channel_id=1, source_target_pairs={{0,1},{1,0},{2,3},{3,2},{4,5},{5,4},{6,7},{7,6},{8,9},{9,8},{10,11... | collective-permute-start | bytes 2457608 | tf_op jit(solution)/shard_map/ppermute | solution.py:412
  102.3 36.4 %copy-start.2 = (f32[12800]{0:T(1024)S(1)}, f32[12800]{0:T(1024)}, u32[]{:S(2)}) copy-start(f32[12800]{0:T(1024)} %param.11) | copy-start | bytes 153604
  119.3 3.1 %collective-permute-start.9 = (f32[100,128]{1,0:T(8,128)S(1)}, f32[100,128]{1,0:T(8,128)S(1)}, u32[]{:S(2)}, u32[]{:S(2)}) collective-permute-start(f32[100,128]{1,0:T(8,128)S(1)} %sum_chips.3.plane), channel_id=1, source_target_pairs={{0,96},{32,0},{64,32},{96,64},{1,97},{33,1},{65,33},{97,65},{2,98}... | collective-permute-start | bytes 153608 | tf_op jit(solution)/shard_map/ppermute | solution.py:430
  119.9 4.5 %collective-permute-start.8 = (f32[100,128]{1,0:T(8,128)S(1)}, f32[100,128]{1,0:T(8,128)S(1)}, u32[]{:S(2)}, u32[]{:S(2)}) collective-permute-start(f32[100,128]{1,0:T(8,128)S(1)} %sum_chips.3.plane), channel_id=1, source_target_pairs={{0,64},{32,96},{64,0},{96,32},{1,65},{33,97},{65,1},{97,33},{2,66}... | collective-permute-start | bytes 153608 | tf_op jit(solution)/shard_map/ppermute | solution.py:430
  120.3 4.6 %collective-permute-start.7 = (f32[100,128]{1,0:T(8,128)S(1)}, f32[100,128]{1,0:T(8,128)S(1)}, u32[]{:S(2)}, u32[]{:S(2)}) collective-permute-start(f32[100,128]{1,0:T(8,128)S(1)} %sum_chips.3.plane), channel_id=1, source_target_pairs={{0,32},{32,64},{64,96},{96,0},{1,33},{33,65},{65,97},{97,1},{2,34}... | collective-permute-start | bytes 153608 | tf_op jit(solution)/shard_map/ppermute | solution.py:430

commit v6 on v5

--- a/solution.py
+++ b/solution.py
@@ -82,7 +82,7 @@
 
         n = ncopy[0]
         fits = n <= COPIES
-        used = jnp.where(fits, n, 1)
+        used = jnp.where(fits, jnp.maximum(n, 2), 2)
         zero = jnp.zeros((SUB, BLOCK), f32)
         dead = jnp.full((SUB, BLOCK), DEAD, f32)
         vregs = full // SUB
@@ -258,7 +258,9 @@
         def finish(i, c):
             r = pl.multiple_of(i * SUB, SUB)
             for out, o in ((keep, 0), (send, half)):
-                out[pl.ds(r, SUB), :] = acc_even[pl.ds(r + o, SUB), :] + acc_odd[pl.ds(r + o, SUB), :]
+                out[pl.ds(r, SUB), :] = (
+                    (acc_even[pl.ds(r + o, SUB), :] + acc_odd[pl.ds(r + o, SUB), :])
+                    + (acc_even[pl.ds(r + (full + o), SUB), :] + acc_odd[pl.ds(r + (full + o), SUB), :]))
             return c
 
         lax.fori_loop(0, half // SUB, finish, 0, unroll=8)
@@ -273,7 +275,7 @@
 
             return lax.fori_loop(0, half // SUB, more, c, unroll=8)
 
-        lax.fori_loop(1, used, finish_copy, 0)
+        lax.fori_loop(2, used, finish_copy, 0)
         if second:
             for store in stores:
                 store.wait()
@@ -358,15 +360,15 @@
 
 
 def gradient_of(plane, shifted, limit):
-    one, two, three = shifted
+    one, three, two = shifted
     return ((plane[...] + two[...]) + (one[...] + three[...])) - limit[...]
 
 
 def spread_gradient(plane, shifted, limit, chips):
     own_rows = plane.shape[0]
 
-    def body(plane, one, two, three, limit, gradient, every):
-        g = gradient_of(plane, (one, two, three), limit)
+    def body(plane, one, three, two, limit, gradient, every):
+        g = gradient_of(plane, (one, three, two), limit)
         gradient[...] = g
         for p in range(chips):
             every[pl.ds(p * own_rows, own_rows), :] = g
@@ -375,8 +377,8 @@
 
 
 def last_gradient(plane, shifted, limit, shards):
-    def body(plane, one, two, three, limit, gradient, parts):
-        g = gradient_of(plane, (one, two, three), limit)
+    def body(plane, one, three, two, limit, gradient, parts):
+        g = gradient_of(plane, (one, three, two), limit)
         gradient[...] = g
         part = jnp.sum(jnp.sum(g * g, axis=0, keepdims=True), axis=1, keepdims=True)
         parts[...] = jnp.broadcast_to(part[None], parts.shape)
@@ -428,7 +430,7 @@
         plane = sum_chips(exchange(chip), chips)
         return plane, [
             lax.ppermute(plane, "grp", [(g, (g + d) % grp_size) for g in range(grp_size)])
-            for d in range(1, grp_size)
+            for d in (1, 3, 2)
         ]
 
     shard_of = candidates // own_rows

time: 140 us -> 141 us (level)
  transfers between devices with their start and end apart: 10 -> 10, of which waited for: 9 -> 8; matrix products, arithmetic and copies ran while one was open for 1% -> 1% of each run, Pallas kernels for 0% -> 0%
where the time goes in v6:
time: 141 us; the launch traced here: 140 us
  blocking collectives  83.4 us (59%)
  Pallas kernels  24.5 us (17%)
  waiting for transfers between devices  14.4 us (10%)
  starting transfers between devices  13.8 us (10%)
  local copies, waits for them, and re-layouts  1.67 us (1%)
  between operations  1.43 us (1%)
    all_to_all x4, blocking collectives, exchange(): lax.all_to_all(x, 'shard', 0, 0, axis_index_groups=same_core, tiled=True)  70 us
    pallas_call x2, Pallas kernels, run(): return call(gidx, sidx, ncopy, *tables, aff, exp, nlive)  23.5 us
    all_to_all x1, blocking collectives, local(): parts = lax.all_to_all(parts, 'shard', 0, 0, tiled=True)  13.3 us
    ppermute x6, waiting for transfers between devices, reduce_loads(): lax.ppermute(plane, 'grp', [(g, (g + d) % grp_size) for g in range(grp_si...  8.27 us
    ppermute x4, starting transfers between devices, swap_cores(): return lax.ppermute(x, AXES, swap)  7.01 us
    ppermute x6, starting transfers between devices, reduce_loads(): lax.ppermute(plane, 'grp', [(g, (g + d) % grp_size) for g in range(grp_si...  6.82 us
    ppermute x4, waiting for transfers between devices, swap_cores(): return lax.ppermute(x, AXES, swap)  6.18 us
  transfers between devices with their start and end apart: 10, of which 8 were waited for; matrix products, arithmetic and copies ran while one was open for 1% of the time, Pallas kernels for 0%

profile of v6, /device:TPU:1, one launch (start us, length us, event | category | flops | bytes accessed | tf_op | source)
XLA Modules:
  0.0 140.3 jit_solution(15348510611202778280)
XLA Ops:
  0.6 0.0 copy-start.3
  0.6 0.0 copy-start.4
  0.7 0.0 copy-start.1
  0.7 0.8 copy-done.1
  1.5 0.1 spread_duals.1
  1.5 21.8 %all_to_all.25 = f32[16,1,12800]{2,1,0:T(1,128)S(1)} all-to-all(f32[16,1,12800]{2,1,0:T(1,128)S(1)} %bitcast.32), channel_id=1, replica_groups={{0,2,4,6,8,10,12,14,16,18,20,22,24,26,28,30},{1,3,5,7,9,11,13,15,17,19,..., dimensions={0} | all-to-all | bytes 1638400 | tf_op jit(solution)/shard_map/all_to_all | solution.py:421
  23.4 1.8 %collective-permute-start = (f32[1600,128]{1,0:T(8,128)S(1)}, f32[1600,128]{1,0:T(8,128)S(1)}, u32[]{:S(2)}, u32[]{:S(2)}) collective-permute-start(f32[1600,128]{1,0:T(8,128)S(1)} %bitcast.29), channel_id=1, source_target_pairs={{0,1},{1,0},{2,3},{3,2},{4,5},{5,4},{6,7},{7,6},{8,9},{9,8},{10,11... | collective-permute-start | bytes 2457608 | tf_op jit(solution)/shard_map/ppermute | solution.py:414
  25.2 0.0 copy-done.3
  25.2 0.1 copy.26
  25.3 0.1 convert_reduce_fusion
  25.5 0.6 fusion.7
  26.7 0.1 copy.28
  26.8 0.1 reshape.83
  27.0 0.1 copy.29
  27.1 0.1 reshape.84.refs_1_
  27.1 0.1 reshape_reshape.3
  27.2 0.1 copy.27
  27.3 0.1 reshape.82.refs_0_
  27.4 0.0 copy-done.4
  27.4 0.0 collective-permute-done.refs_4_
  27.5 0.1 broadcast_in_dim.20.refs_7_.refs_9_
  27.6 11.7 %iterate1.1 = (f32[1600,128]{1,0:T(8,128)S(1)}, f32[1600,128]{1,0:T(8,128)S(1)}) custom-call(s32[4096]{0:T(1024)S(1)} %reshape.82.refs_0_, s32[4096]{0:T(1024)S(1)} %reshape.84.refs_1_, s32[1]{0:T(128)} %bitcast.2.refs_2_, f32[1600,128]{1,0:T(8,128)S(1)} %bitcast.30, f32[1600,128]{1,0:T(8,128)S(1)} %collective-permute-done.refs_4_, f32[4096,128]{1,0:T(8,128)} %bitcast.42, ...), custom_call_target="tpu_custom_call" | custom-call | tf_op jit(solution)/shard_map/iterate1/pallas_call | solution.py:323
  39.3 0.2 collective-permute-start.1
  39.4 2.3 %collective-permute-done.1 = f32[1600,128]{1,0:T(8,128)S(1)} collective-permute-done((f32[1600,128]{1,0:T(8,128)S(1)}, f32[1600,128]{1,0:T(8,128)S(1)}, u32[]{:S(2)}, u32[]{:S(2)}) %collective-permute-start.1) | collective-permute-done | bytes 819232 | tf_op jit(solution)/shard_map/ppermute | solution.py:414
  41.7 0.0 copy-start
  41.7 0.1 add.42
  41.8 16.9 %all_to_all.26 = f32[16,1,12800]{2,1,0:T(1,128)S(1)} all-to-all(f32[16,1,12800]{2,1,0:T(1,128)S(1)} %bitcast.46), channel_id=1, replica_groups={{0,2,4,6,8,10,12,14,16,18,20,22,24,26,28,30},{1,3,5,7,9,11,13,15,17,19,..., dimensions={0} | all-to-all | bytes 1638400 | tf_op jit(solution)/shard_map/all_to_all | solution.py:421
  58.7 3.0 %collective-permute-start.4 = (f32[100,128]{1,0:T(8,128)S(1)}, f32[100,128]{1,0:T(8,128)S(1)}, u32[]{:S(2)}, u32[]{:S(2)}) collective-permute-start(f32[100,128]{1,0:T(8,128)S(1)} %sum_chips.2.plane), channel_id=1, source_target_pairs={{0,64},{32,96},{64,0},{96,32},{1,65},{33,97},{65,1},{97,33},{2,66}... | collective-permute-start | bytes 153608 | tf_op jit(solution)/shard_map/ppermute | solution.py:432
  61.7 0.8 collective-permute-start.3
  62.5 0.7 collective-permute-start.2
  63.2 0.1 collective-permute-done.4.two
  63.3 1.4 collective-permute-done.3.three
  64.7 2.0 %collective-permute-done.2.one = f32[100,128]{1,0:T(8,128)S(1)} collective-permute-done((f32[100,128]{1,0:T(8,128)S(1)}, f32[100,128]{1,0:T(8,128)S(1)}, u32[]{:S(2)}, u32[]{:S(2)}) %collective-permute-start.2) | collective-permute-done | bytes 51232 | tf_op jit(solution)/shard_map/ppermute | solution.py:432
  66.7 0.0 copy-done
  66.7 0.1 spread_gradient.1
  66.8 14.5 %all_to_all.27 = f32[16,1,12800]{2,1,0:T(1,128)S(1)} all-to-all(f32[16,1,12800]{2,1,0:T(1,128)S(1)} %bitcast.37), channel_id=1, replica_groups={{0,2,4,6,8,10,12,14,16,18,20,22,24,26,28,30},{1,3,5,7,9,11,13,15,17,19,..., dimensions={0} | all-to-all | bytes 1638400 | tf_op jit(solution)/shard_map/all_to_all | solution.py:421
  81.3 4.6 %collective-permute-start.5 = (f32[1600,128]{1,0:T(8,128)S(1)}, f32[1600,128]{1,0:T(8,128)S(1)}, u32[]{:S(2)}, u32[]{:S(2)}) collective-permute-start(f32[1600,128]{1,0:T(8,128)S(1)} %bitcast.35), channel_id=1, source_target_pairs={{0,1},{1,0},{2,3},{3,2},{4,5},{5,4},{6,7},{7,6},{8,9},{9,8},{10,11... | collective-permute-start | bytes 2457608 | tf_op jit(solution)/shard_map/ppermute | solution.py:414
  85.8 2.0 %collective-permute-done.5.refs_6_ = f32[1600,128]{1,0:T(8,128)S(1)} collective-permute-done((f32[1600,128]{1,0:T(8,128)S(1)}, f32[1600,128]{1,0:T(8,128)S(1)}, u32[]{:S(2)}, u32[]{:S(2)}) %collective-permute-start.5) | collective-permute-done | bytes 819232 | tf_op jit(solution)/shard_map/ppermute | solution.py:414
  87.8 11.8 %iterate2.1 = (f32[1600,128]{1,0:T(8,128)S(1)}, f32[1600,128]{1,0:T(8,128)S(1)}, f32[4096,128]{1,0:T(8,128)}, f32[8,128]{1,0:T(8,128)S(1)}) custom-call(s32[4096]{0:T(1024)S(1)} %reshape.82.refs_0_, s32[4096]{0:T(1024)S(1)} %reshape.84.refs_1_, s32[1]{0:T(128)} %bitcast.2.refs_2_, f32[1600,128]{1,0:T(8,128)S(1)} %bitcast.31, ...), custom_call_target="tpu_custom_call" | custom-call | tf_op jit(solution)/shard_map/iterate2/pallas_call | solution.py:323
  99.6 0.5 collective-permute-start.6
  100.1 2.0 %collective-permute-done.6 = f32[1600,128]{1,0:T(8,128)S(1)} collective-permute-done((f32[1600,128]{1,0:T(8,128)S(1)}, f32[1600,128]{1,0:T(8,128)S(1)}, u32[]{:S(2)}, u32[]{:S(2)}) %collective-permute-start.6) | collective-permute-done | bytes 819232 | tf_op jit(solution)/shard_map/ppermute | solution.py:414
  102.0 0.0 copy-start.2
  102.0 0.1 add.43
  102.1 16.8 %all_to_all.28 = f32[16,1,12800]{2,1,0:T(1,128)S(1)} all-to-all(f32[16,1,12800]{2,1,0:T(1,128)S(1)} %bitcast.47), channel_id=1, replica_groups={{0,2,4,6,8,10,12,14,16,18,20,22,24,26,28,30},{1,3,5,7,9,11,13,15,17,19,..., dimensions={0} | all-to-all | bytes 1638400 | tf_op jit(solution)/shard_map/all_to_all | solution.py:421
  119.0 0.3 collective-permute-start.9
  119.3 2.1 %collective-permute-start.8 = (f32[100,128]{1,0:T(8,128)S(1)}, f32[100,128]{1,0:T(8,128)S(1)}, u32[]{:S(2)}, u32[]{:S(2)}) collective-permute-start(f32[100,128]{1,0:T(8,128)S(1)} %sum_chips.3.plane), channel_id=1, source_target_pairs={{0,96},{32,0},{64,32},{96,64},{1,97},{33,1},{65,33},{97,65},{2,98}... | collective-permute-start | bytes 153608 | tf_op jit(solution)/shard_map/ppermute | solution.py:432
  121.4 0.0 collective-permute-start.7
  121.4 2.2 %collective-permute-done.9.two = f32[100,128]{1,0:T(8,128)S(1)} collective-permute-done((f32[100,128]{1,0:T(8,128)S(1)}, f32[100,128]{1,0:T(8,128)S(1)}, u32[]{:S(2)}, u32[]{:S(2)}) %collective-permute-start.9) | collective-permute-done | bytes 51232 | tf_op jit(solution)/shard_map/ppermute | solution.py:432
  123.6 0.0 collective-permute-done.8.three
  123.6 2.6 %collective-permute-done.7.one = f32[100,128]{1,0:T(8,128)S(1)} collective-permute-done((f32[100,128]{1,0:T(8,128)S(1)}, f32[100,128]{1,0:T(8,128)S(1)}, u32[]{:S(2)}, u32[]{:S(2)}) %collective-permute-start.7) | collective-permute-done | bytes 51232 | tf_op jit(solution)/shard_map/ppermute | solution.py:432
  126.1 0.1 last_gradient.1
  126.3 13.3 %all_to_all.29.parts = f32[32,1,128]{2,1,0:T(1,128)S(1)} all-to-all(f32[32,1,128]{2,1,0:T(1,128)S(1)} %get-tuple-element.21), channel_id=1, replica_groups=mesh['grp'=4,'shard'=32] {'shard'}, dimensions={0} | all-to-all | bytes 32768 | tf_op jit(solution)/shard_map/all_to_all | solution.py:460
  139.6 0.0 copy-done.2
  139.6 0.7 last_duals.1
  (6 shorter events, 0.1 us)
Async XLA Ops:
  0.6 24.5 %copy-start.3 = (s32[256,16]{0,1:T(8,128)S(1)}, s32[256,16]{0,1:T(8,128)}, u32[]{:S(2)}) copy-start(s32[256,16]{0,1:T(8,128)} %param.6) | copy-start | bytes 49156
  0.6 26.8 %copy-start.4 = (s32[256]{0:T(256)S(1)}, s32[256]{0:T(256)}, u32[]{:S(2)}) copy-start(s32[256]{0:T(256)} %param.9) | copy-start | bytes 3076
  0.7 0.8 copy-start.1
  23.4 4.1 %collective-permute-start = (f32[1600,128]{1,0:T(8,128)S(1)}, f32[1600,128]{1,0:T(8,128)S(1)}, u32[]{:S(2)}, u32[]{:S(2)}) collective-permute-start(f32[1600,128]{1,0:T(8,128)S(1)} %bitcast.29), channel_id=1, source_target_pairs={{0,1},{1,0},{2,3},{3,2},{4,5},{5,4},{6,7},{7,6},{8,9},{9,8},{10,11... | collective-permute-start | bytes 2457608 | tf_op jit(solution)/shard_map/ppermute | solution.py:414
  39.3 2.4 %collective-permute-start.1 = (f32[1600,128]{1,0:T(8,128)S(1)}, f32[1600,128]{1,0:T(8,128)S(1)}, u32[]{:S(2)}, u32[]{:S(2)}) collective-permute-start(f32[1600,128]{1,0:T(8,128)S(1)} %get-tuple-element.13), channel_id=1, source_target_pairs={{0,1},{1,0},{2,3},{3,2},{4,5},{5,4},{6,7},{7,6},{8,9},{9,8},{10,11... | collective-permute-start | bytes 2457608 | tf_op jit(solution)/shard_map/ppermute | solution.py:414
  41.7 25.0 %copy-start = (f32[12800]{0:T(1024)S(1)}, f32[12800]{0:T(1024)}, u32[]{:S(2)}) copy-start(f32[12800]{0:T(1024)} %param.10) | copy-start | bytes 153604
  58.7 4.6 %collective-permute-start.4 = (f32[100,128]{1,0:T(8,128)S(1)}, f32[100,128]{1,0:T(8,128)S(1)}, u32[]{:S(2)}, u32[]{:S(2)}) collective-permute-start(f32[100,128]{1,0:T(8,128)S(1)} %sum_chips.2.plane), channel_id=1, source_target_pairs={{0,64},{32,96},{64,0},{96,32},{1,65},{33,97},{65,1},{97,33},{2,66}... | collective-permute-start | bytes 153608 | tf_op jit(solution)/shard_map/ppermute | solution.py:432
  61.7 3.0 %collective-permute-start.3 = (f32[100,128]{1,0:T(8,128)S(1)}, f32[100,128]{1,0:T(8,128)S(1)}, u32[]{:S(2)}, u32[]{:S(2)}) collective-permute-start(f32[100,128]{1,0:T(8,128)S(1)} %sum_chips.2.plane), channel_id=1, source_target_pairs={{0,96},{32,0},{64,32},{96,64},{1,97},{33,1},{65,33},{97,65},{2,98}... | collective-permute-start | bytes 153608 | tf_op jit(solution)/shard_map/ppermute | solution.py:432
  62.5 4.2 %collective-permute-start.2 = (f32[100,128]{1,0:T(8,128)S(1)}, f32[100,128]{1,0:T(8,128)S(1)}, u32[]{:S(2)}, u32[]{:S(2)}) collective-permute-start(f32[100,128]{1,0:T(8,128)S(1)} %sum_chips.2.plane), channel_id=1, source_target_pairs={{0,32},{32,64},{64,96},{96,0},{1,33},{33,65},{65,97},{97,1},{2,34}... | collective-permute-start | bytes 153608 | tf_op jit(solution)/shard_map/ppermute | solution.py:432
  81.3 6.5 %collective-permute-start.5 = (f32[1600,128]{1,0:T(8,128)S(1)}, f32[1600,128]{1,0:T(8,128)S(1)}, u32[]{:S(2)}, u32[]{:S(2)}) collective-permute-start(f32[1600,128]{1,0:T(8,128)S(1)} %bitcast.35), channel_id=1, source_target_pairs={{0,1},{1,0},{2,3},{3,2},{4,5},{5,4},{6,7},{7,6},{8,9},{9,8},{10,11... | collective-permute-start | bytes 2457608 | tf_op jit(solution)/shard_map/ppermute | solution.py:414
  99.6 2.4 %collective-permute-start.6 = (f32[1600,128]{1,0:T(8,128)S(1)}, f32[1600,128]{1,0:T(8,128)S(1)}, u32[]{:S(2)}, u32[]{:S(2)}) collective-permute-start(f32[1600,128]{1,0:T(8,128)S(1)} %get-tuple-element.19), channel_id=1, source_target_pairs={{0,1},{1,0},{2,3},{3,2},{4,5},{5,4},{6,7},{7,6},{8,9},{9,8},{10,11... | collective-permute-start | bytes 2457608 | tf_op jit(solution)/shard_map/ppermute | solution.py:414
  102.0 37.6 %copy-start.2 = (f32[12800]{0:T(1024)S(1)}, f32[12800]{0:T(1024)}, u32[]{:S(2)}) copy-start(f32[12800]{0:T(1024)} %param.11) | copy-start | bytes 153604
  119.0 4.6 %collective-permute-start.9 = (f32[100,128]{1,0:T(8,128)S(1)}, f32[100,128]{1,0:T(8,128)S(1)}, u32[]{:S(2)}, u32[]{:S(2)}) collective-permute-start(f32[100,128]{1,0:T(8,128)S(1)} %sum_chips.3.plane), channel_id=1, source_target_pairs={{0,64},{32,96},{64,0},{96,32},{1,65},{33,97},{65,1},{97,33},{2,66}... | collective-permute-start | bytes 153608 | tf_op jit(solution)/shard_map/ppermute | solution.py:432
  119.3 4.3 %collective-permute-start.8 = (f32[100,128]{1,0:T(8,128)S(1)}, f32[100,128]{1,0:T(8,128)S(1)}, u32[]{:S(2)}, u32[]{:S(2)}) collective-permute-start(f32[100,128]{1,0:T(8,128)S(1)} %sum_chips.3.plane), channel_id=1, source_target_pairs={{0,96},{32,0},{64,32},{96,64},{1,97},{33,1},{65,33},{97,65},{2,98}... | collective-permute-start | bytes 153608 | tf_op jit(solution)/shard_map/ppermute | solution.py:432
  121.4 4.8 %collective-permute-start.7 = (f32[100,128]{1,0:T(8,128)S(1)}, f32[100,128]{1,0:T(8,128)S(1)}, u32[]{:S(2)}, u32[]{:S(2)}) collective-permute-start(f32[100,128]{1,0:T(8,128)S(1)} %sum_chips.3.plane), channel_id=1, source_target_pairs={{0,32},{32,64},{64,96},{96,0},{1,33},{33,65},{65,97},{97,1},{2,34}... | collective-permute-start | bytes 153608 | tf_op jit(solution)/shard_map/ppermute | solution.py:432

commit v7 on v5

--- a/solution.py
+++ b/solution.py
@@ -82,7 +82,7 @@
 
         n = ncopy[0]
         fits = n <= COPIES
-        used = jnp.where(fits, n, 1)
+        used = jnp.where(fits, jnp.maximum(n, 2), 2)
         zero = jnp.zeros((SUB, BLOCK), f32)
         dead = jnp.full((SUB, BLOCK), DEAD, f32)
         vregs = full // SUB
@@ -258,7 +258,9 @@
         def finish(i, c):
             r = pl.multiple_of(i * SUB, SUB)
             for out, o in ((keep, 0), (send, half)):
-                out[pl.ds(r, SUB), :] = acc_even[pl.ds(r + o, SUB), :] + acc_odd[pl.ds(r + o, SUB), :]
+                out[pl.ds(r, SUB), :] = (
+                    (acc_even[pl.ds(r + o, SUB), :] + acc_odd[pl.ds(r + o, SUB), :])
+                    + (acc_even[pl.ds(r + (full + o), SUB), :] + acc_odd[pl.ds(r + (full + o), SUB), :]))
             return c
 
         lax.fori_loop(0, half // SUB, finish, 0, unroll=8)
@@ -273,7 +275,7 @@
 
             return lax.fori_loop(0, half // SUB, more, c, unroll=8)
 
-        lax.fori_loop(1, used, finish_copy, 0)
+        lax.fori_loop(2, used, finish_copy, 0)
         if second:
             for store in stores:
                 store.wait()

time: 140 us -> 139 us (level)
  no operation moved by 1% of the time
where the time goes in v7:
time: 139 us
  blocking collectives  83.7 us (60%)
  Pallas kernels  24.6 us (18%)
  waiting for transfers between devices  14.1 us (10%)
  starting transfers between devices  12.5 us (9%)
  local copies, waits for them, and re-layouts  1.67 us (1%)
  between operations  1.43 us (1%)
    all_to_all x4, blocking collectives, exchange(): lax.all_to_all(x, 'shard', 0, 0, axis_index_groups=same_core, tiled=True)  70.1 us
    pallas_call x2, Pallas kernels, run(): return call(gidx, sidx, ncopy, *tables, aff, exp, nlive)  23.6 us
    all_to_all x1, blocking collectives, local(): parts = lax.all_to_all(parts, 'shard', 0, 0, tiled=True)  13.6 us
    ppermute x6, waiting for transfers between devices, reduce_loads(): lax.ppermute(plane, 'grp', [(g, (g + d) % grp_size) for g in range(grp_si...  7.9 us
    ppermute x4, starting transfers between devices, swap_cores(): return lax.ppermute(x, AXES, swap)  6.82 us
    ppermute x4, waiting for transfers between devices, swap_cores(): return lax.ppermute(x, AXES, swap)  6.22 us
    ppermute x6, starting transfers between devices, reduce_loads(): lax.ppermute(plane, 'grp', [(g, (g + d) % grp_size) for g in range(grp_si...  5.67 us
  transfers between devices with their start and end apart: 10, of which 9 were waited for; matrix products, arithmetic and copies ran while one was open for 1% of the time, Pallas kernels for 0%

profile of v7, /device:TPU:1, one launch (start us, length us, event | category | flops | bytes accessed | tf_op | source)
XLA Modules:
  0.0 139.0 jit_solution(9359590239687578613)
XLA Ops:
  0.6 0.0 copy-start.3
  0.6 0.0 copy-start.4
  0.7 0.0 copy-start.1
  0.7 0.8 copy-done.1
  1.5 0.1 spread_duals.1
  1.5 21.8 %all_to_all.25 = f32[16,1,12800]{2,1,0:T(1,128)S(1)} all-to-all(f32[16,1,12800]{2,1,0:T(1,128)S(1)} %bitcast.32), channel_id=1, replica_groups={{0,2,4,6,8,10,12,14,16,18,20,22,24,26,28,30},{1,3,5,7,9,11,13,15,17,19,..., dimensions={0} | all-to-all | bytes 1638400 | tf_op jit(solution)/shard_map/all_to_all | solution.py:421
  23.4 1.8 %collective-permute-start = (f32[1600,128]{1,0:T(8,128)S(1)}, f32[1600,128]{1,0:T(8,128)S(1)}, u32[]{:S(2)}, u32[]{:S(2)}) collective-permute-start(f32[1600,128]{1,0:T(8,128)S(1)} %bitcast.29), channel_id=1, source_target_pairs={{0,1},{1,0},{2,3},{3,2},{4,5},{5,4},{6,7},{7,6},{8,9},{9,8},{10,11... | collective-permute-start | bytes 2457608 | tf_op jit(solution)/shard_map/ppermute | solution.py:414
  25.2 0.0 copy-done.3
  25.2 0.1 copy.26
  25.3 0.1 convert_reduce_fusion
  25.5 0.6 fusion.7
  26.7 0.1 copy.28
  26.8 0.1 reshape.83
  27.0 0.1 copy.29
  27.1 0.1 reshape.84.refs_1_
  27.1 0.1 reshape_reshape.3
  27.2 0.1 copy.27
  27.3 0.1 reshape.82.refs_0_
  27.4 0.0 copy-done.4
  27.4 0.0 collective-permute-done.refs_4_
  27.5 0.1 broadcast_in_dim.20.refs_7_.refs_9_
  27.6 11.7 %iterate1.1 = (f32[1600,128]{1,0:T(8,128)S(1)}, f32[1600,128]{1,0:T(8,128)S(1)}) custom-call(s32[4096]{0:T(1024)S(1)} %reshape.82.refs_0_, s32[4096]{0:T(1024)S(1)} %reshape.84.refs_1_, s32[1]{0:T(128)} %bitcast.2.refs_2_, f32[1600,128]{1,0:T(8,128)S(1)} %bitcast.30, f32[1600,128]{1,0:T(8,128)S(1)} %collective-permute-done.refs_4_, f32[4096,128]{1,0:T(8,128)} %bitcast.42, ...), custom_call_target="tpu_custom_call" | custom-call | tf_op jit(solution)/shard_map/iterate1/pallas_call | solution.py:323
  39.3 0.1 collective-permute-start.1
  39.4 2.3 %collective-permute-done.1 = f32[1600,128]{1,0:T(8,128)S(1)} collective-permute-done((f32[1600,128]{1,0:T(8,128)S(1)}, f32[1600,128]{1,0:T(8,128)S(1)}, u32[]{:S(2)}, u32[]{:S(2)}) %collective-permute-start.1) | collective-permute-done | bytes 819232 | tf_op jit(solution)/shard_map/ppermute | solution.py:414
  41.7 0.0 copy-start
  41.7 0.1 add.42
  41.8 16.9 %all_to_all.26 = f32[16,1,12800]{2,1,0:T(1,128)S(1)} all-to-all(f32[16,1,12800]{2,1,0:T(1,128)S(1)} %bitcast.46), channel_id=1, replica_groups={{0,2,4,6,8,10,12,14,16,18,20,22,24,26,28,30},{1,3,5,7,9,11,13,15,17,19,..., dimensions={0} | all-to-all | bytes 1638400 | tf_op jit(solution)/shard_map/all_to_all | solution.py:421
  58.7 2.8 %collective-permute-start.4 = (f32[100,128]{1,0:T(8,128)S(1)}, f32[100,128]{1,0:T(8,128)S(1)}, u32[]{:S(2)}, u32[]{:S(2)}) collective-permute-start(f32[100,128]{1,0:T(8,128)S(1)} %sum_chips.2.plane), channel_id=1, source_target_pairs={{0,96},{32,0},{64,32},{96,64},{1,97},{33,1},{65,33},{97,65},{2,98}... | collective-permute-start | bytes 153608 | tf_op jit(solution)/shard_map/ppermute | solution.py:432
  61.5 0.4 collective-permute-start.3
  61.9 0.7 collective-permute-start.2
  62.6 0.2 collective-permute-done.4.three
  62.7 3.3 %collective-permute-done.3.two = f32[100,128]{1,0:T(8,128)S(1)} collective-permute-done((f32[100,128]{1,0:T(8,128)S(1)}, f32[100,128]{1,0:T(8,128)S(1)}, u32[]{:S(2)}, u32[]{:S(2)}) %collective-permute-start.3) | collective-permute-done | bytes 51232 | tf_op jit(solution)/shard_map/ppermute | solution.py:432
  66.1 0.5 collective-permute-done.2.one
  66.6 0.0 copy-done
  66.6 0.1 spread_gradient.1
  66.7 14.6 %all_to_all.27 = f32[16,1,12800]{2,1,0:T(1,128)S(1)} all-to-all(f32[16,1,12800]{2,1,0:T(1,128)S(1)} %bitcast.37), channel_id=1, replica_groups={{0,2,4,6,8,10,12,14,16,18,20,22,24,26,28,30},{1,3,5,7,9,11,13,15,17,19,..., dimensions={0} | all-to-all | bytes 1638400 | tf_op jit(solution)/shard_map/all_to_all | solution.py:421
  81.3 4.4 %collective-permute-start.5 = (f32[1600,128]{1,0:T(8,128)S(1)}, f32[1600,128]{1,0:T(8,128)S(1)}, u32[]{:S(2)}, u32[]{:S(2)}) collective-permute-start(f32[1600,128]{1,0:T(8,128)S(1)} %bitcast.35), channel_id=1, source_target_pairs={{0,1},{1,0},{2,3},{3,2},{4,5},{5,4},{6,7},{7,6},{8,9},{9,8},{10,11... | collective-permute-start | bytes 2457608 | tf_op jit(solution)/shard_map/ppermute | solution.py:414
  85.7 2.0 %collective-permute-done.5.refs_6_ = f32[1600,128]{1,0:T(8,128)S(1)} collective-permute-done((f32[1600,128]{1,0:T(8,128)S(1)}, f32[1600,128]{1,0:T(8,128)S(1)}, u32[]{:S(2)}, u32[]{:S(2)}) %collective-permute-start.5) | collective-permute-done | bytes 819232 | tf_op jit(solution)/shard_map/ppermute | solution.py:414
  87.7 11.8 %iterate2.1 = (f32[1600,128]{1,0:T(8,128)S(1)}, f32[1600,128]{1,0:T(8,128)S(1)}, f32[4096,128]{1,0:T(8,128)}, f32[8,128]{1,0:T(8,128)S(1)}) custom-call(s32[4096]{0:T(1024)S(1)} %reshape.82.refs_0_, s32[4096]{0:T(1024)S(1)} %reshape.84.refs_1_, s32[1]{0:T(128)} %bitcast.2.refs_2_, f32[1600,128]{1,0:T(8,128)S(1)} %bitcast.31, ...), custom_call_target="tpu_custom_call" | custom-call | tf_op jit(solution)/shard_map/iterate2/pallas_call | solution.py:323
  99.5 0.5 collective-permute-start.6
  100.0 2.0 %collective-permute-done.6 = f32[1600,128]{1,0:T(8,128)S(1)} collective-permute-done((f32[1600,128]{1,0:T(8,128)S(1)}, f32[1600,128]{1,0:T(8,128)S(1)}, u32[]{:S(2)}, u32[]{:S(2)}) %collective-permute-start.6) | collective-permute-done | bytes 819232 | tf_op jit(solution)/shard_map/ppermute | solution.py:414
  101.9 0.0 copy-start.2
  101.9 0.1 add.43
  102.0 16.8 %all_to_all.28 = f32[16,1,12800]{2,1,0:T(1,128)S(1)} all-to-all(f32[16,1,12800]{2,1,0:T(1,128)S(1)} %bitcast.47), channel_id=1, replica_groups={{0,2,4,6,8,10,12,14,16,18,20,22,24,26,28,30},{1,3,5,7,9,11,13,15,17,19,..., dimensions={0} | all-to-all | bytes 1638400 | tf_op jit(solution)/shard_map/all_to_all | solution.py:421
  118.9 0.7 collective-permute-start.9
  119.5 0.4 collective-permute-start.8
  120.0 0.8 collective-permute-start.7
  120.7 1.2 collective-permute-done.9.three
  121.9 2.1 %collective-permute-done.8.two = f32[100,128]{1,0:T(8,128)S(1)} collective-permute-done((f32[100,128]{1,0:T(8,128)S(1)}, f32[100,128]{1,0:T(8,128)S(1)}, u32[]{:S(2)}, u32[]{:S(2)}) %collective-permute-start.8) | collective-permute-done | bytes 51232 | tf_op jit(solution)/shard_map/ppermute | solution.py:432
  124.1 0.5 collective-permute-done.7.one
  124.6 0.1 last_gradient.1
  124.7 13.6 %all_to_all.29.parts = f32[32,1,128]{2,1,0:T(1,128)S(1)} all-to-all(f32[32,1,128]{2,1,0:T(1,128)S(1)} %get-tuple-element.21), channel_id=1, replica_groups=mesh['grp'=4,'shard'=32] {'shard'}, dimensions={0} | all-to-all | bytes 32768 | tf_op jit(solution)/shard_map/all_to_all | solution.py:460
  138.4 0.0 copy-done.2
  138.4 0.7 last_duals.1
  (6 shorter events, 0.1 us)
Async XLA Ops:
  0.6 24.5 %copy-start.3 = (s32[256,16]{0,1:T(8,128)S(1)}, s32[256,16]{0,1:T(8,128)}, u32[]{:S(2)}) copy-start(s32[256,16]{0,1:T(8,128)} %param.6) | copy-start | bytes 49156
  0.6 26.8 %copy-start.4 = (s32[256]{0:T(256)S(1)}, s32[256]{0:T(256)}, u32[]{:S(2)}) copy-start(s32[256]{0:T(256)} %param.9) | copy-start | bytes 3076
  0.7 0.8 copy-start.1
  23.4 4.1 %collective-permute-start = (f32[1600,128]{1,0:T(8,128)S(1)}, f32[1600,128]{1,0:T(8,128)S(1)}, u32[]{:S(2)}, u32[]{:S(2)}) collective-permute-start(f32[1600,128]{1,0:T(8,128)S(1)} %bitcast.29), channel_id=1, source_target_pairs={{0,1},{1,0},{2,3},{3,2},{4,5},{5,4},{6,7},{7,6},{8,9},{9,8},{10,11... | collective-permute-start | bytes 2457608 | tf_op jit(solution)/shard_map/ppermute | solution.py:414
  39.3 2.4 %collective-permute-start.1 = (f32[1600,128]{1,0:T(8,128)S(1)}, f32[1600,128]{1,0:T(8,128)S(1)}, u32[]{:S(2)}, u32[]{:S(2)}) collective-permute-start(f32[1600,128]{1,0:T(8,128)S(1)} %get-tuple-element.13), channel_id=1, source_target_pairs={{0,1},{1,0},{2,3},{3,2},{4,5},{5,4},{6,7},{7,6},{8,9},{9,8},{10,11... | collective-permute-start | bytes 2457608 | tf_op jit(solution)/shard_map/ppermute | solution.py:414
  41.7 24.9 %copy-start = (f32[12800]{0:T(1024)S(1)}, f32[12800]{0:T(1024)}, u32[]{:S(2)}) copy-start(f32[12800]{0:T(1024)} %param.10) | copy-start | bytes 153604
  58.7 4.0 %collective-permute-start.4 = (f32[100,128]{1,0:T(8,128)S(1)}, f32[100,128]{1,0:T(8,128)S(1)}, u32[]{:S(2)}, u32[]{:S(2)}) collective-permute-start(f32[100,128]{1,0:T(8,128)S(1)} %sum_chips.2.plane), channel_id=1, source_target_pairs={{0,96},{32,0},{64,32},{96,64},{1,97},{33,1},{65,33},{97,65},{2,98}... | collective-permute-start | bytes 153608 | tf_op jit(solution)/shard_map/ppermute | solution.py:432
  61.5 4.5 %collective-permute-start.3 = (f32[100,128]{1,0:T(8,128)S(1)}, f32[100,128]{1,0:T(8,128)S(1)}, u32[]{:S(2)}, u32[]{:S(2)}) collective-permute-start(f32[100,128]{1,0:T(8,128)S(1)} %sum_chips.2.plane), channel_id=1, source_target_pairs={{0,64},{32,96},{64,0},{96,32},{1,65},{33,97},{65,1},{97,33},{2,66}... | collective-permute-start | bytes 153608 | tf_op jit(solution)/shard_map/ppermute | solution.py:432
  61.9 4.7 %collective-permute-start.2 = (f32[100,128]{1,0:T(8,128)S(1)}, f32[100,128]{1,0:T(8,128)S(1)}, u32[]{:S(2)}, u32[]{:S(2)}) collective-permute-start(f32[100,128]{1,0:T(8,128)S(1)} %sum_chips.2.plane), channel_id=1, source_target_pairs={{0,32},{32,64},{64,96},{96,0},{1,33},{33,65},{65,97},{97,1},{2,34}... | collective-permute-start | bytes 153608 | tf_op jit(solution)/shard_map/ppermute | solution.py:432
  81.3 6.4 %collective-permute-start.5 = (f32[1600,128]{1,0:T(8,128)S(1)}, f32[1600,128]{1,0:T(8,128)S(1)}, u32[]{:S(2)}, u32[]{:S(2)}) collective-permute-start(f32[1600,128]{1,0:T(8,128)S(1)} %bitcast.35), channel_id=1, source_target_pairs={{0,1},{1,0},{2,3},{3,2},{4,5},{5,4},{6,7},{7,6},{8,9},{9,8},{10,11... | collective-permute-start | bytes 2457608 | tf_op jit(solution)/shard_map/ppermute | solution.py:414
  99.5 2.4 %collective-permute-start.6 = (f32[1600,128]{1,0:T(8,128)S(1)}, f32[1600,128]{1,0:T(8,128)S(1)}, u32[]{:S(2)}, u32[]{:S(2)}) collective-permute-start(f32[1600,128]{1,0:T(8,128)S(1)} %get-tuple-element.19), channel_id=1, source_target_pairs={{0,1},{1,0},{2,3},{3,2},{4,5},{5,4},{6,7},{7,6},{8,9},{9,8},{10,11... | collective-permute-start | bytes 2457608 | tf_op jit(solution)/shard_map/ppermute | solution.py:414
  101.9 36.4 %copy-start.2 = (f32[12800]{0:T(1024)S(1)}, f32[12800]{0:T(1024)}, u32[]{:S(2)}) copy-start(f32[12800]{0:T(1024)} %param.11) | copy-start | bytes 153604
  118.9 3.1 %collective-permute-start.9 = (f32[100,128]{1,0:T(8,128)S(1)}, f32[100,128]{1,0:T(8,128)S(1)}, u32[]{:S(2)}, u32[]{:S(2)}) collective-permute-start(f32[100,128]{1,0:T(8,128)S(1)} %sum_chips.3.plane), channel_id=1, source_target_pairs={{0,96},{32,0},{64,32},{96,64},{1,97},{33,1},{65,33},{97,65},{2,98}... | collective-permute-start | bytes 153608 | tf_op jit(solution)/shard_map/ppermute | solution.py:432
  119.5 4.5 %collective-permute-start.8 = (f32[100,128]{1,0:T(8,128)S(1)}, f32[100,128]{1,0:T(8,128)S(1)}, u32[]{:S(2)}, u32[]{:S(2)}) collective-permute-start(f32[100,128]{1,0:T(8,128)S(1)} %sum_chips.3.plane), channel_id=1, source_target_pairs={{0,64},{32,96},{64,0},{96,32},{1,65},{33,97},{65,1},{97,33},{2,66}... | collective-permute-start | bytes 153608 | tf_op jit(solution)/shard_map/ppermute | solution.py:432
  120.0 4.6 %collective-permute-start.7 = (f32[100,128]{1,0:T(8,128)S(1)}, f32[100,128]{1,0:T(8,128)S(1)}, u32[]{:S(2)}, u32[]{:S(2)}) collective-permute-start(f32[100,128]{1,0:T(8,128)S(1)} %sum_chips.3.plane), channel_id=1, source_target_pairs={{0,32},{32,64},{64,96},{96,0},{1,33},{33,65},{65,97},{97,1},{2,34}... | collective-permute-start | bytes 153608 | tf_op jit(solution)/shard_map/ppermute | solution.py:432

commit v8 on v7

--- a/solution.py
+++ b/solution.py
@@ -360,15 +360,15 @@
 
 
 def gradient_of(plane, shifted, limit):
-    one, two, three = shifted
+    two, one, three = shifted
     return ((plane[...] + two[...]) + (one[...] + three[...])) - limit[...]
 
 
 def spread_gradient(plane, shifted, limit, chips):
     own_rows = plane.shape[0]
 
-    def body(plane, one, two, three, limit, gradient, every):
-        g = gradient_of(plane, (one, two, three), limit)
+    def body(plane, two, one, three, limit, gradient, every):
+        g = gradient_of(plane, (two, one, three), limit)
         gradient[...] = g
         for p in range(chips):
             every[pl.ds(p * own_rows, own_rows), :] = g
@@ -377,8 +377,8 @@
 
 
 def last_gradient(plane, shifted, limit, shards):
-    def body(plane, one, two, three, limit, gradient, parts):
-        g = gradient_of(plane, (one, two, three), limit)
+    def body(plane, two, one, three, limit, gradient, parts):
+        g = gradient_of(plane, (two, one, three), limit)
         gradient[...] = g
         part = jnp.sum(jnp.sum(g * g, axis=0, keepdims=True), axis=1, keepdims=True)
         parts[...] = jnp.broadcast_to(part[None], parts.shape)
@@ -430,7 +430,7 @@
         plane = sum_chips(exchange(chip), chips)
         return plane, [
             lax.ppermute(plane, "grp", [(g, (g + d) % grp_size) for g in range(grp_size)])
-            for d in range(1, grp_size)
+            for d in (2, 1, 3)
         ]
 
     shard_of = candidates // own_rows

time: 139 us -> 141 us (1.014)
  starting transfers between devices: 12.5 us -> 15 us
    ppermute x6, starting transfers between devices: 5.67 us -> 8.21 us  [reduce_loads(): lax.ppermute(plane, 'grp', [(g, (g + d) % grp_size) for g in range(grp_si...]
  transfers between devices with their start and end apart: 10 -> 10, of which waited for: 9 -> 5; matrix products, arithmetic and copies ran while one was open for 1% -> 1% of each run, Pallas kernels for 0% -> 0%
where the time goes in v8:
time: 141 us; the launch traced here: 140 us
  blocking collectives  83.7 us (59%)
  Pallas kernels  24.6 us (17%)
  starting transfers between devices  15 us (11%)
  waiting for transfers between devices  12.8 us (9%)
  local copies, waits for them, and re-layouts  1.67 us (1%)
  between operations  1.43 us (1%)
    all_to_all x4, blocking collectives, exchange(): lax.all_to_all(x, 'shard', 0, 0, axis_index_groups=same_core, tiled=True)  70.1 us
    pallas_call x2, Pallas kernels, run(): return call(gidx, sidx, ncopy, *tables, aff, exp, nlive)  23.6 us
    all_to_all x1, blocking collectives, local(): parts = lax.all_to_all(parts, 'shard', 0, 0, tiled=True)  13.6 us
    ppermute x6, starting transfers between devices, reduce_loads(): lax.ppermute(plane, 'grp', [(g, (g + d) % grp_size) for g in range(grp_si...  8.21 us
    ppermute x4, starting transfers between devices, swap_cores(): return lax.ppermute(x, AXES, swap)  6.84 us
    ppermute x6, waiting for transfers between devices, reduce_loads(): lax.ppermute(plane, 'grp', [(g, (g + d) % grp_size) for g in range(grp_si...  6.64 us
    ppermute x4, waiting for transfers between devices, swap_cores(): return lax.ppermute(x, AXES, swap)  6.2 us
  transfers between devices with their start and end apart: 10, of which 5 were waited for; matrix products, arithmetic and copies ran while one was open for 1% of the time, Pallas kernels for 0%

profile of v8, /device:TPU:1, one launch (start us, length us, event | category | flops | bytes accessed | tf_op | source)
XLA Modules:
  0.0 140.3 jit_solution(5650309423555167137)
XLA Ops:
  0.6 0.0 copy-start.3
  0.6 0.0 copy-start.4
  0.7 0.0 copy-start.1
  0.7 0.8 copy-done.1
  1.5 0.1 spread_duals.1
  1.5 21.8 %all_to_all.25 = f32[16,1,12800]{2,1,0:T(1,128)S(1)} all-to-all(f32[16,1,12800]{2,1,0:T(1,128)S(1)} %bitcast.32), channel_id=1, replica_groups={{0,2,4,6,8,10,12,14,16,18,20,22,24,26,28,30},{1,3,5,7,9,11,13,15,17,19,..., dimensions={0} | all-to-all | bytes 1638400 | tf_op jit(solution)/shard_map/all_to_all | solution.py:421
  23.4 1.8 %collective-permute-start = (f32[1600,128]{1,0:T(8,128)S(1)}, f32[1600,128]{1,0:T(8,128)S(1)}, u32[]{:S(2)}, u32[]{:S(2)}) collective-permute-start(f32[1600,128]{1,0:T(8,128)S(1)} %bitcast.29), channel_id=1, source_target_pairs={{0,1},{1,0},{2,3},{3,2},{4,5},{5,4},{6,7},{7,6},{8,9},{9,8},{10,11... | collective-permute-start | bytes 2457608 | tf_op jit(solution)/shard_map/ppermute | solution.py:414
  25.2 0.0 copy-done.3
  25.2 0.1 copy.26
  25.3 0.1 convert_reduce_fusion
  25.5 0.6 fusion.7
  26.7 0.1 copy.28
  26.8 0.1 reshape.83
  27.0 0.1 copy.29
  27.1 0.1 reshape.84.refs_1_
  27.1 0.1 reshape_reshape.3
  27.2 0.1 copy.27
  27.3 0.1 reshape.82.refs_0_
  27.4 0.0 copy-done.4
  27.4 0.0 collective-permute-done.refs_4_
  27.5 0.1 broadcast_in_dim.20.refs_7_.refs_9_
  27.6 11.7 %iterate1.1 = (f32[1600,128]{1,0:T(8,128)S(1)}, f32[1600,128]{1,0:T(8,128)S(1)}) custom-call(s32[4096]{0:T(1024)S(1)} %reshape.82.refs_0_, s32[4096]{0:T(1024)S(1)} %reshape.84.refs_1_, s32[1]{0:T(128)} %bitcast.2.refs_2_, f32[1600,128]{1,0:T(8,128)S(1)} %bitcast.30, f32[1600,128]{1,0:T(8,128)S(1)} %collective-permute-done.refs_4_, f32[4096,128]{1,0:T(8,128)} %bitcast.42, ...), custom_call_target="tpu_custom_call" | custom-call | tf_op jit(solution)/shard_map/iterate1/pallas_call | solution.py:323
  39.3 0.1 collective-permute-start.1
  39.4 2.3 %collective-permute-done.1 = f32[1600,128]{1,0:T(8,128)S(1)} collective-permute-done((f32[1600,128]{1,0:T(8,128)S(1)}, f32[1600,128]{1,0:T(8,128)S(1)}, u32[]{:S(2)}, u32[]{:S(2)}) %collective-permute-start.1) | collective-permute-done | bytes 819232 | tf_op jit(solution)/shard_map/ppermute | solution.py:414
  41.7 0.0 copy-start
  41.7 0.1 add.42
  41.8 16.9 %all_to_all.26 = f32[16,1,12800]{2,1,0:T(1,128)S(1)} all-to-all(f32[16,1,12800]{2,1,0:T(1,128)S(1)} %bitcast.46), channel_id=1, replica_groups={{0,2,4,6,8,10,12,14,16,18,20,22,24,26,28,30},{1,3,5,7,9,11,13,15,17,19,..., dimensions={0} | all-to-all | bytes 1638400 | tf_op jit(solution)/shard_map/all_to_all | solution.py:421
  58.7 2.8 %collective-permute-start.4 = (f32[100,128]{1,0:T(8,128)S(1)}, f32[100,128]{1,0:T(8,128)S(1)}, u32[]{:S(2)}, u32[]{:S(2)}) collective-permute-start(f32[100,128]{1,0:T(8,128)S(1)} %sum_chips.2.plane), channel_id=1, source_target_pairs={{0,96},{32,0},{64,32},{96,64},{1,97},{33,1},{65,33},{97,65},{2,98}... | collective-permute-start | bytes 153608 | tf_op jit(solution)/shard_map/ppermute | solution.py:432
  61.6 0.0 collective-permute-start.3
  61.6 1.6 %collective-permute-start.2 = (f32[100,128]{1,0:T(8,128)S(1)}, f32[100,128]{1,0:T(8,128)S(1)}, u32[]{:S(2)}, u32[]{:S(2)}) collective-permute-start(f32[100,128]{1,0:T(8,128)S(1)} %sum_chips.2.plane), channel_id=1, source_target_pairs={{0,64},{32,96},{64,0},{96,32},{1,65},{33,97},{65,1},{97,33},{2,66}... | collective-permute-start | bytes 153608 | tf_op jit(solution)/shard_map/ppermute | solution.py:432
  63.2 0.0 collective-permute-done.4.three
  63.2 3.1 %collective-permute-done.3.one = f32[100,128]{1,0:T(8,128)S(1)} collective-permute-done((f32[100,128]{1,0:T(8,128)S(1)}, f32[100,128]{1,0:T(8,128)S(1)}, u32[]{:S(2)}, u32[]{:S(2)}) %collective-permute-start.3) | collective-permute-done | bytes 51232 | tf_op jit(solution)/shard_map/ppermute | solution.py:432
  66.3 0.0 collective-permute-done.2.two
  66.3 0.0 copy-done
  66.3 0.1 spread_gradient.1
  66.4 14.6 %all_to_all.27 = f32[16,1,12800]{2,1,0:T(1,128)S(1)} all-to-all(f32[16,1,12800]{2,1,0:T(1,128)S(1)} %bitcast.37), channel_id=1, replica_groups={{0,2,4,6,8,10,12,14,16,18,20,22,24,26,28,30},{1,3,5,7,9,11,13,15,17,19,..., dimensions={0} | all-to-all | bytes 1638400 | tf_op jit(solution)/shard_map/all_to_all | solution.py:421
  81.0 4.4 %collective-permute-start.5 = (f32[1600,128]{1,0:T(8,128)S(1)}, f32[1600,128]{1,0:T(8,128)S(1)}, u32[]{:S(2)}, u32[]{:S(2)}) collective-permute-start(f32[1600,128]{1,0:T(8,128)S(1)} %bitcast.35), channel_id=1, source_target_pairs={{0,1},{1,0},{2,3},{3,2},{4,5},{5,4},{6,7},{7,6},{8,9},{9,8},{10,11... | collective-permute-start | bytes 2457608 | tf_op jit(solution)/shard_map/ppermute | solution.py:414
  85.5 2.0 %collective-permute-done.5.refs_6_ = f32[1600,128]{1,0:T(8,128)S(1)} collective-permute-done((f32[1600,128]{1,0:T(8,128)S(1)}, f32[1600,128]{1,0:T(8,128)S(1)}, u32[]{:S(2)}, u32[]{:S(2)}) %collective-permute-start.5) | collective-permute-done | bytes 819232 | tf_op jit(solution)/shard_map/ppermute | solution.py:414
  87.4 11.8 %iterate2.1 = (f32[1600,128]{1,0:T(8,128)S(1)}, f32[1600,128]{1,0:T(8,128)S(1)}, f32[4096,128]{1,0:T(8,128)}, f32[8,128]{1,0:T(8,128)S(1)}) custom-call(s32[4096]{0:T(1024)S(1)} %reshape.82.refs_0_, s32[4096]{0:T(1024)S(1)} %reshape.84.refs_1_, s32[1]{0:T(128)} %bitcast.2.refs_2_, f32[1600,128]{1,0:T(8,128)S(1)} %bitcast.31, ...), custom_call_target="tpu_custom_call" | custom-call | tf_op jit(solution)/shard_map/iterate2/pallas_call | solution.py:323
  99.3 0.5 collective-permute-start.6
  99.7 2.0 %collective-permute-done.6 = f32[1600,128]{1,0:T(8,128)S(1)} collective-permute-done((f32[1600,128]{1,0:T(8,128)S(1)}, f32[1600,128]{1,0:T(8,128)S(1)}, u32[]{:S(2)}, u32[]{:S(2)}) %collective-permute-start.6) | collective-permute-done | bytes 819232 | tf_op jit(solution)/shard_map/ppermute | solution.py:414
  101.7 0.0 copy-start.2
  101.7 0.1 add.43
  101.8 16.8 %all_to_all.28 = f32[16,1,12800]{2,1,0:T(1,128)S(1)} all-to-all(f32[16,1,12800]{2,1,0:T(1,128)S(1)} %bitcast.47), channel_id=1, replica_groups={{0,2,4,6,8,10,12,14,16,18,20,22,24,26,28,30},{1,3,5,7,9,11,13,15,17,19,..., dimensions={0} | all-to-all | bytes 1638400 | tf_op jit(solution)/shard_map/all_to_all | solution.py:421
  118.6 2.5 %collective-permute-start.9 = (f32[100,128]{1,0:T(8,128)S(1)}, f32[100,128]{1,0:T(8,128)S(1)}, u32[]{:S(2)}, u32[]{:S(2)}) collective-permute-start(f32[100,128]{1,0:T(8,128)S(1)} %sum_chips.3.plane), channel_id=1, source_target_pairs={{0,96},{32,0},{64,32},{96,64},{1,97},{33,1},{65,33},{97,65},{2,98}... | collective-permute-start | bytes 153608 | tf_op jit(solution)/shard_map/ppermute | solution.py:432
  121.1 0.0 collective-permute-start.8
  121.1 1.3 collective-permute-start.7
  122.4 0.0 collective-permute-done.9.three
  122.4 3.5 %collective-permute-done.8.one = f32[100,128]{1,0:T(8,128)S(1)} collective-permute-done((f32[100,128]{1,0:T(8,128)S(1)}, f32[100,128]{1,0:T(8,128)S(1)}, u32[]{:S(2)}, u32[]{:S(2)}) %collective-permute-start.8) | collective-permute-done | bytes 51232 | tf_op jit(solution)/shard_map/ppermute | solution.py:432
  125.9 0.0 collective-permute-done.7.two
  125.9 0.1 last_gradient.1
  126.0 13.6 %all_to_all.29.parts = f32[32,1,128]{2,1,0:T(1,128)S(1)} all-to-all(f32[32,1,128]{2,1,0:T(1,128)S(1)} %get-tuple-element.21), channel_id=1, replica_groups=mesh['grp'=4,'shard'=32] {'shard'}, dimensions={0} | all-to-all | bytes 32768 | tf_op jit(solution)/shard_map/all_to_all | solution.py:460
  139.6 0.0 copy-done.2
  139.6 0.7 last_duals.1
  (6 shorter events, 0.1 us)
Async XLA Ops:
  0.6 24.5 %copy-start.3 = (s32[256,16]{0,1:T(8,128)S(1)}, s32[256,16]{0,1:T(8,128)}, u32[]{:S(2)}) copy-start(s32[256,16]{0,1:T(8,128)} %param.6) | copy-start | bytes 49156
  0.6 26.8 %copy-start.4 = (s32[256]{0:T(256)S(1)}, s32[256]{0:T(256)}, u32[]{:S(2)}) copy-start(s32[256]{0:T(256)} %param.9) | copy-start | bytes 3076
  0.7 0.8 copy-start.1
  23.4 4.1 %collective-permute-start = (f32[1600,128]{1,0:T(8,128)S(1)}, f32[1600,128]{1,0:T(8,128)S(1)}, u32[]{:S(2)}, u32[]{:S(2)}) collective-permute-start(f32[1600,128]{1,0:T(8,128)S(1)} %bitcast.29), channel_id=1, source_target_pairs={{0,1},{1,0},{2,3},{3,2},{4,5},{5,4},{6,7},{7,6},{8,9},{9,8},{10,11... | collective-permute-start | bytes 2457608 | tf_op jit(solution)/shard_map/ppermute | solution.py:414
  39.3 2.4 %collective-permute-start.1 = (f32[1600,128]{1,0:T(8,128)S(1)}, f32[1600,128]{1,0:T(8,128)S(1)}, u32[]{:S(2)}, u32[]{:S(2)}) collective-permute-start(f32[1600,128]{1,0:T(8,128)S(1)} %get-tuple-element.13), channel_id=1, source_target_pairs={{0,1},{1,0},{2,3},{3,2},{4,5},{5,4},{6,7},{7,6},{8,9},{9,8},{10,11... | collective-permute-start | bytes 2457608 | tf_op jit(solution)/shard_map/ppermute | solution.py:414
  41.7 24.6 %copy-start = (f32[12800]{0:T(1024)S(1)}, f32[12800]{0:T(1024)}, u32[]{:S(2)}) copy-start(f32[12800]{0:T(1024)} %param.10) | copy-start | bytes 153604
  58.7 4.5 %collective-permute-start.4 = (f32[100,128]{1,0:T(8,128)S(1)}, f32[100,128]{1,0:T(8,128)S(1)}, u32[]{:S(2)}, u32[]{:S(2)}) collective-permute-start(f32[100,128]{1,0:T(8,128)S(1)} %sum_chips.2.plane), channel_id=1, source_target_pairs={{0,96},{32,0},{64,32},{96,64},{1,97},{33,1},{65,33},{97,65},{2,98}... | collective-permute-start | bytes 153608 | tf_op jit(solution)/shard_map/ppermute | solution.py:432
  61.6 4.8 %collective-permute-start.3 = (f32[100,128]{1,0:T(8,128)S(1)}, f32[100,128]{1,0:T(8,128)S(1)}, u32[]{:S(2)}, u32[]{:S(2)}) collective-permute-start(f32[100,128]{1,0:T(8,128)S(1)} %sum_chips.2.plane), channel_id=1, source_target_pairs={{0,32},{32,64},{64,96},{96,0},{1,33},{33,65},{65,97},{97,1},{2,34}... | collective-permute-start | bytes 153608 | tf_op jit(solution)/shard_map/ppermute | solution.py:432
  61.6 4.8 %collective-permute-start.2 = (f32[100,128]{1,0:T(8,128)S(1)}, f32[100,128]{1,0:T(8,128)S(1)}, u32[]{:S(2)}, u32[]{:S(2)}) collective-permute-start(f32[100,128]{1,0:T(8,128)S(1)} %sum_chips.2.plane), channel_id=1, source_target_pairs={{0,64},{32,96},{64,0},{96,32},{1,65},{33,97},{65,1},{97,33},{2,66}... | collective-permute-start | bytes 153608 | tf_op jit(solution)/shard_map/ppermute | solution.py:432
  81.0 6.4 %collective-permute-start.5 = (f32[1600,128]{1,0:T(8,128)S(1)}, f32[1600,128]{1,0:T(8,128)S(1)}, u32[]{:S(2)}, u32[]{:S(2)}) collective-permute-start(f32[1600,128]{1,0:T(8,128)S(1)} %bitcast.35), channel_id=1, source_target_pairs={{0,1},{1,0},{2,3},{3,2},{4,5},{5,4},{6,7},{7,6},{8,9},{9,8},{10,11... | collective-permute-start | bytes 2457608 | tf_op jit(solution)/shard_map/ppermute | solution.py:414
  99.3 2.4 %collective-permute-start.6 = (f32[1600,128]{1,0:T(8,128)S(1)}, f32[1600,128]{1,0:T(8,128)S(1)}, u32[]{:S(2)}, u32[]{:S(2)}) collective-permute-start(f32[1600,128]{1,0:T(8,128)S(1)} %get-tuple-element.19), channel_id=1, source_target_pairs={{0,1},{1,0},{2,3},{3,2},{4,5},{5,4},{6,7},{7,6},{8,9},{9,8},{10,11... | collective-permute-start | bytes 2457608 | tf_op jit(solution)/shard_map/ppermute | solution.py:414
  101.7 38.0 %copy-start.2 = (f32[12800]{0:T(1024)S(1)}, f32[12800]{0:T(1024)}, u32[]{:S(2)}) copy-start(f32[12800]{0:T(1024)} %param.11) | copy-start | bytes 153604
  118.6 3.8 %collective-permute-start.9 = (f32[100,128]{1,0:T(8,128)S(1)}, f32[100,128]{1,0:T(8,128)S(1)}, u32[]{:S(2)}, u32[]{:S(2)}) collective-permute-start(f32[100,128]{1,0:T(8,128)S(1)} %sum_chips.3.plane), channel_id=1, source_target_pairs={{0,96},{32,0},{64,32},{96,64},{1,97},{33,1},{65,33},{97,65},{2,98}... | collective-permute-start | bytes 153608 | tf_op jit(solution)/shard_map/ppermute | solution.py:432
  121.1 4.8 %collective-permute-start.8 = (f32[100,128]{1,0:T(8,128)S(1)}, f32[100,128]{1,0:T(8,128)S(1)}, u32[]{:S(2)}, u32[]{:S(2)}) collective-permute-start(f32[100,128]{1,0:T(8,128)S(1)} %sum_chips.3.plane), channel_id=1, source_target_pairs={{0,32},{32,64},{64,96},{96,0},{1,33},{33,65},{65,97},{97,1},{2,34}... | collective-permute-start | bytes 153608 | tf_op jit(solution)/shard_map/ppermute | solution.py:432
  121.1 4.8 %collective-permute-start.7 = (f32[100,128]{1,0:T(8,128)S(1)}, f32[100,128]{1,0:T(8,128)S(1)}, u32[]{:S(2)}, u32[]{:S(2)}) collective-permute-start(f32[100,128]{1,0:T(8,128)S(1)} %sum_chips.3.plane), channel_id=1, source_target_pairs={{0,64},{32,96},{64,0},{96,32},{1,65},{33,97},{65,1},{97,33},{2,66}... | collective-permute-start | bytes 153608 | tf_op jit(solution)/shard_map/ppermute | solution.py:432

commit v9 on v7

--- a/solution.py
+++ b/solution.py
@@ -63,13 +63,13 @@
             total = jnp.sum(jnp.sum(s, axis=1, keepdims=True), axis=0, keepdims=True)
             total = jnp.broadcast_to(total, (SUB, BLOCK))
             sumsq[...] = total
-            scale = jnp.sqrt(total / item_count + 1e-6)
+            step = 0.5 / jnp.sqrt(total / item_count + 1e-6)
 
             def fill_table(i, c):
                 r = pl.multiple_of(i * SUB, SUB)
                 for d, g, off in ((own_d, own_g, 0), (other_d, other_g, half)):
                     table[pl.ds(r + off, SUB), :] = jnp.maximum(
-                        d[pl.ds(r, SUB), :] + 0.5 * g[pl.ds(r, SUB), :] / scale, 0.0)
+                        d[pl.ds(r, SUB), :] + g[pl.ds(r, SUB), :] * step, 0.0)
                 return c
         else:
             def fill_table(i, c):

time: 139 us -> 140 us (level)
  no operation moved by 1% of the time
where the time goes in v9:
time: 140 us; the launch traced here: 139 us
  blocking collectives  83.8 us (60%)
  Pallas kernels  24.5 us (18%)
  waiting for transfers between devices  14.3 us (10%)
  starting transfers between devices  12.5 us (9%)
  local copies, waits for them, and re-layouts  1.67 us (1%)
  between operations  1.43 us (1%)
    all_to_all x4, blocking collectives, exchange(): lax.all_to_all(x, 'shard', 0, 0, axis_index_groups=same_core, tiled=True)  70.1 us
    pallas_call x2, Pallas kernels, run(): return call(gidx, sidx, ncopy, *tables, aff, exp, nlive)  23.5 us
    all_to_all x1, blocking collectives, local(): parts = lax.all_to_all(parts, 'shard', 0, 0, tiled=True)  13.6 us
    ppermute x6, waiting for transfers between devices, reduce_loads(): lax.ppermute(plane, 'grp', [(g, (g + d) % grp_size) for g in range(grp_si...  8.1 us
    ppermute x4, starting transfers between devices, swap_cores(): return lax.ppermute(x, AXES, swap)  6.85 us
    ppermute x4, waiting for transfers between devices, swap_cores(): return lax.ppermute(x, AXES, swap)  6.2 us
    ppermute x6, starting transfers between devices, reduce_loads(): lax.ppermute(plane, 'grp', [(g, (g + d) % grp_size) for g in range(grp_si...  5.67 us
  transfers between devices with their start and end apart: 10, of which 9 were waited for; matrix products, arithmetic and copies ran while one was open for 1% of the time, Pallas kernels for 0%

profile of v9, /device:TPU:1, one launch (start us, length us, event | category | flops | bytes accessed | tf_op | source)
XLA Modules:
  0.0 139.2 jit_solution(15669213360034942038)
XLA Ops:
  0.6 0.0 copy-start.3
  0.6 0.0 copy-start.4
  0.7 0.0 copy-start.1
  0.7 0.8 copy-done.1
  1.5 0.1 spread_duals.1
  1.5 21.8 %all_to_all.25 = f32[16,1,12800]{2,1,0:T(1,128)S(1)} all-to-all(f32[16,1,12800]{2,1,0:T(1,128)S(1)} %bitcast.32), channel_id=1, replica_groups={{0,2,4,6,8,10,12,14,16,18,20,22,24,26,28,30},{1,3,5,7,9,11,13,15,17,19,..., dimensions={0} | all-to-all | bytes 1638400 | tf_op jit(solution)/shard_map/all_to_all | solution.py:421
  23.4 1.8 %collective-permute-start = (f32[1600,128]{1,0:T(8,128)S(1)}, f32[1600,128]{1,0:T(8,128)S(1)}, u32[]{:S(2)}, u32[]{:S(2)}) collective-permute-start(f32[1600,128]{1,0:T(8,128)S(1)} %bitcast.29), channel_id=1, source_target_pairs={{0,1},{1,0},{2,3},{3,2},{4,5},{5,4},{6,7},{7,6},{8,9},{9,8},{10,11... | collective-permute-start | bytes 2457608 | tf_op jit(solution)/shard_map/ppermute | solution.py:414
  25.2 0.0 copy-done.3
  25.2 0.1 copy.26
  25.3 0.1 convert_reduce_fusion
  25.5 0.6 fusion.7
  26.7 0.1 copy.28
  26.8 0.1 reshape.83
  27.0 0.1 copy.29
  27.1 0.1 reshape.84.refs_1_
  27.1 0.1 reshape_reshape.3
  27.2 0.1 copy.27
  27.3 0.1 reshape.82.refs_0_
  27.4 0.0 copy-done.4
  27.4 0.0 collective-permute-done.refs_4_
  27.5 0.1 broadcast_in_dim.20.refs_7_.refs_9_
  27.6 11.7 %iterate1.1 = (f32[1600,128]{1,0:T(8,128)S(1)}, f32[1600,128]{1,0:T(8,128)S(1)}) custom-call(s32[4096]{0:T(1024)S(1)} %reshape.82.refs_0_, s32[4096]{0:T(1024)S(1)} %reshape.84.refs_1_, s32[1]{0:T(128)} %bitcast.2.refs_2_, f32[1600,128]{1,0:T(8,128)S(1)} %bitcast.30, f32[1600,128]{1,0:T(8,128)S(1)} %collective-permute-done.refs_4_, f32[4096,128]{1,0:T(8,128)} %bitcast.42, ...), custom_call_target="tpu_custom_call" | custom-call | tf_op jit(solution)/shard_map/iterate1/pallas_call | solution.py:323
  39.3 0.1 collective-permute-start.1
  39.4 2.3 %collective-permute-done.1 = f32[1600,128]{1,0:T(8,128)S(1)} collective-permute-done((f32[1600,128]{1,0:T(8,128)S(1)}, f32[1600,128]{1,0:T(8,128)S(1)}, u32[]{:S(2)}, u32[]{:S(2)}) %collective-permute-start.1) | collective-permute-done | bytes 819232 | tf_op jit(solution)/shard_map/ppermute | solution.py:414
  41.7 0.0 copy-start
  41.7 0.1 add.42
  41.8 16.9 %all_to_all.26 = f32[16,1,12800]{2,1,0:T(1,128)S(1)} all-to-all(f32[16,1,12800]{2,1,0:T(1,128)S(1)} %bitcast.46), channel_id=1, replica_groups={{0,2,4,6,8,10,12,14,16,18,20,22,24,26,28,30},{1,3,5,7,9,11,13,15,17,19,..., dimensions={0} | all-to-all | bytes 1638400 | tf_op jit(solution)/shard_map/all_to_all | solution.py:421
  58.7 2.8 %collective-permute-start.4 = (f32[100,128]{1,0:T(8,128)S(1)}, f32[100,128]{1,0:T(8,128)S(1)}, u32[]{:S(2)}, u32[]{:S(2)}) collective-permute-start(f32[100,128]{1,0:T(8,128)S(1)} %sum_chips.2.plane), channel_id=1, source_target_pairs={{0,96},{32,0},{64,32},{96,64},{1,97},{33,1},{65,33},{97,65},{2,98}... | collective-permute-start | bytes 153608 | tf_op jit(solution)/shard_map/ppermute | solution.py:432
  61.6 0.3 collective-permute-start.3
  61.9 0.7 collective-permute-start.2
  62.6 0.2 collective-permute-done.4.three
  62.8 3.3 %collective-permute-done.3.two = f32[100,128]{1,0:T(8,128)S(1)} collective-permute-done((f32[100,128]{1,0:T(8,128)S(1)}, f32[100,128]{1,0:T(8,128)S(1)}, u32[]{:S(2)}, u32[]{:S(2)}) %collective-permute-start.3) | collective-permute-done | bytes 51232 | tf_op jit(solution)/shard_map/ppermute | solution.py:432
  66.1 0.5 collective-permute-done.2.one
  66.6 0.0 copy-done
  66.6 0.1 spread_gradient.1
  66.7 14.6 %all_to_all.27 = f32[16,1,12800]{2,1,0:T(1,128)S(1)} all-to-all(f32[16,1,12800]{2,1,0:T(1,128)S(1)} %bitcast.37), channel_id=1, replica_groups={{0,2,4,6,8,10,12,14,16,18,20,22,24,26,28,30},{1,3,5,7,9,11,13,15,17,19,..., dimensions={0} | all-to-all | bytes 1638400 | tf_op jit(solution)/shard_map/all_to_all | solution.py:421
  81.3 4.4 %collective-permute-start.5 = (f32[1600,128]{1,0:T(8,128)S(1)}, f32[1600,128]{1,0:T(8,128)S(1)}, u32[]{:S(2)}, u32[]{:S(2)}) collective-permute-start(f32[1600,128]{1,0:T(8,128)S(1)} %bitcast.35), channel_id=1, source_target_pairs={{0,1},{1,0},{2,3},{3,2},{4,5},{5,4},{6,7},{7,6},{8,9},{9,8},{10,11... | collective-permute-start | bytes 2457608 | tf_op jit(solution)/shard_map/ppermute | solution.py:414
  85.7 2.0 %collective-permute-done.5.refs_6_ = f32[1600,128]{1,0:T(8,128)S(1)} collective-permute-done((f32[1600,128]{1,0:T(8,128)S(1)}, f32[1600,128]{1,0:T(8,128)S(1)}, u32[]{:S(2)}, u32[]{:S(2)}) %collective-permute-start.5) | collective-permute-done | bytes 819232 | tf_op jit(solution)/shard_map/ppermute | solution.py:414
  87.7 11.8 %iterate2.1 = (f32[1600,128]{1,0:T(8,128)S(1)}, f32[1600,128]{1,0:T(8,128)S(1)}, f32[4096,128]{1,0:T(8,128)}, f32[8,128]{1,0:T(8,128)S(1)}) custom-call(s32[4096]{0:T(1024)S(1)} %reshape.82.refs_0_, s32[4096]{0:T(1024)S(1)} %reshape.84.refs_1_, s32[1]{0:T(128)} %bitcast.2.refs_2_, f32[1600,128]{1,0:T(8,128)S(1)} %bitcast.31, ...), custom_call_target="tpu_custom_call" | custom-call | tf_op jit(solution)/shard_map/iterate2/pallas_call | solution.py:323
  99.5 0.5 collective-permute-start.6
  100.0 2.0 %collective-permute-done.6 = f32[1600,128]{1,0:T(8,128)S(1)} collective-permute-done((f32[1600,128]{1,0:T(8,128)S(1)}, f32[1600,128]{1,0:T(8,128)S(1)}, u32[]{:S(2)}, u32[]{:S(2)}) %collective-permute-start.6) | collective-permute-done | bytes 819232 | tf_op jit(solution)/shard_map/ppermute | solution.py:414
  101.9 0.0 copy-start.2
  101.9 0.1 add.43
  102.0 16.8 %all_to_all.28 = f32[16,1,12800]{2,1,0:T(1,128)S(1)} all-to-all(f32[16,1,12800]{2,1,0:T(1,128)S(1)} %bitcast.47), channel_id=1, replica_groups={{0,2,4,6,8,10,12,14,16,18,20,22,24,26,28,30},{1,3,5,7,9,11,13,15,17,19,..., dimensions={0} | all-to-all | bytes 1638400 | tf_op jit(solution)/shard_map/all_to_all | solution.py:421
  118.9 0.8 collective-permute-start.9
  119.7 0.2 collective-permute-start.8
  119.9 0.8 collective-permute-start.7
  120.7 1.2 collective-permute-done.9.three
  121.9 2.3 %collective-permute-done.8.two = f32[100,128]{1,0:T(8,128)S(1)} collective-permute-done((f32[100,128]{1,0:T(8,128)S(1)}, f32[100,128]{1,0:T(8,128)S(1)}, u32[]{:S(2)}, u32[]{:S(2)}) %collective-permute-start.8) | collective-permute-done | bytes 51232 | tf_op jit(solution)/shard_map/ppermute | solution.py:432
  124.3 0.5 collective-permute-done.7.one
  124.8 0.1 last_gradient.1
  124.9 13.6 %all_to_all.29.parts = f32[32,1,128]{2,1,0:T(1,128)S(1)} all-to-all(f32[32,1,128]{2,1,0:T(1,128)S(1)} %get-tuple-element.21), channel_id=1, replica_groups=mesh['grp'=4,'shard'=32] {'shard'}, dimensions={0} | all-to-all | bytes 32768 | tf_op jit(solution)/shard_map/all_to_all | solution.py:460
  138.5 0.0 copy-done.2
  138.5 0.7 last_duals.1
  (6 shorter events, 0.1 us)
Async XLA Ops:
  0.6 24.5 %copy-start.3 = (s32[256,16]{0,1:T(8,128)S(1)}, s32[256,16]{0,1:T(8,128)}, u32[]{:S(2)}) copy-start(s32[256,16]{0,1:T(8,128)} %param.6) | copy-start | bytes 49156
  0.6 26.8 %copy-start.4 = (s32[256]{0:T(256)S(1)}, s32[256]{0:T(256)}, u32[]{:S(2)}) copy-start(s32[256]{0:T(256)} %param.9) | copy-start | bytes 3076
  0.7 0.8 copy-start.1
  23.4 4.1 %collective-permute-start = (f32[1600,128]{1,0:T(8,128)S(1)}, f32[1600,128]{1,0:T(8,128)S(1)}, u32[]{:S(2)}, u32[]{:S(2)}) collective-permute-start(f32[1600,128]{1,0:T(8,128)S(1)} %bitcast.29), channel_id=1, source_target_pairs={{0,1},{1,0},{2,3},{3,2},{4,5},{5,4},{6,7},{7,6},{8,9},{9,8},{10,11... | collective-permute-start | bytes 2457608 | tf_op jit(solution)/shard_map/ppermute | solution.py:414
  39.3 2.4 %collective-permute-start.1 = (f32[1600,128]{1,0:T(8,128)S(1)}, f32[1600,128]{1,0:T(8,128)S(1)}, u32[]{:S(2)}, u32[]{:S(2)}) collective-permute-start(f32[1600,128]{1,0:T(8,128)S(1)} %get-tuple-element.13), channel_id=1, source_target_pairs={{0,1},{1,0},{2,3},{3,2},{4,5},{5,4},{6,7},{7,6},{8,9},{9,8},{10,11... | collective-permute-start | bytes 2457608 | tf_op jit(solution)/shard_map/ppermute | solution.py:414
  41.7 24.9 %copy-start = (f32[12800]{0:T(1024)S(1)}, f32[12800]{0:T(1024)}, u32[]{:S(2)}) copy-start(f32[12800]{0:T(1024)} %param.10) | copy-start | bytes 153604
  58.7 4.0 %collective-permute-start.4 = (f32[100,128]{1,0:T(8,128)S(1)}, f32[100,128]{1,0:T(8,128)S(1)}, u32[]{:S(2)}, u32[]{:S(2)}) collective-permute-start(f32[100,128]{1,0:T(8,128)S(1)} %sum_chips.2.plane), channel_id=1, source_target_pairs={{0,96},{32,0},{64,32},{96,64},{1,97},{33,1},{65,33},{97,65},{2,98}... | collective-permute-start | bytes 153608 | tf_op jit(solution)/shard_map/ppermute | solution.py:432
  61.6 4.5 %collective-permute-start.3 = (f32[100,128]{1,0:T(8,128)S(1)}, f32[100,128]{1,0:T(8,128)S(1)}, u32[]{:S(2)}, u32[]{:S(2)}) collective-permute-start(f32[100,128]{1,0:T(8,128)S(1)} %sum_chips.2.plane), channel_id=1, source_target_pairs={{0,64},{32,96},{64,0},{96,32},{1,65},{33,97},{65,1},{97,33},{2,66}... | collective-permute-start | bytes 153608 | tf_op jit(solution)/shard_map/ppermute | solution.py:432
  61.9 4.7 %collective-permute-start.2 = (f32[100,128]{1,0:T(8,128)S(1)}, f32[100,128]{1,0:T(8,128)S(1)}, u32[]{:S(2)}, u32[]{:S(2)}) collective-permute-start(f32[100,128]{1,0:T(8,128)S(1)} %sum_chips.2.plane), channel_id=1, source_target_pairs={{0,32},{32,64},{64,96},{96,0},{1,33},{33,65},{65,97},{97,1},{2,34}... | collective-permute-start | bytes 153608 | tf_op jit(solution)/shard_map/ppermute | solution.py:432
  81.3 6.4 %collective-permute-start.5 = (f32[1600,128]{1,0:T(8,128)S(1)}, f32[1600,128]{1,0:T(8,128)S(1)}, u32[]{:S(2)}, u32[]{:S(2)}) collective-permute-start(f32[1600,128]{1,0:T(8,128)S(1)} %bitcast.35), channel_id=1, source_target_pairs={{0,1},{1,0},{2,3},{3,2},{4,5},{5,4},{6,7},{7,6},{8,9},{9,8},{10,11... | collective-permute-start | bytes 2457608 | tf_op jit(solution)/shard_map/ppermute | solution.py:414
  99.5 2.4 %collective-permute-start.6 = (f32[1600,128]{1,0:T(8,128)S(1)}, f32[1600,128]{1,0:T(8,128)S(1)}, u32[]{:S(2)}, u32[]{:S(2)}) collective-permute-start(f32[1600,128]{1,0:T(8,128)S(1)} %get-tuple-element.19), channel_id=1, source_target_pairs={{0,1},{1,0},{2,3},{3,2},{4,5},{5,4},{6,7},{7,6},{8,9},{9,8},{10,11... | collective-permute-start | bytes 2457608 | tf_op jit(solution)/shard_map/ppermute | solution.py:414
  101.9 36.6 %copy-start.2 = (f32[12800]{0:T(1024)S(1)}, f32[12800]{0:T(1024)}, u32[]{:S(2)}) copy-start(f32[12800]{0:T(1024)} %param.11) | copy-start | bytes 153604
  118.9 3.1 %collective-permute-start.9 = (f32[100,128]{1,0:T(8,128)S(1)}, f32[100,128]{1,0:T(8,128)S(1)}, u32[]{:S(2)}, u32[]{:S(2)}) collective-permute-start(f32[100,128]{1,0:T(8,128)S(1)} %sum_chips.3.plane), channel_id=1, source_target_pairs={{0,96},{32,0},{64,32},{96,64},{1,97},{33,1},{65,33},{97,65},{2,98}... | collective-permute-start | bytes 153608 | tf_op jit(solution)/shard_map/ppermute | solution.py:432
  119.7 4.5 %collective-permute-start.8 = (f32[100,128]{1,0:T(8,128)S(1)}, f32[100,128]{1,0:T(8,128)S(1)}, u32[]{:S(2)}, u32[]{:S(2)}) collective-permute-start(f32[100,128]{1,0:T(8,128)S(1)} %sum_chips.3.plane), channel_id=1, source_target_pairs={{0,64},{32,96},{64,0},{96,32},{1,65},{33,97},{65,1},{97,33},{2,66}... | collective-permute-start | bytes 153608 | tf_op jit(solution)/shard_map/ppermute | solution.py:432
  119.9 4.8 %collective-permute-start.7 = (f32[100,128]{1,0:T(8,128)S(1)}, f32[100,128]{1,0:T(8,128)S(1)}, u32[]{:S(2)}, u32[]{:S(2)}) collective-permute-start(f32[100,128]{1,0:T(8,128)S(1)} %sum_chips.3.plane), channel_id=1, source_target_pairs={{0,32},{32,64},{64,96},{96,0},{1,33},{33,65},{65,97},{97,1},{2,34}... | collective-permute-start | bytes 153608 | tf_op jit(solution)/shard_map/ppermute | solution.py:432
